TPU v7x, 32 devices: a whole 2x2x4 slice. The times are simulated.
32 devices in a mesh: fsdp: 16 (over z, y, x), win: 2 (over core).
Axes of the slice: x: 2, y: 2, z: 4, core: 2. Of those that a mesh axis runs over, the one named last changes fastest.
Arguments:
- images: bfloat16 [512, 14, 14, 512], P('fsdp', 'win'), may hold values from -6 to 6
- norm1_gain: bfloat16 [512], P('fsdp'), may hold values from 0.099609375 to 1.8984375
- norm1_bias: bfloat16 [512], P('fsdp'), may hold values from -3 to 3
- qkv_weight: bfloat16 [512, 1536], P('fsdp'), may hold values from -0.25 to 0.25
- q_bias: bfloat16 [512], P('fsdp'), may hold values from -3 to 3
- v_bias: bfloat16 [512], P('fsdp'), may hold values from -3 to 3
- proj_weight: bfloat16 [512, 512], P('fsdp'), may hold values from -0.75 to 0.75
- proj_bias: bfloat16 [512], P('fsdp'), may hold values from -3 to 3
- norm2_gain: bfloat16 [512], P('fsdp'), may hold values from 0.099609375 to 1.8984375
- norm2_bias: bfloat16 [512], P('fsdp'), may hold values from -3 to 3
- fc1_weight: bfloat16 [512, 2048], P('fsdp'), may hold values from -0.25 to 0.25
- fc1_bias: bfloat16 [2048], P('fsdp'), may hold values from -3 to 3
- fc2_weight: bfloat16 [2048, 512], P('fsdp'), may hold values from -0.125 to 0.125
- fc2_bias: bfloat16 [512], P('fsdp'), may hold values from -3 to 3
- bias_table: float32 [169, 16], replicated, may hold values from -4 to 4
- regions: int32 [2, 2, 49], P('win'), may hold values from 0 to 3
- rel_index: int32 [49, 49], replicated, may hold values from 0 to 168
- cotangent: bfloat16 [512, 14, 14, 512], P('fsdp', 'win'), may hold values from -6 to 6
Outputs:
- activations: bfloat16 [512, 14, 14, 512], P('fsdp', 'win')
- input_grad: float32 [512, 14, 14, 512], P('fsdp', 'win')
- norm1_gain_grad: float32 [512], P('fsdp')
- norm1_bias_grad: float32 [512], P('fsdp')
- qkv_weight_grad: float32 [512, 1536], P('fsdp')
- q_bias_grad: float32 [512], P('fsdp')
- v_bias_grad: float32 [512], P('fsdp')
- proj_weight_grad: float32 [512, 512], P('fsdp')
- proj_bias_grad: float32 [512], P('fsdp')
- norm2_gain_grad: float32 [512], P('fsdp')
- norm2_bias_grad: float32 [512], P('fsdp')
- fc1_weight_grad: float32 [512, 2048], P('fsdp')
- fc1_bias_grad: float32 [2048], P('fsdp')
- fc2_weight_grad: float32 [2048, 512], P('fsdp')
- fc2_bias_grad: float32 [512], P('fsdp')
- bias_table_grad: float32 [169, 16], replicated
All inputs are finite; a program needn't handle non-finite values.
Results may differ from a plain program's by a relative error of at most 0.014.
Values may be sent and summed in bfloat16 or wider, within the bound.
A program may use at most 320 MiB of HBM per device.

v0:
```python
import jax
import jax.numpy as jnp
from jax import lax
from jax.sharding import PartitionSpec as P

HEADS = 16
HD = 32
WIN = 7
SHIFT = 3
MICRO = 4


EPS = 1e-05
HIGHEST = lax.Precision.HIGHEST


def shifted(array, axis, by):
    length = lax.axis_size(axis)
    return lax.ppermute(array, axis, [(i, (i + by) % length) for i in range(length)])


def in_blocks(array, dim, length):
    shape = array.shape
    blocks = array.reshape(*shape[:dim], length, shape[dim] // length, *shape[dim + 1 :])
    return jnp.moveaxis(blocks, dim, 0)


def summed_on_arrival(array, axis, dim):
    length = lax.axis_size(axis)
    blocks = lax.all_to_all(in_blocks(array, dim, length), axis, 0, 0, tiled=True)
    return jnp.sum(blocks.astype(jnp.float32), axis=0)


def side_by_side(arrays, axis, dim, along):
    columns = [a.reshape(*a.shape[:along], -1) for a in arrays]
    both = jnp.concatenate(columns, axis=along)
    result, at, finished = (summed_on_arrival(both, axis, dim), 0, [])
    for a, column in zip(arrays, columns):
        slab = result[..., at : at + column.shape[along]]
        finished.append(slab.reshape(*slab.shape[:along], *a.shape[along:]))
        at += column.shape[along]
    return tuple(finished)


def shortened(array):

    def short(part):
        return part.astype(jnp.bfloat16) if part.dtype == jnp.float32 else part

    return jax.tree.map(short, array)


def layer_norm(values, norm_gain, norm_bias):
    average = jnp.mean(values, axis=-1, keepdims=True)
    centered = values - average
    variance = jnp.mean(centered * centered, axis=-1, keepdims=True)
    return centered * lax.rsqrt(variance + EPS) * norm_gain + norm_bias


def gelu_exact(values):
    return 0.5 * values * (1.0 + jax.scipy.special.erf(values * 0.7071067811865476))


def to_windows(field_map):
    image_count = field_map.shape[0]
    feat_width = field_map.shape[-1]
    win_rows = field_map.shape[1] // WIN
    win_cols = field_map.shape[2] // WIN
    shaped = field_map.reshape(image_count, win_rows, WIN, win_cols, WIN, feat_width)
    return shaped.transpose(0, 1, 3, 2, 4, 5).reshape(
        image_count, win_rows * win_cols, WIN * WIN, feat_width
    )


def from_windows(window_rows, win_rows, win_cols):
    image_count = window_rows.shape[0]
    feat_width = window_rows.shape[-1]
    shaped = window_rows.reshape(image_count, win_rows, win_cols, WIN, WIN, feat_width)
    return shaped.transpose(0, 1, 3, 2, 4, 5).reshape(
        image_count, win_rows * WIN, win_cols * WIN, feat_width
    )


def rows_ahead(field_map):
    incoming = shifted(field_map[:, :SHIFT], "win", -1)
    joined = jnp.concatenate([field_map[:, SHIFT:], incoming], axis=1)
    return jnp.roll(joined, -SHIFT, axis=2)


def rows_behind(field_map):
    local_height = field_map.shape[1]
    incoming = shifted(field_map[:, local_height - SHIFT :], "win", 1)
    joined = jnp.concatenate([incoming, field_map[:, : local_height - SHIFT]], axis=1)
    return jnp.roll(joined, SHIFT, axis=2)


def grad_ahead(field_map):
    incoming = shifted(field_map[:, :SHIFT], "win", -1)
    joined = jnp.concatenate([field_map[:, SHIFT:], incoming], axis=1)
    return jnp.roll(joined, -SHIFT, axis=2)


def grad_behind(field_map):
    local_height = field_map.shape[1]
    incoming = shifted(field_map[:, local_height - SHIFT :], "win", 1)
    joined = jnp.concatenate([incoming, field_map[:, : local_height - SHIFT]], axis=1)
    return jnp.roll(joined, SHIFT, axis=2)


def attention_scores(queries, key_rows, relative, mask_add):
    head_shape = queries.shape[:3] + (HEADS, HD)
    scores = jnp.einsum(
        "bnthe,bnshe->bnhts",
        queries.reshape(head_shape),
        key_rows.reshape(head_shape),
        preferred_element_type=jnp.float32,
    ) * HD ** (-0.5)
    return scores + relative[None, None] + mask_add[None, :, None]


def forward_pass(micro_images, weights, relative, mask_add):
    (
        norm1_gain,
        norm1_bias,
        qkv_weight,
        q_bias,
        v_bias,
        proj_weight,
        proj_bias,
        norm2_gain,
        norm2_bias,
        fc1_weight,
        fc1_bias,
        fc2_weight,
        fc2_bias,
    ) = weights
    feat_width = micro_images.shape[-1]
    local_rows = micro_images.shape[1] // WIN
    local_cols = micro_images.shape[2] // WIN
    source = micro_images.astype(jnp.float32)
    normed = layer_norm(
        source, norm1_gain.astype(jnp.float32), norm1_bias.astype(jnp.float32)
    ).astype(jnp.bfloat16)
    window_rows = to_windows(rows_ahead(normed))
    qkv_rows = jnp.einsum(
        "bntd,de->bnte", window_rows, qkv_weight, preferred_element_type=jnp.float32
    )
    queries = (qkv_rows[..., :feat_width] + q_bias.astype(jnp.float32)).astype(jnp.bfloat16)
    key_rows = qkv_rows[..., feat_width : 2 * feat_width].astype(jnp.bfloat16)
    value_rows = (qkv_rows[..., 2 * feat_width :] + v_bias.astype(jnp.float32)).astype(jnp.bfloat16)
    head_shape = queries.shape[:3] + (HEADS, HD)
    scores = attention_scores(queries, key_rows, relative, mask_add)
    row_peak = jnp.max(scores, axis=-1, keepdims=True)
    raised = jnp.exp(scores - row_peak)
    row_total = jnp.sum(raised, axis=-1, keepdims=True)
    attn_probs = raised / row_total
    log_total = row_peak + jnp.log(row_total)
    attended = jnp.einsum(
        "bnhts,bnshe->bnthe",
        attn_probs.astype(jnp.bfloat16),
        value_rows.reshape(head_shape),
        preferred_element_type=jnp.float32,
    )
    attended = attended.reshape(queries.shape).astype(jnp.bfloat16)
    unrolled = rows_behind(from_windows(attended, local_rows, local_cols))
    projected = jnp.einsum(
        "bijd,de->bije", unrolled, proj_weight, preferred_element_type=jnp.float32
    )
    middle = source + projected + proj_bias.astype(jnp.float32)
    normed2 = layer_norm(
        middle, norm2_gain.astype(jnp.float32), norm2_bias.astype(jnp.float32)
    ).astype(jnp.bfloat16)
    hidden = jnp.einsum(
        "bijd,df->bijf", normed2, fc1_weight, preferred_element_type=jnp.float32
    ) + fc1_bias.astype(jnp.float32)
    active = gelu_exact(hidden).astype(jnp.bfloat16)
    branch = jnp.einsum(
        "bijf,fe->bije", active, fc2_weight, preferred_element_type=jnp.float32
    ) + fc2_bias.astype(jnp.float32)
    output = (middle + branch).astype(jnp.bfloat16)
    kept_values = (
        window_rows,
        queries,
        key_rows,
        value_rows,
        log_total,
        unrolled,
        middle,
        normed2,
        hidden,
        active,
    )
    return (output, kept_values)


def backward_pass(micro_images, micro_grad, weights, kept_values, relative, mask_add):
    (
        norm1_gain,
        norm1_bias,
        qkv_weight,
        q_bias,
        v_bias,
        proj_weight,
        proj_bias,
        norm2_gain,
        norm2_bias,
        fc1_weight,
        fc1_bias,
        fc2_weight,
        fc2_bias,
    ) = weights
    (
        window_rows,
        queries,
        key_rows,
        value_rows,
        log_total,
        unrolled,
        middle,
        normed2,
        hidden,
        active,
    ) = kept_values
    local_rows = micro_images.shape[1] // WIN
    local_cols = micro_images.shape[2] // WIN
    sum_axes = (0, 1, 2)
    grad_out = micro_grad.astype(jnp.float32)
    fc2_w_grad = jnp.einsum("bijf,bije->fe", active, micro_grad, preferred_element_type=jnp.float32)
    fc2_b_grad = jnp.sum(grad_out, axis=sum_axes)
    grad_active = jnp.einsum(
        "bije,fe->bijf", micro_grad, fc2_weight, preferred_element_type=jnp.float32
    )
    _, gelu_back = jax.vjp(gelu_exact, hidden)
    grad_hidden = gelu_back(grad_active)[0].astype(jnp.bfloat16)
    fc1_w_grad = jnp.einsum(
        "bijd,bijf->df", normed2, grad_hidden, preferred_element_type=jnp.float32
    )
    fc1_b_grad = jnp.sum(grad_hidden.astype(jnp.float32), axis=sum_axes)
    grad_normed2 = jnp.einsum(
        "bijf,df->bijd", grad_hidden, fc1_weight, preferred_element_type=jnp.float32
    )
    _, norm2_back = jax.vjp(
        layer_norm, middle, norm2_gain.astype(jnp.float32), norm2_bias.astype(jnp.float32)
    )
    grad_mid_part, norm2_g_grad, norm2_b_grad = norm2_back(grad_normed2)
    grad_middle = grad_out + grad_mid_part
    grad_proj = grad_middle.astype(jnp.bfloat16)
    proj_w_grad = jnp.einsum(
        "bijd,bije->de", unrolled, grad_proj, preferred_element_type=jnp.float32
    )
    proj_b_grad = jnp.sum(grad_proj.astype(jnp.float32), axis=sum_axes)
    grad_unrolled = jnp.einsum(
        "bije,de->bijd", grad_proj, proj_weight, preferred_element_type=jnp.float32
    ).astype(jnp.bfloat16)
    grad_attended = to_windows(grad_ahead(grad_unrolled))
    head_shape = queries.shape[:3] + (HEADS, HD)
    grad_heads = grad_attended.reshape(head_shape)
    scores = attention_scores(queries, key_rows, relative, mask_add)
    attn_probs = jnp.exp(scores - log_total)
    grad_probs = jnp.einsum(
        "bnthe,bnshe->bnhts",
        grad_heads,
        value_rows.reshape(head_shape),
        preferred_element_type=jnp.float32,
    )
    grad_values = jnp.einsum(
        "bnhts,bnthe->bnshe",
        attn_probs.astype(jnp.bfloat16),
        grad_heads,
        preferred_element_type=jnp.float32,
    ).astype(jnp.bfloat16)
    row_inner = jnp.sum(grad_probs * attn_probs, axis=-1, keepdims=True)
    grad_scores = (attn_probs * (grad_probs - row_inner)).astype(jnp.bfloat16)
    bias_part = jnp.sum(grad_scores.astype(jnp.float32), axis=(0, 1))
    grad_query = (
        jnp.einsum(
            "bnhts,bnshe->bnthe",
            grad_scores,
            key_rows.reshape(head_shape),
            preferred_element_type=jnp.float32,
        )
        * HD ** (-0.5)
    ).astype(jnp.bfloat16)
    grad_keys = (
        jnp.einsum(
            "bnhts,bnthe->bnshe",
            grad_scores,
            queries.reshape(head_shape),
            preferred_element_type=jnp.float32,
        )
        * HD ** (-0.5)
    ).astype(jnp.bfloat16)
    grad_query = grad_query.reshape(queries.shape)
    grad_keys = grad_keys.reshape(queries.shape)
    grad_values = grad_values.reshape(queries.shape)
    grad_qkv = jnp.concatenate([grad_query, grad_keys, grad_values], axis=-1)
    qkv_w_grad = jnp.einsum(
        "bntd,bnte->de", window_rows, grad_qkv, preferred_element_type=jnp.float32
    )
    q_b_grad = jnp.sum(grad_query.astype(jnp.float32), axis=sum_axes)
    v_b_grad = jnp.sum(grad_values.astype(jnp.float32), axis=sum_axes)
    grad_windows = jnp.einsum(
        "bnte,de->bntd", grad_qkv, qkv_weight, preferred_element_type=jnp.float32
    ).astype(jnp.bfloat16)
    grad_normed = grad_behind(from_windows(grad_windows, local_rows, local_cols)).astype(
        jnp.float32
    )
    _, norm1_back = jax.vjp(
        layer_norm,
        micro_images.astype(jnp.float32),
        norm1_gain.astype(jnp.float32),
        norm1_bias.astype(jnp.float32),
    )
    grad_src_part, norm1_g_grad, norm1_b_grad = norm1_back(grad_normed)
    grad_input = grad_middle + grad_src_part
    grad_terms = (
        norm1_g_grad,
        norm1_b_grad,
        qkv_w_grad,
        q_b_grad,
        v_b_grad,
        proj_w_grad,
        proj_b_grad,
        norm2_g_grad,
        norm2_b_grad,
        fc1_w_grad,
        fc1_b_grad,
        fc2_w_grad,
        fc2_b_grad,
    )
    return (grad_input, grad_terms, bias_part)


def per_device(
    images,
    norm1_gain,
    norm1_bias,
    qkv_weight,
    q_bias,
    v_bias,
    proj_weight,
    proj_bias,
    norm2_gain,
    norm2_bias,
    fc1_weight,
    fc1_bias,
    fc2_weight,
    fc2_bias,
    bias_table,
    regions,
    rel_index,
    cotangent,
):
    shards = (
        norm1_gain,
        norm1_bias,
        qkv_weight,
        q_bias,
        v_bias,
        proj_weight,
        proj_bias,
        norm2_gain,
        norm2_bias,
        fc1_weight,
        fc1_bias,
        fc2_weight,
        fc2_bias,
    )
    batch_size = images.shape[0] // MICRO
    local_rows = images.shape[1] // WIN
    local_cols = images.shape[2] // WIN
    window_tokens = WIN * WIN
    flat_regions = regions.reshape(local_rows * local_cols, window_tokens)
    mask_add = jnp.where(flat_regions[:, :, None] == flat_regions[:, None, :], 0.0, -100.0).astype(
        jnp.float32
    )
    onehot_table = (
        rel_index.reshape(window_tokens * window_tokens, 1)
        == jnp.arange(bias_table.shape[0], dtype=jnp.int32)[None, :]
    ).astype(jnp.float32)
    relative = (
        jnp.dot(onehot_table, bias_table, precision=HIGHEST)
        .reshape(window_tokens, window_tokens, -1)
        .transpose(2, 0, 1)
    )
    outputs = []
    stored = []
    for micro_index in range(MICRO):
        micro_images = images[micro_index * batch_size : (micro_index + 1) * batch_size]
        weights = (
            lax.all_gather(shards[0], "fsdp", axis=0, tiled=True),
            lax.all_gather(shards[1], "fsdp", axis=0, tiled=True),
            lax.all_gather(shards[2], "fsdp", axis=0, tiled=True),
            lax.all_gather(shards[3], "fsdp", axis=0, tiled=True),
            lax.all_gather(shards[4], "fsdp", axis=0, tiled=True),
            lax.all_gather(shards[5], "fsdp", axis=0, tiled=True),
            lax.all_gather(shards[6], "fsdp", axis=0, tiled=True),
            lax.all_gather(shards[7], "fsdp", axis=0, tiled=True),
            lax.all_gather(shards[8], "fsdp", axis=0, tiled=True),
            lax.all_gather(shards[9], "fsdp", axis=0, tiled=True),
            lax.all_gather(shards[10], "fsdp", axis=0, tiled=True),
            lax.all_gather(shards[11], "fsdp", axis=0, tiled=True),
            lax.all_gather(shards[12], "fsdp", axis=0, tiled=True),
        )
        output, kept_values = forward_pass(micro_images, weights, relative, mask_add)
        outputs.append(output)
        stored.append(kept_values)
    grad_inputs = []
    grad_total = None
    bias_total = jnp.zeros(relative.shape, jnp.float32)
    for micro_index in range(MICRO):
        micro_images = images[micro_index * batch_size : (micro_index + 1) * batch_size]
        micro_grad = cotangent[micro_index * batch_size : (micro_index + 1) * batch_size]
        weights = (
            lax.all_gather(shards[0], "fsdp", axis=0, tiled=True),
            lax.all_gather(shards[1], "fsdp", axis=0, tiled=True),
            lax.all_gather(shards[2], "fsdp", axis=0, tiled=True),
            lax.all_gather(shards[3], "fsdp", axis=0, tiled=True),
            lax.all_gather(shards[4], "fsdp", axis=0, tiled=True),
            lax.all_gather(shards[5], "fsdp", axis=0, tiled=True),
            lax.all_gather(shards[6], "fsdp", axis=0, tiled=True),
            lax.all_gather(shards[7], "fsdp", axis=0, tiled=True),
            lax.all_gather(shards[8], "fsdp", axis=0, tiled=True),
            lax.all_gather(shards[9], "fsdp", axis=0, tiled=True),
            lax.all_gather(shards[10], "fsdp", axis=0, tiled=True),
            lax.all_gather(shards[11], "fsdp", axis=0, tiled=True),
            lax.all_gather(shards[12], "fsdp", axis=0, tiled=True),
        )
        grad_input, grad_terms, bias_part = backward_pass(
            micro_images, micro_grad, weights, stored[micro_index], relative, mask_add
        )
        grad_inputs.append(grad_input)
        grad_total = (
            grad_terms if micro_index == 0 else jax.tree.map(jnp.add, grad_total, grad_terms)
        )
        bias_total = bias_total + bias_part
    shard_grads = (
        summed_on_arrival(grad_total[0].astype(jnp.bfloat16), "fsdp", 0),
        *side_by_side(
            (
                grad_total[1].astype(jnp.bfloat16),
                grad_total[2].astype(jnp.bfloat16),
                grad_total[3].astype(jnp.bfloat16),
                grad_total[4].astype(jnp.bfloat16),
                grad_total[5].astype(jnp.bfloat16),
                grad_total[6].astype(jnp.bfloat16),
                grad_total[7].astype(jnp.bfloat16),
                grad_total[8].astype(jnp.bfloat16),
                grad_total[9].astype(jnp.bfloat16),
            ),
            "fsdp",
            0,
            1,
        ),
        *side_by_side(
            (grad_total[10].astype(jnp.bfloat16), grad_total[11].astype(jnp.bfloat16)), "fsdp", 0, 1
        ),
        summed_on_arrival(grad_total[12].astype(jnp.bfloat16), "fsdp", 0),
    )
    shard_grads = jax.tree.map(
        lambda part: part.astype(jnp.float32), lax.psum(shortened(shard_grads), "win")
    )
    table_part = jnp.dot(
        onehot_table.T,
        bias_total.transpose(1, 2, 0).reshape(window_tokens * window_tokens, -1),
        precision=HIGHEST,
    )
    table_grad = lax.psum(table_part, ("fsdp", "win"))
    return (
        jnp.concatenate(outputs, axis=0),
        jnp.concatenate(grad_inputs, axis=0),
        shard_grads[0],
        shard_grads[1],
        shard_grads[2],
        shard_grads[3],
        shard_grads[4],
        shard_grads[5],
        shard_grads[6],
        shard_grads[7],
        shard_grads[8],
        shard_grads[9],
        shard_grads[10],
        shard_grads[11],
        shard_grads[12],
        table_grad,
    )


def solution(mesh):
    in_specs = (
        P("fsdp", "win", None, None),
        P("fsdp"),
        P("fsdp"),
        P("fsdp", None),
        P("fsdp"),
        P("fsdp"),
        P("fsdp", None),
        P("fsdp"),
        P("fsdp"),
        P("fsdp"),
        P("fsdp", None),
        P("fsdp"),
        P("fsdp", None),
        P("fsdp"),
        P(),
        P("win", None, None),
        P(),
        P("fsdp", "win", None, None),
    )
    out_specs = (
        P("fsdp", "win", None, None),
        P("fsdp", "win", None, None),
        P("fsdp"),
        P("fsdp"),
        P("fsdp", None),
        P("fsdp"),
        P("fsdp"),
        P("fsdp", None),
        P("fsdp"),
        P("fsdp"),
        P("fsdp"),
        P("fsdp", None),
        P("fsdp"),
        P("fsdp", None),
        P("fsdp"),
        P(),
    )
    return jax.shard_map(
        per_device, mesh=mesh, in_specs=in_specs, out_specs=out_specs, check_vma=False
    )
```

profile of v0, /device:TPU:0, one launch (start us, length us, event | category | flops | bytes accessed | tf_op | source)
XLA Modules:
  0.0 962.0 jit_solution(2914355139419629172)
XLA Ops:
  17.4 45.1 %all-reduce.8 = (bf16[512]{0:T(512)(128)(2,1)S(1)}, bf16[512]{0:T(512)(128)(2,1)S(1)}, bf16[512]{0:T(512)(128)(2,1)S(1)}, bf16[512]{0:T(512)(128)(2,1)S(1)}, bf1...) all-reduce(bf16[512]{0:T(512)(128)(2,1)S(1)} %dynamic-update-slice., ...), channel_id=1, replica_groups=mesh['fsdp'=16,'win'=2] {'fsdp'}, use_global_device_ids=true, to_apply=%add.4 | all-reduce | flops 4096 | bytes 16384
  76.0 41.3 %all_gather.31 = bf16[512,512]{1,0:T(8,128)(2,1)} all-gather(bf16[32,512]{1,0:T(8,128)(2,1)S(1)} %copy-done.233), channel_id=1, replica_groups=mesh['fsdp'=16,'win'=2] {'fsdp'}, dimensions={0}, use_global_device_ids=true | all-gather | bytes 557056 | tf_op jit(solution)/shard_map/all_gather | solution.py:396
  117.5 3.7 fusion.247
  129.0 37.9 %all-gather = bf16[16,1,128]{2,1,0:T(2,128)(2,1)S(1)} all-gather(bf16[1,1,128]{2,1,0:T(2,128)(2,1)S(1)} %bitcast.572), channel_id=1, replica_groups=mesh['fsdp'=16,'win'=2] {'fsdp'}, dimensions={0}, use_global_device_ids=true | all-gather | bytes 4352 | tf_op jit(solution)/shard_map/all_gather | solution.py:401
  201.7 15.9 %fusion.131 = (bf16[8,2,49,512]{3,0,2,1:T(8,128)(2,1)}, bf16[8,2,49,512]{3,0,2,1:T(8,128)(2,1)}, bf16[8,2,49,512]{3,0,2,1:T(8,128)(2,1)}, bf16[8,2,49,512]{3,0,2,1:T(8,128)(2,1)}) fusion(f32[8,2,49,512]{3,2,1,0:T(8,128)S(1)} %get-tuple-element.175, f32[512]{0:T(512)S(1)} %convert_element_type.690, f32[8,2,49,512]{3,2,1,0:T(8,128)S(1)} %get-tuple-element.177, ...), kind=kLoop, calls=%fused_computation.281 | loop fusion | flops 3211264 | bytes 9635840 | tf_op jit(solution)/shard_map/convert_element_type | solution.py:150
  220.6 8.0 fusion.130
  234.4 4.5 fusion.249
  245.2 7.2 copy.617
  252.4 5.8 convert_element_type.735
  270.1 4.5 fusion.253
  298.8 4.5 fusion.255
  319.6 7.2 copy.602
  326.8 5.4 convert_element_type.724
  335.0 7.2 copy.587
  342.2 5.4 convert_element_type.713
  350.4 7.2 copy.572
  357.6 5.8 convert_element_type.697
  380.7 6.8 fusion.76
  387.6 8.8 convert_reduce_fusion.4
  396.4 4.3 multiply_reduce_fusion.4
  405.3 8.5 convert_reduce_fusion.5
  413.7 4.3 fusion.70
  418.1 10.5 %multiply_convert_fusion.7 = (bf16[8,7,14,2048]{3,2,1,0:T(8,128)(2,1)}, bf16[8,7,14,2048]{3,2,1,0:T(8,128)(2,1)}, bf16[8,7,14,2048]{3,2,1,0:T(8,128)(2,1)}, bf16...) fusion(f32[2048]{0:T(1024)S(1)} %bitcast.559, f32[8,7,14,2048]{3,2,1,0:T(8,128)S(1)} %bitcast.512, ...), kind=kOutput, calls=%fused_computation.40 | convolution fusion | flops 1684709376 | bytes 42256512 | tf_op jit(solution)/shard_map/bijd,df->bijf/dot_general | solution.py:173
  428.6 8.7 convert_reduce_fusion.7
  437.3 3.4 fusion.74
  440.8 6.7 convert_reduce_fusion.6
  447.5 7.1 multiply_reduce_fusion.6
  470.5 4.6 fusion.234
  475.1 4.5 fusion.233
  479.6 4.6 fusion.232
  492.7 4.6 fusion.196
  502.3 4.4 fusion.8
  512.1 4.6 all-to-all-start.2
  516.7 10.1 %fusion.9 = bf16[512,2048]{1,0:T(8,128)(2,1)} fusion(f32[512,2048,1,1]{1,0,3,2:T(8,128)} %fusion.234, f32[512,2048,1,1]{1,0,3,2:T(8,128)} %fusion.233, f32[512,2048,1,1]{1,0,3,2:T(8,128)} %fusion.232, bf16[8,7,14,2048]{3,2,1,0:T(8,128)(2,1)} %copy-done.261, f32[8,7,14,512]{3,2,1,0:T(8,128)S(1)} %copy-done.137, f32[8,7,14]{2,1,0:T(8,128)S(1)} %copy-done.236, ...), kind=kOutput, calls=%fused_computation.58 | convolution fusion | flops 1650368512 | bytes 19507328 | tf_op jit(solution)/shard_map/bijd,bijf->df/dot_general | solution.py:235
  536.6 6.0 copy.678
  542.7 7.8 convert_reduce_fusion.8
  552.9 3.9 convert_reduce_fusion
  556.8 3.3 multiply_convert_fusion.8
  581.6 6.2 copy.660
  587.8 7.8 convert_reduce_fusion.9
  598.1 3.5 convert_reduce_fusion.1
  601.6 3.3 multiply_convert_fusion.10
  624.5 4.8 reshape_reshape.12
  629.3 5.9 copy.624
  635.2 7.8 convert_reduce_fusion.11
  645.5 3.5 convert_reduce_fusion.3
  671.7 4.8 reshape_reshape.13
  676.5 6.1 copy.642
  682.6 7.8 convert_reduce_fusion.10
  692.8 3.5 convert_reduce_fusion.2
  744.1 3.4 fusion.122
  747.7 4.8 fusion.123
  753.2 4.9 convert_reduce_fusion.24
  758.1 4.8 convert_reduce_fusion.25
  764.5 9.1 concatenate.173
  773.6 7.2 all-to-all-start.1
  780.9 4.9 add_convert_fusion.4
  794.0 3.6 copy.708
  804.9 94.7 %psum.111 = f32[169,16]{0,1:T(8,128)} all-reduce(f32[169,16]{0,1:T(8,128)} %fusion.46), channel_id=1, replica_groups=mesh['fsdp'=16,'win'=2] {'fsdp','win'}, use_global_device_ids=true, to_apply=%region_101.102 | all-reduce | flops 2704 | bytes 21632 | tf_op jit(solution)/shard_map/psum | solution.py:468
  902.5 4.4 convert_reduce_fusion.26
  909.9 6.7 all-to-all-start
  924.7 6.9 all-to-all-start.3
  934.8 6.4 copy.709
  941.6 3.5 all-reduce.9
  (934 shorter events, 368.7 us)
Async XLA Ops:
  7.2 114.0 %copy-start = (f32[169,16]{0,1:T(8,128)S(1)}, f32[169,16]{0,1:T(8,128)}, u32[]{:S(2)}) copy-start(f32[169,16]{0,1:T(8,128)} %param.32) | copy-start | bytes 32452
  7.2 175.4 %all-gather.5.cloned.1.call-start = ((), (), s32[]{:S(2)}) async-start(), calls=%async_computation.4 | async-start | bytes 1671168 | tf_op jit(solution)/shard_map/all_gather | solution.py:393
  7.9 372.8 %all-gather.7.cloned.1.call-start = ((), (), s32[]{:S(2)}) async-start(), calls=%async_computation.5 | async-start | bytes 2228224 | tf_op jit(solution)/shard_map/all_gather | solution.py:400
  8.7 378.9 %all-gather.9.cloned.1.call-start = ((), (), s32[]{:S(2)}) async-start(), calls=%async_computation.6 | async-start | bytes 2228224 | tf_op jit(solution)/shard_map/all_gather | solution.py:402
  64.6 305.1 %copy-start.6 = (bf16[8,7,14,512]{3,0,2,1:T(8,128)(2,1)}, bf16[8,7,14,512]{3,0,2,1:T(8,128)(2,1)S(1)}, u32[]{:S(2)}) copy-start(bf16[8,7,14,512]{3,0,2,1:T(8,128)(2,1)S(1)} %get-tuple-element.189) | copy-start | bytes 2408452
  64.6 307.9 %copy-start.8 = (bf16[8,7,14,512]{3,0,2,1:T(8,128)(2,1)}, bf16[8,7,14,512]{3,0,2,1:T(8,128)(2,1)S(1)}, u32[]{:S(2)}) copy-start(bf16[8,7,14,512]{3,0,2,1:T(8,128)(2,1)S(1)} %get-tuple-element.187) | copy-start | bytes 2408452
  64.6 309.4 %copy-start.12 = (bf16[8,7,14,512]{3,0,2,1:T(8,128)(2,1)}, bf16[8,7,14,512]{3,0,2,1:T(8,128)(2,1)S(1)}, u32[]{:S(2)}) copy-start(bf16[8,7,14,512]{3,0,2,1:T(8,128)(2,1)S(1)} %get-tuple-element.188) | copy-start | bytes 2408452
  64.7 311.8 %copy-start.10 = (bf16[8,7,14,512]{3,0,2,1:T(8,128)(2,1)}, bf16[8,7,14,512]{3,0,2,1:T(8,128)(2,1)S(1)}, u32[]{:S(2)}) copy-start(bf16[8,7,14,512]{3,0,2,1:T(8,128)(2,1)S(1)} %get-tuple-element.186) | copy-start | bytes 2408452
  71.7 45.6 %copy-start.237 = (s32[49,49]{1,0:T(8,128)S(1)}, s32[49,49]{1,0:T(8,128)}, u32[]{:S(2)}) copy-start(s32[49,49]{1,0:T(8,128)} %param.34) | copy-start | bytes 28816
  72.5 94.4 %collective-permute-start = (bf16[8,3,14,512]{3,2,1,0:T(8,128)(2,1)}, bf16[8,3,14,512]{3,2,1,0:T(8,128)(2,1)}, u32[]{:S(2)}, u32[]{:S(2)}) collective-permute-start(bf16[8,3,14,512]{3,2,1,0:T(8,128)(2,1)} %slice.404), channel_id=1, source_target_pairs={{0,1},{1,0},{2,3},{3,2},{4,5},{5,4},{6,7},{7,6},{8,9},{9,8},{10,11... | collective-permute-start | bytes 1032200 | tf_op jit(solution)/shard_map/ppermute | solution.py:19
  73.8 97.2 %collective-permute-start.2 = (bf16[8,3,14,512]{3,2,1,0:T(8,128)(2,1)}, bf16[8,3,14,512]{3,2,1,0:T(8,128)(2,1)}, u32[]{:S(2)}, u32[]{:S(2)}) collective-permute-start(bf16[8,3,14,512]{3,2,1,0:T(8,128)(2,1)} %slice.415), channel_id=1, source_target_pairs={{0,1},{1,0},{2,3},{3,2},{4,5},{5,4},{6,7},{7,6},{8,9},{9,8},{10,11... | collective-permute-start | bytes 1032200 | tf_op jit(solution)/shard_map/ppermute | solution.py:19
  74.6 100.3 %collective-permute-start.4 = (bf16[8,3,14,512]{3,2,1,0:T(8,128)(2,1)}, bf16[8,3,14,512]{3,2,1,0:T(8,128)(2,1)}, u32[]{:S(2)}, u32[]{:S(2)}) collective-permute-start(bf16[8,3,14,512]{3,2,1,0:T(8,128)(2,1)} %slice.426), channel_id=1, source_target_pairs={{0,1},{1,0},{2,3},{3,2},{4,5},{5,4},{6,7},{7,6},{8,9},{9,8},{10,11... | collective-permute-start | bytes 1032200 | tf_op jit(solution)/shard_map/ppermute | solution.py:19
  75.8 102.9 %collective-permute-start.6 = (bf16[8,3,14,512]{3,2,1,0:T(8,128)(2,1)}, bf16[8,3,14,512]{3,2,1,0:T(8,128)(2,1)}, u32[]{:S(2)}, u32[]{:S(2)}) collective-permute-start(bf16[8,3,14,512]{3,2,1,0:T(8,128)(2,1)} %slice.437), channel_id=1, source_target_pairs={{0,1},{1,0},{2,3},{3,2},{4,5},{5,4},{6,7},{7,6},{8,9},{9,8},{10,11... | collective-permute-start | bytes 1032200 | tf_op jit(solution)/shard_map/ppermute | solution.py:19
  125.9 246.6 %copy-start.247 = (f32[512]{0:T(512)}, f32[512]{0:T(512)S(1)}, u32[]{:S(2)}) copy-start(f32[512]{0:T(512)S(1)} %convert_element_type.698) | copy-start | bytes 6148
  129.0 39.4 %copy-start.80 = (bf16[8,4,14,512]{3,2,1,0:T(8,128)(2,1)S(1)}, bf16[8,4,14,512]{3,2,1,0:T(8,128)(2,1)}, u32[]{:S(2)}) copy-start(bf16[8,4,14,512]{3,2,1,0:T(8,128)(2,1)} %slice.403) | copy-start | bytes 1376260
  261.2 105.9 %collective-permute-start.7 = (bf16[8,3,14,512]{3,2,1,0:T(8,128)(2,1)}, bf16[8,3,14,512]{3,2,1,0:T(8,128)(2,1)}, u32[]{:S(2)}, u32[]{:S(2)}) collective-permute-start(bf16[8,3,14,512]{3,2,1,0:T(8,128)(2,1)} %copy.785), channel_id=1, source_target_pairs={{0,1},{1,0},{2,3},{3,2},{4,5},{5,4},{6,7},{7,6},{8,9},{9,8},{10,11... | collective-permute-start | bytes 1032200 | tf_op jit(solution)/shard_map/ppermute | solution.py:19
  364.9 3.5 collective-permute-start.5
  365.6 3.1 collective-permute-start.3
  365.8 3.6 collective-permute-start.1
  371.2 25.2 %copy-start.222 = (f32[8,7,14]{2,1,0:T(8,128)}, f32[8,7,14]{2,1,0:T(8,128)S(1)}, u32[]{:S(2)}) copy-start(f32[8,7,14]{2,1,0:T(8,128)S(1)} %broadcast_multiply_fusion) | copy-start | bytes 9412
  380.0 16.5 %copy-start.234 = (f32[8,7,14]{2,1,0:T(8,128)}, f32[8,7,14]{2,1,0:T(8,128)S(1)}, u32[]{:S(2)}) copy-start(f32[8,7,14]{2,1,0:T(8,128)S(1)} %fusion.220) | copy-start | bytes 9412
  380.0 20.7 %copy-start.196 = (f32[8,7,14]{2,1,0:T(8,128)}, f32[8,7,14]{2,1,0:T(8,128)S(1)}, u32[]{:S(2)}) copy-start(f32[8,7,14]{2,1,0:T(8,128)S(1)} %fusion.218) | copy-start | bytes 9412
  387.6 8.9 copy-start.126
  403.0 15.0 %slice-start.8 = ((s8[7340032]{0:T(1024)(128)(4,1)}), s8[4194304]{0:T(1024)(128)(4,1)S(1)}, s32[]{:S(2)}) async-start(s8[7340032]{0:T(1024)(128)(4,1)} %bitcast.511), calls=%async_computation.16 | async-start | bytes 8388608
  405.2 12.8 %slice-start.9 = ((s8[7340032]{0:T(1024)(128)(4,1)}), s8[3145728]{0:T(1024)(128)(4,1)S(1)}, s32[]{:S(2)}) async-start(s8[7340032]{0:T(1024)(128)(4,1)} %bitcast.511), calls=%async_computation.17 | async-start | bytes 6291456
  418.1 10.5 %copy-start.71 = (bf16[8,7,14,512]{3,0,2,1:T(8,128)(2,1)S(1)}, bf16[8,7,14,512]{3,0,2,1:T(8,128)(2,1)}, u32[]{:S(2)}) copy-start(bf16[8,7,14,512]{3,0,2,1:T(8,128)(2,1)} %get-tuple-element.184) | copy-start | bytes 2408452
  457.4 28.9 %copy-start.44 = (f32[8,7,14,512]{3,2,1,0:T(8,128)}, f32[8,7,14,512]{3,2,1,0:T(8,128)S(1)}, u32[]{:S(2)}) copy-start(f32[8,7,14,512]{3,2,1,0:T(8,128)S(1)} %get-tuple-element.213) | copy-start | bytes 4816900
  462.8 21.4 %copy-start.156 = (bf16[8,7,14,512]{3,2,1,0:T(8,128)(2,1)}, bf16[8,7,14,512]{3,2,1,0:T(8,128)(2,1)S(1)}, u32[]{:S(2)}) copy-start(bf16[8,7,14,512]{3,2,1,0:T(8,128)(2,1)S(1)} %convolution_convert_fusion) | copy-start | bytes 2408452
  466.2 18.7 %copy-start.158 = (bf16[8,7,14,512]{3,2,1,0:T(8,128)(2,1)}, bf16[8,7,14,512]{3,2,1,0:T(8,128)(2,1)S(1)}, u32[]{:S(2)}) copy-start(bf16[8,7,14,512]{3,2,1,0:T(8,128)(2,1)S(1)} %convolution_convert_fusion.1) | copy-start | bytes 2408452
  484.9 45.8 %collective-permute-start.14 = (bf16[8,3,14,512]{3,2,1,0:T(8,128)(2,1)}, bf16[8,3,14,512]{3,2,1,0:T(8,128)(2,1)}, u32[]{:S(2)}, u32[]{:S(2)}) collective-permute-start(bf16[8,3,14,512]{3,2,1,0:T(8,128)(2,1)} %slice.472), channel_id=1, source_target_pairs={{0,1},{1,0},{2,3},{3,2},{4,5},{5,4},{6,7},{7,6},{8,9},{9,8},{10,11... | collective-permute-start | bytes 1032200 | tf_op jit(solution)/shard_map/ppermute | solution.py:19
  485.8 89.9 %collective-permute-start.12 = (bf16[8,3,14,512]{3,2,1,0:T(8,128)(2,1)}, bf16[8,3,14,512]{3,2,1,0:T(8,128)(2,1)}, u32[]{:S(2)}, u32[]{:S(2)}) collective-permute-start(bf16[8,3,14,512]{3,2,1,0:T(8,128)(2,1)} %slice.464), channel_id=1, source_target_pairs={{0,1},{1,0},{2,3},{3,2},{4,5},{5,4},{6,7},{7,6},{8,9},{9,8},{10,11... | collective-permute-start | bytes 1032200 | tf_op jit(solution)/shard_map/ppermute | solution.py:19
  489.4 131.2 %collective-permute-start.8 = (bf16[8,3,14,512]{3,2,1,0:T(8,128)(2,1)}, bf16[8,3,14,512]{3,2,1,0:T(8,128)(2,1)}, u32[]{:S(2)}, u32[]{:S(2)}) collective-permute-start(bf16[8,3,14,512]{3,2,1,0:T(8,128)(2,1)} %slice.448), channel_id=1, source_target_pairs={{0,1},{1,0},{2,3},{3,2},{4,5},{5,4},{6,7},{7,6},{8,9},{9,8},{10,11... | collective-permute-start | bytes 1032200 | tf_op jit(solution)/shard_map/ppermute | solution.py:19
  489.4 178.4 %collective-permute-start.10 = (bf16[8,3,14,512]{3,2,1,0:T(8,128)(2,1)}, bf16[8,3,14,512]{3,2,1,0:T(8,128)(2,1)}, u32[]{:S(2)}, u32[]{:S(2)}) collective-permute-start(bf16[8,3,14,512]{3,2,1,0:T(8,128)(2,1)} %slice.456), channel_id=1, source_target_pairs={{0,1},{1,0},{2,3},{3,2},{4,5},{5,4},{6,7},{7,6},{8,9},{9,8},{10,11... | collective-permute-start | bytes 1032200 | tf_op jit(solution)/shard_map/ppermute | solution.py:19
  512.1 261.5 %all-to-all-start.2 = ((bf16[16,128,513]{1,2,0:T(8,128)(2,1)}), bf16[16,128,513]{1,2,0:T(8,128)(2,1)}, u32[]{:S(2)}, u32[]{:S(2)}) async-start(bf16[16,128,513]{1,2,0:T(8,128)(2,1)} %pad_maximum_fusion.6), calls=%async_computation.2 | async-start | bytes 4259840 | tf_op jit(solution)/shard_map/all_to_all | solution.py:30
  516.7 10.1 %copy-start.163 = (bf16[8,7,14,512]{3,2,1,0:T(8,128)(2,1)S(1)}, bf16[8,7,14,512]{3,2,1,0:T(8,128)(2,1)}, u32[]{:S(2)}) copy-start(bf16[8,7,14,512]{3,2,1,0:T(8,128)(2,1)} %copy-done.162) | copy-start | bytes 2408452
  516.7 10.1 %copy-start.184 = (bf16[8,7,14,512]{3,2,1,0:T(8,128)(2,1)S(1)}, bf16[8,7,14,512]{3,2,1,0:T(8,128)(2,1)}, u32[]{:S(2)}) copy-start(bf16[8,7,14,512]{3,2,1,0:T(8,128)(2,1)} %copy-done.183) | copy-start | bytes 2408452
  516.7 10.1 %copy-start.213 = (bf16[8,7,3,512]{3,2,1,0:T(4,128)(2,1)S(1)}, bf16[8,7,3,512]{3,2,1,0:T(4,128)(2,1)}, u32[]{:S(2)}) copy-start(bf16[8,7,3,512]{3,2,1,0:T(4,128)(2,1)} %copy-done.212) | copy-start | bytes 516100
  516.7 10.1 %copy-start.262 = (f32[512,512]{1,0:T(8,128)S(1)}, f32[512,512]{1,0:T(8,128)}, u32[]{:S(2)}) copy-start(f32[512,512]{1,0:T(8,128)} %convolution_bitcast_fusion.4) | copy-start | bytes 3145732
  516.7 10.1 %copy-start.263 = (f32[512,512]{1,0:T(8,128)S(1)}, f32[512,512]{1,0:T(8,128)}, u32[]{:S(2)}) copy-start(f32[512,512]{1,0:T(8,128)} %convolution_bitcast_fusion.5) | copy-start | bytes 3145732
  516.7 10.1 %copy-start.264 = (f32[512,512]{1,0:T(8,128)S(1)}, f32[512,512]{1,0:T(8,128)}, u32[]{:S(2)}) copy-start(f32[512,512]{1,0:T(8,128)} %convolution_bitcast_fusion.6) | copy-start | bytes 3145732
  536.6 13.9 %slice-start.6 = ((s8[7340032]{0:T(1024)(128)(4,1)}), s8[3145728]{0:T(1024)(128)(4,1)S(1)}, s32[]{:S(2)}) async-start(s8[7340032]{0:T(1024)(128)(4,1)} %bitcast.461), calls=%async_computation.14 | async-start | bytes 6291456
  581.6 14.1 %slice-start.4 = ((s8[7340032]{0:T(1024)(128)(4,1)}), s8[3145728]{0:T(1024)(128)(4,1)S(1)}, s32[]{:S(2)}) async-start(s8[7340032]{0:T(1024)(128)(4,1)} %bitcast.459), calls=%async_computation.12 | async-start | bytes 6291456
  587.8 7.8 slice-start.5
  587.8 7.8 copy-start.28
  624.5 18.5 %slice-start.2 = ((s8[7340032]{0:T(1024)(128)(4,1)}), s8[3145728]{0:T(1024)(128)(4,1)S(1)}, s32[]{:S(2)}) async-start(s8[7340032]{0:T(1024)(128)(4,1)} %bitcast.457), calls=%async_computation.10 | async-start | bytes 6291456
  671.7 18.7 %slice-start = ((s8[7340032]{0:T(1024)(128)(4,1)}), s8[3145728]{0:T(1024)(128)(4,1)S(1)}, s32[]{:S(2)}) async-start(s8[7340032]{0:T(1024)(128)(4,1)} %bitcast.455), calls=%async_computation.8 | async-start | bytes 6291456
  682.5 7.8 slice-start.1
  721.6 16.8 %collective-permute-start.15 = (bf16[8,3,14,512]{3,2,1,0:T(8,128)(2,1)}, bf16[8,3,14,512]{3,2,1,0:T(8,128)(2,1)}, u32[]{:S(2)}, u32[]{:S(2)}) collective-permute-start(bf16[8,3,14,512]{3,2,1,0:T(8,128)(2,1)} %copy.797), channel_id=1, source_target_pairs={{0,1},{1,0},{2,3},{3,2},{4,5},{5,4},{6,7},{7,6},{8,9},{9,8},{10,11... | collective-permute-start | bytes 1032200 | tf_op jit(solution)/shard_map/ppermute | solution.py:19
  722.4 14.6 %collective-permute-start.13 = (bf16[8,3,14,512]{3,2,1,0:T(8,128)(2,1)}, bf16[8,3,14,512]{3,2,1,0:T(8,128)(2,1)}, u32[]{:S(2)}, u32[]{:S(2)}) collective-permute-start(bf16[8,3,14,512]{3,2,1,0:T(8,128)(2,1)} %copy.794), channel_id=1, source_target_pairs={{0,1},{1,0},{2,3},{3,2},{4,5},{5,4},{6,7},{7,6},{8,9},{9,8},{10,11... | collective-permute-start | bytes 1032200 | tf_op jit(solution)/shard_map/ppermute | solution.py:19
  723.8 15.8 %collective-permute-start.9 = (bf16[8,3,14,512]{3,2,1,0:T(8,128)(2,1)}, bf16[8,3,14,512]{3,2,1,0:T(8,128)(2,1)}, u32[]{:S(2)}, u32[]{:S(2)}) collective-permute-start(bf16[8,3,14,512]{3,2,1,0:T(8,128)(2,1)} %copy.788), channel_id=1, source_target_pairs={{0,1},{1,0},{2,3},{3,2},{4,5},{5,4},{6,7},{7,6},{8,9},{9,8},{10,11... | collective-permute-start | bytes 1032200 | tf_op jit(solution)/shard_map/ppermute | solution.py:19
  724.7 16.2 %collective-permute-start.11 = (bf16[8,3,14,512]{3,2,1,0:T(8,128)(2,1)}, bf16[8,3,14,512]{3,2,1,0:T(8,128)(2,1)}, u32[]{:S(2)}, u32[]{:S(2)}) collective-permute-start(bf16[8,3,14,512]{3,2,1,0:T(8,128)(2,1)} %copy.791), channel_id=1, source_target_pairs={{0,1},{1,0},{2,3},{3,2},{4,5},{5,4},{6,7},{7,6},{8,9},{9,8},{10,11... | collective-permute-start | bytes 1032200 | tf_op jit(solution)/shard_map/ppermute | solution.py:19
  740.9 11.7 %copy-start.48 = (bf16[8,7,14,512]{3,2,1,0:T(8,128)(2,1)}, bf16[8,7,14,512]{3,2,1,0:T(8,128)(2,1)S(1)}, u32[]{:S(2)}) copy-start(bf16[8,7,14,512]{3,2,1,0:T(8,128)(2,1)S(1)} %copy_dynamic-update-slice_fusion.3) | copy-start | bytes 2408452
  742.4 15.6 %copy-start.50 = (bf16[8,7,14,512]{3,2,1,0:T(8,128)(2,1)}, bf16[8,7,14,512]{3,2,1,0:T(8,128)(2,1)S(1)}, u32[]{:S(2)}) copy-start(bf16[8,7,14,512]{3,2,1,0:T(8,128)(2,1)S(1)} %copy_dynamic-update-slice_fusion.2) | copy-start | bytes 2408452
  743.8 8.8 copy-start.117
  744.0 14.1 %copy-start.119 = (bf16[8,7,3,512]{3,2,1,0:T(4,128)(2,1)}, bf16[8,7,3,512]{3,2,1,0:T(4,128)(2,1)S(1)}, u32[]{:S(2)}) copy-start(bf16[8,7,3,512]{3,2,1,0:T(4,128)(2,1)S(1)} %slice.461) | copy-start | bytes 516100
  773.6 136.3 %all-to-all-start.1 = ((bf16[16,32,4102]{2,1,0:T(8,128)(2,1)}), bf16[16,32,4102]{2,1,0:T(8,128)(2,1)}, u32[]{:S(2)}, u32[]{:S(2)}) async-start(bf16[16,32,4102]{2,1,0:T(8,128)(2,1)} %concatenate.173), calls=%async_computation.1 | async-start | bytes 8650752 | tf_op jit(solution)/shard_map/all_to_all | solution.py:30
  797.7 104.8 %copy-start.47 = (f32[8,7,14,512]{3,2,1,0:T(8,128)S(1)}, f32[8,7,14,512]{3,2,1,0:T(8,128)}, u32[]{:S(2)}) copy-start(f32[8,7,14,512]{3,2,1,0:T(8,128)} %copy-done.46) | copy-start | bytes 4816900
  907.0 9.9 %copy-start.240 = (f32[512]{0:T(512)S(1)}, f32[512]{0:T(512)}, u32[]{:S(2)}) copy-start(f32[512]{0:T(512)} %get-tuple-element.196) | copy-start | bytes 6148
  907.0 9.9 %copy-start.241 = (f32[512]{0:T(512)S(1)}, f32[512]{0:T(512)}, u32[]{:S(2)}) copy-start(f32[512]{0:T(512)} %get-tuple-element.194) | copy-start | bytes 6148
  909.9 14.9 %all-to-all-start = ((bf16[16,1,32]{2,1,0:T(2,128)(2,1)}), bf16[16,1,32]{2,1,0:T(2,128)(2,1)S(1)}, u32[]{:S(2)}, u32[]{:S(2)}) async-start(bf16[16,1,32]{2,1,0:T(2,128)(2,1)} %convert_element_type.860), calls=%async_computation | async-start | bytes 16384 | tf_op jit(solution)/shard_map/all_to_all | solution.py:30
  916.6 33.7 %all-reduce.13.cloned.1.call-start = ((), (), s32[]{:S(2)}) async-start(), calls=%async_computation.7 | async-start | bytes 720896 | tf_op jit(solution)/shard_map/psum | solution.py:461
  920.2 11.5 %copy-start.66 = (f32[8,7,14,512]{3,2,1,0:T(8,128)S(1)}, f32[8,7,14,512]{3,2,1,0:T(8,128)}, u32[]{:S(2)}) copy-start(f32[8,7,14,512]{3,2,1,0:T(8,128)} %get-tuple-element.197) | copy-start | bytes 4816900
  924.7 16.5 %all-to-all-start.3 = ((bf16[16,1,32]{2,1,0:T(2,128)(2,1)}), bf16[16,1,32]{2,1,0:T(2,128)(2,1)S(1)}, u32[]{:S(2)}, u32[]{:S(2)}) async-start(bf16[16,1,32]{2,1,0:T(2,128)(2,1)} %convert_element_type.865), calls=%async_computation.3 | async-start | bytes 16384 | tf_op jit(solution)/shard_map/all_to_all | solution.py:30
  934.8 20.4 %copy-start.1 = (f32[169,16]{0,1:T(8,128)S(1)}, f32[169,16]{0,1:T(8,128)}, u32[]{:S(2)}) copy-start(f32[169,16]{0,1:T(8,128)} %param.32) | copy-start | bytes 32452
  (235 other events, 858.1 us)
Sparse Core Ops, SparseCore 0:
  10.8 61.0 all-gather.4
  74.6 60.4 all-gather.6
  137.9 59.2 all-gather.8
  924.9 19.8 all-reduce.12
where the time goes:
time: 968 us; the launch traced here: 962 us
  local copies, waits for them, and re-layouts  290 us (30%)
  matrix products  266 us (27%)
  blocking collectives  222 us (23%)
  other arithmetic  133 us (14%)
  starting transfers between devices  29.6 us (3%)
  between operations  18.7 us (2%)
    psum x1, blocking collectives, per_device(): table_grad = lax.psum(table_part, ('fsdp', 'win'))  94.7 us
    convert_element_type x8, local copies, waits for them, and re-layouts, forward_pass(): attended = attended.reshape(queries.shape).astype(jnp.bfloat16)  51.2 us
    unnamed x586, local copies, waits for them, and re-layouts  48.9 us
    unnamed x1, blocking collectives  45.1 us
    all_gather x1, blocking collectives, per_device(): lax.all_gather(shards[5], 'fsdp', axis=0, tiled=True)  41.3 us
    another operation x8, local copies, waits for them, and re-layouts, backward_pass(): grad_heads = grad_attended.reshape(head_shape)  39.7 us
    all_gather x1, blocking collectives, per_device(): lax.all_gather(shards[10], 'fsdp', axis=0, tiled=True)  37.9 us
    dot_general x4, matrix products, backward_pass(): jnp.einsum('bije,fe->bijf', micro_grad, fc2_weight, preferred_element_typ...  32.7 us
  transfers between devices with their start and end apart: 24, of which 0 were waited for; matrix products, arithmetic and copies ran while one was open for 59% of the time, Pallas kernels for 0%

commit v1 on v0

v1 whole, which is shorter than its diff:
```python
import functools
import jax
import jax.numpy as jnp
import numpy as np
from jax import lax
from jax.experimental import pallas as pl
from jax.experimental.pallas import tpu as pltpu
from jax.sharding import PartitionSpec as P

HEADS = 16
HD = 32
WIN = 7
SHIFT = 3
TOK = 98
PAD = 112
LANES = 128
GROUPS = 4
NB = 8
EPS = 1e-05
FAR = -1e30
F32 = jnp.float32
BF = jnp.bfloat16
HIGHEST = lax.Precision.HIGHEST


def mm(a, b):
    return lax.dot_general(a, b, (((1,), (0,)), ((), ())), preferred_element_type=F32)


def mm_nt(a, b):
    return lax.dot_general(a, b, (((1,), (1,)), ((), ())), preferred_element_type=F32)


def mm_tn(a, b):
    return lax.dot_general(a, b, (((0,), (0,)), ((), ())), preferred_element_type=F32)


def normalized(x):
    mean = jnp.mean(x, axis=-1, keepdims=True)
    c = x - mean
    var = jnp.mean(c * c, axis=-1, keepdims=True)
    r = lax.rsqrt(var + EPS)
    return c * r, r


def norm_back(u, n, r):
    return r * (u - jnp.mean(u, axis=-1, keepdims=True) - n * jnp.mean(u * n, axis=-1, keepdims=True))


def col_sum(v):
    return jnp.sum(v, axis=0, keepdims=True)


def erf(x):
    x = jnp.clip(x, -3.7439211627767994, 3.7439211627767994)
    s = x * x
    a = (0.00022905065861350646, 0.0034082910107109506, 0.050955695062380861, 0.18520832239976145, 1.128379143519084)
    b = (-1.1791602954361697e-7, 0.000023547966471313185, 0.0010179625278914885, 0.014070470171167667, 0.11098505178285362, 0.49746925110067538, 1.0)
    p = a[0]
    for c in a[1:]:
        p = p * s + c
    q = b[0]
    for c in b[1:]:
        q = q * s + c
    return x * p / q


def head_masks():
    lane = lax.broadcasted_iota(jnp.int32, (1, LANES), 1) // HD
    return [(lane == h).astype(BF) for h in range(GROUPS)]


def attend_kernel(x_ref, g_ref, b_ref, w_ref, qb_ref, rel_ref, qkv_ref, att_ref, prob_ref, wide, joined):
    d = x_ref.shape[-1]
    n, _ = normalized(x_ref[...].astype(F32).reshape(TOK * NB, d))
    normed = (n * g_ref[...] + b_ref[...]).astype(BF)
    lanes3 = 3 * d // LANES
    chunk = 512

    @pl.when(pl.program_id(0) == 0)
    def _():
        wide[:, TOK * NB :, :] = jnp.zeros((lanes3, (PAD - TOK) * NB, LANES), F32)

    for c in range(3 * d // chunk):
        part = mm(normed, w_ref[:, c * chunk : (c + 1) * chunk]) + qb_ref[:, c * chunk : (c + 1) * chunk]
        for k in range(chunk // LANES):
            wide[c * (chunk // LANES) + k, : TOK * NB, :] = part[:, k * LANES : (k + 1) * LANES]
    masks = head_masks()
    per = d // LANES
    scale = HD ** (-0.5)

    def one(i, carry):
        for g in range(per):
            q = wide[g, pl.ds(i, PAD, stride=NB), :].astype(BF)
            k = wide[per + g, pl.ds(i, PAD, stride=NB), :].astype(BF)
            v = wide[2 * per + g, pl.ds(i, PAD, stride=NB), :].astype(BF)
            qkv_ref[i, g] = q
            qkv_ref[i, per + g] = k
            qkv_ref[i, 2 * per + g] = v
            total = None
            for h in range(GROUPS):
                s = mm_nt(q * masks[h], k) * scale + rel_ref[g * GROUPS + h][:, :PAD]
                e = jnp.exp(s - jnp.max(s, axis=-1, keepdims=True))
                p = (e / jnp.sum(e, axis=-1, keepdims=True)).astype(BF)
                prob_ref[i, g * GROUPS + h] = p
                o = mm(p, v * masks[h])
                total = o if total is None else total + o
            joined[g, pl.ds(i, PAD, stride=NB), :] = total
        return carry

    lax.fori_loop(0, NB, one, 0)
    for g in range(per):
        att_ref[:, :, g * LANES : (g + 1) * LANES] = joined[g, : TOK * NB, :].astype(BF).reshape(TOK, NB, LANES)


def attend(x, g, b, w, qb, rel):
    _, imgs, d = x.shape
    full = lambda *shape: pl.BlockSpec(shape, lambda i: (0,) * len(shape), pipeline_mode=pl.Buffered(1))
    per = d // LANES
    return pl.pallas_call(
        attend_kernel,
        grid=(imgs // NB,),
        in_specs=[
            pl.BlockSpec((TOK, NB, d), lambda i: (0, i, 0)),
            full(1, d), full(1, d), full(d, 3 * d), full(1, 3 * d), full(HEADS, PAD, LANES),
        ],
        out_specs=[
            pl.BlockSpec((NB, 3 * per, PAD, LANES), lambda i: (i, 0, 0, 0)),
            pl.BlockSpec((TOK, NB, d), lambda i: (0, i, 0)),
            pl.BlockSpec((NB, HEADS, PAD, PAD), lambda i: (i, 0, 0, 0)),
        ],
        out_shape=[
            jax.ShapeDtypeStruct((imgs, 3 * per, PAD, LANES), BF),
            jax.ShapeDtypeStruct((TOK, imgs, d), BF),
            jax.ShapeDtypeStruct((imgs, HEADS, PAD, PAD), BF),
        ],
        scratch_shapes=[
            pltpu.VMEM((3 * per, PAD * NB, LANES), F32),
            pltpu.VMEM((per, PAD * NB, LANES), F32),
        ],
        compiler_params=pltpu.CompilerParams(vmem_limit_bytes=60 << 20),
        name="attend",
    )(x, g, b, w, qb, rel)


def mlp_kernel(x_ref, att_ref, ct_ref, wp_ref, bp_ref, g_ref, b_ref, w1_ref, b1_ref, w2_ref, b2_ref,
               out_ref, gm_ref, gatt_ref, dwp_ref, dw1_ref, dw2_ref, db1_ref, small_ref,
               awp, aw1, aw2, ab1, asm):
    step = pl.program_id(0)
    d = x_ref.shape[-1]
    ff = w1_ref.shape[-1]
    chunk = 512

    @pl.when(step == 0)
    def _():
        awp[...] = jnp.zeros_like(awp)
        aw1[...] = jnp.zeros_like(aw1)
        aw2[...] = jnp.zeros_like(aw2)
        ab1[...] = jnp.zeros_like(ab1)
        asm[...] = jnp.zeros_like(asm)

    att = att_ref[...]
    gb = ct_ref[...]
    grad_out = gb.astype(F32)
    middle = x_ref[...].astype(F32) + mm(att, wp_ref[...]) + bp_ref[...]
    n, r = normalized(middle)
    normed = (n * g_ref[...] + b_ref[...]).astype(BF)
    normed_t = normed.T
    gb_t = gb.T
    out = middle + b2_ref[...]
    m = None
    for c in range(ff // chunk):
        at = slice(c * chunk, (c + 1) * chunk)
        hidden = mm(normed, w1_ref[:, at]) + b1_ref[:, at]
        cdf = 0.5 * (1.0 + erf(hidden * 0.7071067811865476))
        slope = cdf + hidden * (0.3989422804014327 * jnp.exp(-0.5 * hidden * hidden))
        active = (hidden * cdf).astype(BF)
        out = out + mm(active, w2_ref[at, :])
        gh = mm_nt(gb, w2_ref[at, :]) * slope
        ghb = gh.astype(BF)
        ab1[:, at] += col_sum(ghb.astype(F32))
        aw2[:, at] += mm(gb_t, active)
        aw1[:, at] += mm(normed_t, ghb)
        part = mm_nt(ghb, w1_ref[:, at])
        m = part if m is None else m + part
    out_ref[...] = out.astype(BF)
    grad_middle = grad_out + norm_back(m * g_ref[...], n, r)
    gm_ref[...] = grad_middle
    gp = grad_middle.astype(BF)
    gatt_ref[...] = mm_nt(gp, wp_ref[...]).astype(BF)
    awp[...] += mm_tn(att, gp)
    asm[0:1, :] += col_sum(m * n)
    asm[1:2, :] += col_sum(m)
    asm[2:3, :] += col_sum(gp.astype(F32))
    asm[3:4, :] += col_sum(grad_out)

    @pl.when(step == pl.num_programs(0) - 1)
    def _():
        dwp_ref[...] = awp[...].astype(BF)
        dw1_ref[...] = aw1[...].astype(BF)
        for c in range(ff // chunk):
            at = slice(c * chunk, (c + 1) * chunk)
            dw2_ref[at, :] = aw2[:, at].T.astype(BF)
        db1_ref[...] = ab1[...]
        small_ref[...] = asm[...]


def mlp(x, att, ct, wp, bp, g, b, w1, b1, w2, b2, tile=448):
    rows, d = x.shape
    ff = w1.shape[-1]
    full = lambda *shape: pl.BlockSpec(shape, lambda i: (0,) * len(shape), pipeline_mode=pl.Buffered(1))
    row = pl.BlockSpec((tile, d), lambda i: (i, 0))
    return pl.pallas_call(
        mlp_kernel,
        grid=(rows // tile,),
        in_specs=[row, row, row, full(d, d), full(1, d), full(1, d), full(1, d), full(d, ff), full(1, ff),
                  full(ff, d), full(1, d)],
        out_specs=[row, row, row, full(d, d), full(d, ff), full(ff, d), full(1, ff), full(8, d)],
        out_shape=[
            jax.ShapeDtypeStruct((rows, d), BF),
            jax.ShapeDtypeStruct((rows, d), F32),
            jax.ShapeDtypeStruct((rows, d), BF),
            jax.ShapeDtypeStruct((d, d), BF),
            jax.ShapeDtypeStruct((d, ff), BF),
            jax.ShapeDtypeStruct((ff, d), BF),
            jax.ShapeDtypeStruct((1, ff), F32),
            jax.ShapeDtypeStruct((8, d), F32),
        ],
        scratch_shapes=[
            pltpu.VMEM((d, d), F32), pltpu.VMEM((d, ff), F32), pltpu.VMEM((d, ff), F32),
            pltpu.VMEM((1, ff), F32), pltpu.VMEM((8, d), F32),
        ],
        compiler_params=pltpu.CompilerParams(vmem_limit_bytes=60 << 20),
        name="mlp",
    )(x, att, ct, wp, bp, g, b, w1, b1, w2, b2)


def back_kernel(x_ref, gm_ref, gatt_ref, qkv_ref, prob_ref, g_ref, b_ref, w_ref,
                gin_ref, dw_ref, small_ref, bsum_ref, rel_ref, wide, grads, aw, asm, abs_):
    step = pl.program_id(0)
    d = x_ref.shape[-1]
    per = d // LANES
    scale = HD ** (-0.5)

    @pl.when(step == 0)
    def _():
        aw[...] = jnp.zeros_like(aw)
        asm[...] = jnp.zeros_like(asm)
        abs_[...] = jnp.zeros_like(abs_)
        rel_ref[...] = jnp.zeros_like(rel_ref)
        wide[:, TOK * NB :, :] = jnp.zeros((per, (PAD - TOK) * NB, LANES), F32)

    for g in range(per):
        wide[g, : TOK * NB, :] = gatt_ref[:, :, g * LANES : (g + 1) * LANES].astype(F32).reshape(TOK * NB, LANES)
    masks = head_masks()

    def one(i, carry):
        for g in range(per):
            ga = wide[g, pl.ds(i, PAD, stride=NB), :].astype(BF)
            q = qkv_ref[i, g]
            k = qkv_ref[i, per + g]
            v = qkv_ref[i, 2 * per + g]
            dq = dk = dv = None
            for h in range(GROUPS):
                p = prob_ref[i, g * GROUPS + h]
                pf = p.astype(F32)
                gah = ga * masks[h]
                dp = mm_nt(gah, v)
                inner = jnp.sum(pf * dp, axis=-1, keepdims=True)
                ds = (pf * (dp - inner)).astype(BF)
                rel_ref[g * GROUPS + h] += ds.astype(F32)
                a, b, c = mm(ds, k * masks[h]), mm_tn(ds, q * masks[h]), mm_tn(p, gah)
                dq = a if dq is None else dq + a
                dk = b if dk is None else dk + b
                dv = c if dv is None else dv + c
            grads[g, pl.ds(i, PAD, stride=NB), :] = dq * scale
            grads[per + g, pl.ds(i, PAD, stride=NB), :] = dk * scale
            grads[2 * per + g, pl.ds(i, PAD, stride=NB), :] = dv
        return carry

    lax.fori_loop(0, NB, one, 0)
    n, r = normalized(x_ref[...].astype(F32).reshape(TOK * NB, d))
    normed = (n * g_ref[...] + b_ref[...]).astype(BF)
    normed_t = normed.T
    dn = None
    for c in range(3):
        at = slice(c * d, (c + 1) * d)
        dqkv = jnp.concatenate([grads[c * per + g, : TOK * NB, :].astype(BF) for g in range(per)], axis=-1)
        abs_[:, at] += col_sum(dqkv.astype(F32))
        aw[:, at] += mm(normed_t, dqkv)
        part = mm_nt(dqkv, w_ref[:, at])
        dn = part if dn is None else dn + part
    dn = dn.astype(BF).astype(F32)
    asm[0:1, :] += col_sum(dn * n)
    asm[1:2, :] += col_sum(dn)
    gin = gm_ref[...].reshape(TOK * NB, d) + norm_back(dn * g_ref[...], n, r)
    gin_ref[...] = gin.reshape(TOK, NB, d)

    @pl.when(step == pl.num_programs(0) - 1)
    def _():
        dw_ref[...] = aw[...].astype(BF)
        small_ref[...] = asm[...]
        bsum_ref[...] = abs_[...]


def back(x, gm, gatt, qkv, prob, g, b, w):
    _, imgs, d = x.shape
    per = d // LANES
    full = lambda *shape: pl.BlockSpec(shape, lambda i: (0,) * len(shape), pipeline_mode=pl.Buffered(1))
    tok = pl.BlockSpec((TOK, NB, d), lambda i: (0, i, 0))
    return pl.pallas_call(
        back_kernel,
        grid=(imgs // NB,),
        in_specs=[
            tok, tok, tok,
            pl.BlockSpec((NB, 3 * per, PAD, LANES), lambda i: (i, 0, 0, 0)),
            pl.BlockSpec((NB, HEADS, PAD, PAD), lambda i: (i, 0, 0, 0)),
            full(1, d), full(1, d), full(d, 3 * d),
        ],
        out_specs=[tok, full(d, 3 * d), full(8, d), full(1, 3 * d), full(HEADS, PAD, PAD)],
        out_shape=[
            jax.ShapeDtypeStruct((TOK, imgs, d), F32),
            jax.ShapeDtypeStruct((d, 3 * d), BF),
            jax.ShapeDtypeStruct((8, d), F32),
            jax.ShapeDtypeStruct((1, 3 * d), F32),
            jax.ShapeDtypeStruct((HEADS, PAD, PAD), F32),
        ],
        scratch_shapes=[
            pltpu.VMEM((per, PAD * NB, LANES), F32),
            pltpu.VMEM((3 * per, PAD * NB, LANES), F32),
            pltpu.VMEM((d, 3 * d), F32),
            pltpu.VMEM((8, d), F32),
            pltpu.VMEM((1, 3 * d), F32),
        ],
        compiler_params=pltpu.CompilerParams(vmem_limit_bytes=60 << 20),
        name="back",
    )(x, gm, gatt, qkv, prob, g, b, w)


def swap_rows(array, rows):
    incoming = lax.ppermute(array[:rows], "win", [(0, 1), (1, 0)])
    return jnp.concatenate([incoming, array[rows:]], axis=0)


def window_of_tokens():
    row, col = np.arange(TOK) // (2 * WIN), np.arange(TOK) % (2 * WIN)
    row, col = (row - SHIFT) % WIN, (col - SHIFT) % (2 * WIN)
    return col // WIN, row * WIN + col % WIN


def spread_matrix():
    _, place = window_of_tokens()
    return (place[:, None] == np.arange(WIN * WIN)[None, :]).astype(np.float32)


def relative_parts(rel_index, table):
    count = WIN * WIN
    onehot = (rel_index.reshape(count * count, 1) == jnp.arange(table.shape[0], dtype=jnp.int32)[None, :]).astype(F32)
    relative = jnp.dot(onehot, table, precision=HIGHEST).reshape(count, count, -1).transpose(2, 0, 1)
    return onehot, relative


def bias_of_pairs(relative, regions):
    side, place = window_of_tokens()
    spread = jnp.asarray(spread_matrix())
    wide = jnp.einsum("at,hts,bs->hab", spread, relative, spread, precision=HIGHEST)
    region = regions.reshape(2, WIN * WIN)
    region = jnp.concatenate(
        [jnp.roll(region[s].reshape(WIN, WIN), SHIFT, axis=0)[:, c] for s, c in ((1, slice(4, 7)), (0, slice(0, 7)), (1, slice(0, 4)))],
        axis=1,
    ).reshape(TOK)
    mask = jnp.where(region[:, None] == region[None, :], 0.0, -100.0)
    same = jnp.asarray(side[:, None] == side[None, :])
    bias = jnp.where(same[None], wide + mask[None], FAR)
    return jnp.pad(
        jnp.pad(bias, ((0, 0), (0, 0), (0, LANES - TOK)), constant_values=FAR),
        ((0, 0), (0, PAD - TOK), (0, 0)),
    )


def owner_blocks(array, count):
    return array.reshape(count, array.shape[0] // count, *array.shape[1:])


def delivered(blocks):
    mine = lax.all_to_all(blocks, "fsdp", 0, 0, tiled=True)
    mine = jnp.sum(mine.astype(F32), axis=0).astype(BF)
    other = lax.ppermute(mine, "win", [(0, 1), (1, 0)])
    return mine.astype(F32) + other.astype(F32)


def per_device(
    images, norm1_gain, norm1_bias, qkv_weight, q_bias, v_bias, proj_weight, proj_bias, norm2_gain, norm2_bias,
    fc1_weight, fc1_bias, fc2_weight, fc2_bias, bias_table, regions, rel_index, cotangent,
):
    imgs, rows, cols, d = images.shape
    top = SHIFT * cols
    owners = lax.axis_size("fsdp")
    x = swap_rows(images.transpose(1, 2, 0, 3).reshape(rows * cols, imgs, d), top)
    ct = swap_rows(cotangent.transpose(1, 2, 0, 3).reshape(rows * cols, imgs, d), top)
    vectors = (norm1_gain, norm1_bias, q_bias, v_bias, proj_bias, norm2_gain, norm2_bias, fc2_bias, fc1_bias)
    packed = lax.all_gather(jnp.concatenate(vectors), "fsdp", axis=0).astype(F32)
    at, whole = 0, []
    for v in vectors:
        whole.append(packed[:, at : at + v.shape[0]].reshape(1, -1))
        at += v.shape[0]
    g1, b1, qb, vb, bp, g2, b2, b_out, b_in = whole
    gather = functools.partial(lax.all_gather, axis_name="fsdp", axis=0, tiled=True)
    w_qkv, w_proj, w_in, w_out = gather(qkv_weight), gather(proj_weight), gather(fc1_weight), gather(fc2_weight)
    onehot, relative = relative_parts(rel_index, bias_table)
    rel = bias_of_pairs(relative, regions)
    qkv_bias = jnp.concatenate([qb, jnp.zeros_like(qb), vb], axis=1)

    qkv, att, prob = attend(x, g1, b1, w_qkv, qkv_bias, rel)
    flat = lambda v: v.reshape(rows * cols * imgs, d)
    out, gm, gatt, dwp, dw1, dw2, db_in, small2 = mlp(
        flat(x), flat(att), flat(ct), w_proj, bp, g2, b2, w_in, b_in, w_out, b_out
    )
    tall = lambda v: v.reshape(rows * cols, imgs, d)
    gin, dwq, small1, bsum, rel_sum = back(x, tall(gm), tall(gatt), qkv, prob, g1, b1, w_qkv)

    dw1, dw2, dwp, dwq = (delivered(owner_blocks(v, owners)) for v in (dw1, dw2, dwp, dwq))
    grads = (
        small1[0], small1[1], bsum[0, :d], bsum[0, 2 * d :], small2[2], small2[0], small2[1], small2[3], db_in[0],
    )
    sums = delivered(jnp.concatenate([v.reshape(owners, -1) for v in grads], axis=1).astype(BF))
    at, own = 0, []
    for v in vectors:
        own.append(sums[at : at + v.shape[0]].reshape(-1) if sums.ndim == 1 else sums[0, at : at + v.shape[0]])
        at += v.shape[0]
    dg1, db1, dqb, dvb, dbp, dg2, db2, db_out, db_in = own
    spread = jnp.asarray(spread_matrix())
    pairs = jnp.einsum("at,hab,bs->tsh", spread, rel_sum[:, :TOK, :TOK], spread, precision=HIGHEST)
    table = jnp.dot(onehot.T, pairs.reshape(WIN**4, -1), precision=HIGHEST)
    table = lax.psum(table, ("fsdp", "win"))
    back_to_images = lambda v: swap_rows(v, top).reshape(rows, cols, imgs, d).transpose(2, 0, 1, 3)
    return (
        back_to_images(tall(out)), back_to_images(gin), dg1, db1, dwq, dqb, dvb, dwp, dbp, dg2, db2, dw1, db_in, dw2,
        db_out, table,
    )


def solution(mesh):
    vec, mat, img = P("fsdp"), P("fsdp", None), P("fsdp", "win", None, None)
    in_specs = (
        img, vec, vec, mat, vec, vec, mat, vec, vec, vec, mat, vec, mat, vec, P(), P("win", None, None), P(), img,
    )
    out_specs = (img, img, vec, vec, mat, vec, vec, mat, vec, vec, vec, mat, vec, mat, vec, P())
    return jax.shard_map(per_device, mesh=mesh, in_specs=in_specs, out_specs=out_specs, check_vma=False)
```

time: 968 us -> 659 us (0.68)
  Pallas kernels: 0 us -> 288 us
  local copies, waits for them, and re-layouts: 290 us -> 29.3 us
  matrix products: 266 us -> 5.76 us
  other arithmetic: 133 us -> 28.6 us
  blocking collectives: 222 us -> 261 us
  starting transfers between devices: 29.6 us -> 6.33 us
  waiting for transfers between devices: 1.49 us -> 23.8 us
    pallas_call x0 -> x3, Pallas kernels: none -> 288 us  [the longest x1 152 us: back(): pl.pallas_call(back_kernel, grid=(imgs // NB,), in_specs=[tok, tok, tok,...]
    dot_general x74 -> x6, matrix products: 266 us -> 5.76 us  [the longest x2 2.41 us: bias_of_pairs(): jnp.einsum('at,hts,bs->hab', spread, relative, spread, precision=HIGHEST)]
    all_to_all x0 -> x4, blocking collectives: none -> 118 us  [delivered(): mine = lax.all_to_all(blocks, 'fsdp', 0, 0, tiled=True)]
    reshape x26 -> x10, local copies, waits for them, and re-layouts: 66.7 us -> 4.42 us  [the longest x8 4.05 us: per_device(): whole.append(packed[:, at:at + v.shape[0]].reshape(1, -1))]
    reduce_sum x34 -> x5, other arithmetic: 64.2 us -> 4.04 us  [delivered(): mine = jnp.sum(mine.astype(F32), axis=0).astype(BF)]
    convert_element_type x22 -> x0, local copies, waits for them, and re-layouts: 59.8 us -> none  [the longest x8 51.2 us: forward_pass(): attended = attended.reshape(queries.shape).astype(jnp.bfloat16)]
    unnamed x586 -> x54, local copies, waits for them, and re-layouts: 48.9 us -> 1.43 us
    unnamed x1 -> x0, blocking collectives: 45.1 us -> none
  transfers between devices with their start and end apart: 24 -> 13, of which waited for: 0 -> 3; matrix products, arithmetic and copies ran while one was open for 59% -> 9% of each run, Pallas kernels for 0% -> 8%
where the time goes in v1:
time: 659 us; the launch traced here: 658 us
  Pallas kernels  288 us (44%)
  blocking collectives  261 us (40%)
  local copies, waits for them, and re-layouts  29.3 us (4%)
  other arithmetic  28.6 us (4%)
  waiting for transfers between devices  23.8 us (4%)
  between operations  14.1 us (2%)
    pallas_call x1, Pallas kernels, back(): pl.pallas_call(back_kernel, grid=(imgs // NB,), in_specs=[tok, tok, tok,...  152 us
    all_to_all x4, blocking collectives, delivered(): mine = lax.all_to_all(blocks, 'fsdp', 0, 0, tiled=True)  118 us
    pallas_call x1, Pallas kernels, mlp(): pl.pallas_call(mlp_kernel, grid=(rows // tile,), in_specs=[row, row, row,...  80.9 us
    psum x1, blocking collectives, per_device(): table = lax.psum(table, ('fsdp', 'win'))  58.3 us
    pallas_call x1, Pallas kernels, attend(): pl.pallas_call(attend_kernel, grid=(imgs // NB,), in_specs=[pl.BlockSpec(...  55.1 us
    all_gather x1, blocking collectives, per_device(): lax.all_gather(jnp.concatenate(vectors), 'fsdp', axis=0).astype(F32)  42.8 us
    all_gather x1, blocking collectives, per_device(): gather(proj_weight)  41.8 us
    all_gather x1, waiting for transfers between devices, per_device(): gather(fc1_weight)  21.4 us
  transfers between devices with their start and end apart: 13, of which 3 were waited for; matrix products, arithmetic and copies ran while one was open for 9% of the time, Pallas kernels for 8%

profile of v1, /device:TPU:0, one launch (start us, length us, event | category | flops | bytes accessed | tf_op | source)
XLA Modules:
  0.0 657.7 jit_solution(17953072648698253078)
XLA Ops:
  7.2 0.7 all-gather.6.cloned.1.call-update
  8.0 0.7 all-gather.10.cloned.1.call-update
  8.7 0.7 all-gather.8.cloned.1.call-update
  9.5 2.7 slice.225
  12.3 0.5 collective-permute-start
  12.8 2.6 slice.231
  15.5 42.8 %all-gather.1 = bf16[16,1,384]{2,1,0:T(2,128)(2,1)S(1)} all-gather(bf16[1,1,384]{2,1,0:T(2,128)(2,1)S(1)} %reshape.317), channel_id=2, replica_groups=mesh['fsdp'=16,'win'=2] {'fsdp'}, dimensions={0}, use_global_device_ids=true | all-gather | bytes 13056 | tf_op jit(solution)/shard_map/all_gather | solution.py:402
  59.1 1.3 fusion.1
  60.6 1.4 slice.226
  62.0 1.1 copy-done.4
  63.1 0.2 slice.232
  63.3 0.6 slice.236
  64.1 0.2 reshape.298
  64.3 0.7 reshape.294.g_ref
  64.9 0.7 reshape.295.b_ref
  65.6 0.7 reshape.301.bp_ref
  66.2 0.6 reshape.302.g_ref
  66.9 0.7 reshape.303.b_ref
  67.5 0.7 reshape.305.b2_ref
  68.2 0.9 fusion.7
  69.1 1.5 fusion.2
  70.6 1.0 pad_select_fusion.rel_ref
  71.7 0.6 fusion.9.qb_ref
  72.3 41.8 %all_gather.21.wp_ref = bf16[512,512]{1,0:T(8,128)(2,1)} all-gather(bf16[32,512]{1,0:T(8,128)(2,1)S(1)} %copy-done.10), channel_id=1, replica_groups=mesh['fsdp'=16,'win'=2] {'fsdp'}, dimensions={0}, use_global_device_ids=true | all-gather | bytes 557056 | tf_op jit(solution)/shard_map/all_gather | solution.py:409
  114.1 3.3 pad_maximum_fusion.1.x_ref
  117.4 3.5 pad_maximum_fusion.2
  120.9 55.1 %attend.1 = (bf16[32,12,112,128]{3,2,1,0:T(8,128)(2,1)}, bf16[98,32,512]{2,1,0:T(8,128)(2,1)}, bf16[32,16,112,112]{3,2,1,0:T(8,128)(2,1)}) custom-call(bf16[98,32,512]{2,1,0:T(8,128)(2,1)} %pad_maximum_fusion.1.x_ref, f32[1,512]{1,0:T(1,128)} %reshape.294.g_ref, f32[1,512]{1,0:T(1,128)} %reshape.295.b_ref, ...), custom_call_target="tpu_custom_call" | custom-call | tf_op jit(solution)/shard_map/attend/pallas_call | solution.py:120
  176.0 21.4 %all-gather.8.cloned.1.call-done.w1_ref = bf16[512,2048]{1,0:T(8,128)(2,1)} async-done(((bf16[32,2048]{1,0:T(8,128)(2,1)}), bf16[512,2048]{1,0:T(8,128)(2,1)}) %all-gather.8.cloned.1.call-update) | async-done | bytes 2097168 | tf_op jit(solution)/shard_map/all_gather | solution.py:409
  197.3 80.9 %mlp.1 = (bf16[3136,512]{1,0:T(8,128)(2,1)}, f32[3136,512]{1,0:T(8,128)}, bf16[3136,512]{1,0:T(8,128)(2,1)}, bf16[512,512]{1,0:T(8,128)(2,1)}, bf16[512,2048]{1,...) custom-call(bf16[3136,512]{1,0:T(8,128)(2,1)} %bitcast.48, ...), custom_call_target="tpu_custom_call" | custom-call | tf_op jit(solution)/shard_map/mlp/pallas_call | solution.py:213
  278.3 152.5 %back.1 = (f32[98,32,512]{2,1,0:T(8,128)}, bf16[512,1536]{1,0:T(8,128)(2,1)}, f32[8,512]{1,0:T(8,128)}, f32[1,1536]{1,0:T(1,128)}, f32[16,112,112]{2,1,0:T(8,128)}) custom-call(bf16[98,32,512]{2,1,0:T(8,128)(2,1)} %pad_maximum_fusion.1.x_ref, f32[98,32,512]{2,1,0:T(8,128)} %bitcast.54, bf16[98,32,512]{2,1,0:T(8,128)(2,1)} %bitcast.61, ...), custom_call_target="tpu_custom_call" | custom-call | tf_op jit(solution)/shard_map/back/pallas_call | solution.py:311
  430.7 0.9 convert.39
  431.8 0.7 convert.40
  433.1 0.2 concatenate.76
  433.4 0.5 broadcast.55
  433.9 0.7 reduce.38
  434.7 11.5 %all_to_all.26 = bf16[16,2,192]{2,1,0:T(2,128)(2,1)S(1)} all-to-all(bf16[16,2,192]{2,1,0:T(2,128)(2,1)S(1)} %reshape.356), channel_id=1, replica_groups=mesh['fsdp'=16,'win'=2] {'fsdp'}, dimensions={0} | all-to-all | bytes 24576 | tf_op jit(solution)/shard_map/all_to_all | solution.py:386
  446.2 15.6 %all_to_all.27 = bf16[16,32,512]{2,1,0:T(8,128)(2,1)S(1)} all-to-all(bf16[16,32,512]{2,1,0:T(8,128)(2,1)S(1)} %bitcast.65), channel_id=1, replica_groups=mesh['fsdp'=16,'win'=2] {'fsdp'}, dimensions={0} | all-to-all | bytes 1048576 | tf_op jit(solution)/shard_map/all_to_all | solution.py:386
  461.8 40.1 %all_to_all.28 = bf16[16,32,1536]{2,1,0:T(8,128)(2,1)} all-to-all(bf16[16,32,1536]{2,1,0:T(8,128)(2,1)} %bitcast.64), channel_id=1, replica_groups=mesh['fsdp'=16,'win'=2] {'fsdp'}, dimensions={0} | all-to-all | bytes 3145728 | tf_op jit(solution)/shard_map/all_to_all | solution.py:386
  501.9 51.2 %all_to_all.29 = bf16[16,128,512]{2,1,0:T(8,128)(2,1)} all-to-all(bf16[16,128,512]{2,1,0:T(8,128)(2,1)S(1)} %bitcast.63), channel_id=1, replica_groups=mesh['fsdp'=16,'win'=2] {'fsdp'}, dimensions={0} | all-to-all | bytes 4194304 | tf_op jit(solution)/shard_map/all_to_all | solution.py:386
  553.2 3.9 all-to-all-start.3
  557.1 3.8 slice.205
  560.9 2.6 slice.201
  563.4 0.4 collective-permute-start.2
  563.9 0.7 fusion.5
  564.5 0.5 convolution_bitcast_fusion
  565.1 0.2 reshape.314
  565.2 0.9 fusion
  566.4 58.3 %psum.7 = f32[169,16]{0,1:T(8,128)} all-reduce(f32[169,16]{0,1:T(8,128)S(1)} %fusion), channel_id=1, replica_groups=mesh['fsdp'=16,'win'=2] {'fsdp','win'}, use_global_device_ids=true, to_apply=%region_5.6 | all-reduce | flops 2704 | bytes 21632 | tf_op jit(solution)/shard_map/psum | solution.py:435
  624.7 4.7 slice.206
  629.4 1.4 slice.203
  630.9 0.6 fusion.11
  631.5 0.5 slice.222
  632.1 0.6 convert_add_fusion.3
  632.8 3.9 pad_maximum_fusion.3
  636.6 1.6 reduce_sum.61
  638.3 0.5 collective-permute-start.5
  638.8 7.0 %pad_maximum_fusion = f32[98,32,512]{2,1,0:T(8,128)} fusion(f32[56,32,512]{2,1,0:T(8,128)} %slice.206, f32[42,32,512]{2,1,0:T(8,128)} %collective-permute-done.3), kind=kLoop, calls=%fused_computation | loop fusion | flops 1605632 | bytes 12845056 | tf_op jit(solution)/shard_map/concatenate | solution.py:342
  645.8 1.9 reduce_sum.64
  647.8 0.7 convert_add_fusion.2
  648.5 0.4 reduce_sum.63
  648.9 0.5 collective-permute-start.7
  649.4 0.7 convert_add_fusion
  650.2 0.2 collective-permute-done.7
  650.4 0.7 convert_add_fusion.1
  (106 shorter events, 3.1 us)
Async XLA Ops:
  7.2 51.9 %copy-start = (f32[169,16]{0,1:T(8,128)S(1)}, f32[169,16]{0,1:T(8,128)}, u32[]{:S(2)}) copy-start(f32[169,16]{0,1:T(8,128)} %param.35) | copy-start | bytes 32452
  7.2 113.7 %all-gather.6.cloned.1.call-start = ((), (), s32[]{:S(2)}) async-start(), calls=%async_computation.5 | async-start | bytes 1671168 | tf_op jit(solution)/shard_map/all_gather | solution.py:409
  7.9 168.0 %all-gather.10.cloned.1.call-start = ((), (), s32[]{:S(2)}) async-start(), calls=%async_computation.7 | async-start | bytes 2228224 | tf_op jit(solution)/shard_map/all_gather | solution.py:409
  8.7 188.6 %all-gather.8.cloned.1.call-start = ((), (), s32[]{:S(2)}) async-start(), calls=%async_computation.6 | async-start | bytes 2228224 | tf_op jit(solution)/shard_map/all_gather | solution.py:409
  9.4 6.0 copy-start.16
  9.4 5.9 copy-start.17
  9.4 5.9 copy-start.18
  9.4 5.9 copy-start.19
  9.5 5.9 copy-start.20
  9.5 5.9 copy-start.21
  9.5 5.9 copy-start.22
  9.5 5.9 copy-start.23
  9.5 5.9 copy-start.24
  9.5 48.8 %copy-start.15 = (s32[1,2,49]{2,1,0:T(2,128)S(1)}, s32[1,2,49]{2,1,0:T(2,128)}, u32[]{:S(2)}) copy-start(s32[1,2,49]{2,1,0:T(2,128)} %param.36) | copy-start | bytes 1180
  9.5 49.3 %copy-start.11 = (s32[49,49]{1,0:T(8,128)S(1)}, s32[49,49]{1,0:T(8,128)}, u32[]{:S(2)}) copy-start(s32[49,49]{1,0:T(8,128)} %param.37) | copy-start | bytes 28816
  9.5 51.1 %copy-start.3 = (bf16[32,7,14,512]{3,0,2,1:T(8,128)(2,1)S(1)}, bf16[32,7,14,512]{3,0,2,1:T(8,128)(2,1)}, u32[]{:S(2)}) copy-start(bf16[32,7,14,512]{3,0,2,1:T(8,128)(2,1)} %param.21) | copy-start | bytes 9633796
  12.3 101.8 %collective-permute-start = (bf16[42,32,512]{2,1,0:T(8,128)(2,1)}, bf16[42,32,512]{2,1,0:T(8,128)(2,1)}, u32[]{:S(2)}, u32[]{:S(2)}) collective-permute-start(bf16[42,32,512]{2,1,0:T(8,128)(2,1)} %bitcast.1), channel_id=1, source_target_pairs={{0,1},{1,0},{2,3},{3,2},{4,5},{5,4},{6,7},{7,6},{8,9},{9,8},{10,11... | collective-permute-start | bytes 4128776 | tf_op jit(solution)/shard_map/ppermute | solution.py:341
  15.4 102.0 %collective-permute-start.1 = (bf16[42,32,512]{2,1,0:T(8,128)(2,1)}, bf16[42,32,512]{2,1,0:T(8,128)(2,1)}, u32[]{:S(2)}, u32[]{:S(2)}) collective-permute-start(bf16[42,32,512]{2,1,0:T(8,128)(2,1)} %bitcast.8), channel_id=1, source_target_pairs={{0,1},{1,0},{2,3},{3,2},{4,5},{5,4},{6,7},{7,6},{8,9},{9,8},{10,11... | collective-permute-start | bytes 4128776 | tf_op jit(solution)/shard_map/ppermute | solution.py:341
  60.5 2.6 copy-start.4
  63.1 5.1 copy-start.9
  63.1 6.0 copy-start.13
  63.3 9.0 %copy-start.10 = (bf16[32,512]{1,0:T(8,128)(2,1)S(1)}, bf16[32,512]{1,0:T(8,128)(2,1)}, u32[]{:S(2)}) copy-start(bf16[32,512]{1,0:T(8,128)(2,1)} %param.27) | copy-start | bytes 98308
  68.2 45.9 %copy-start.2 = (bf16[4,14,32,512]{3,2,1,0:T(8,128)(2,1)S(1)}, bf16[4,14,32,512]{3,2,1,0:T(8,128)(2,1)}, u32[]{:S(2)}) copy-start(bf16[4,14,32,512]{3,2,1,0:T(8,128)(2,1)} %slice.226) | copy-start | bytes 5505028
  278.2 154.5 %copy-start.12 = (f32[8,512]{1,0:T(8,128)S(1)}, f32[8,512]{1,0:T(8,128)}, u32[]{:S(2)}) copy-start(f32[8,512]{1,0:T(8,128)} %get-tuple-element.41) | copy-start | bytes 49156
  278.3 154.8 %copy-start.14 = (f32[1,2048]{1,0:T(1,128)S(1)}, f32[1,2048]{1,0:T(1,128)}, u32[]{:S(2)}) copy-start(f32[1,2048]{1,0:T(1,128)} %get-tuple-element.42) | copy-start | bytes 24580
  278.3 168.0 %copy-start.8 = (bf16[512,512]{1,0:T(8,128)(2,1)S(1)}, bf16[512,512]{1,0:T(8,128)(2,1)}, u32[]{:S(2)}) copy-start(bf16[512,512]{1,0:T(8,128)(2,1)} %get-tuple-element.44) | copy-start | bytes 1572868
  430.7 71.2 %copy-start.6 = (bf16[2048,512]{1,0:T(8,128)(2,1)S(1)}, bf16[2048,512]{1,0:T(8,128)(2,1)}, u32[]{:S(2)}) copy-start(bf16[2048,512]{1,0:T(8,128)(2,1)} %get-tuple-element.46) | copy-start | bytes 6291460
  553.2 95.4 %all-to-all-start.3 = ((bf16[16,32,2048]{2,1,0:T(8,128)(2,1)}), bf16[16,32,2048]{2,1,0:T(8,128)(2,1)S(1)}, u32[]{:S(2)}, u32[]{:S(2)}) async-start(bf16[16,32,2048]{2,1,0:T(8,128)(2,1)} %bitcast.62), calls=%async_computation.3 | async-start | bytes 4194304 | tf_op jit(solution)/shard_map/all_to_all | solution.py:386
  560.8 3.0 copy-start.7
  560.9 77.9 %collective-permute-start.3 = (f32[42,32,512]{2,1,0:T(8,128)}, f32[42,32,512]{2,1,0:T(8,128)}, u32[]{:S(2)}, u32[]{:S(2)}) collective-permute-start(f32[42,32,512]{2,1,0:T(8,128)} %slice.205), channel_id=1, source_target_pairs={{0,1},{1,0},{2,3},{3,2},{4,5},{5,4},{6,7},{7,6},{8,9},{9,8},{10,11... | collective-permute-start | bytes 8257544 | tf_op jit(solution)/shard_map/ppermute | solution.py:341
  563.4 69.3 %collective-permute-start.2 = (bf16[42,32,512]{2,1,0:T(8,128)(2,1)}, bf16[42,32,512]{2,1,0:T(8,128)(2,1)}, u32[]{:S(2)}, u32[]{:S(2)}) collective-permute-start(bf16[42,32,512]{2,1,0:T(8,128)(2,1)} %bitcast.12), channel_id=1, source_target_pairs={{0,1},{1,0},{2,3},{3,2},{4,5},{5,4},{6,7},{7,6},{8,9},{9,8},{10,11... | collective-permute-start | bytes 4128776 | tf_op jit(solution)/shard_map/ppermute | solution.py:341
  566.3 64.5 %collective-permute-start.4 = (bf16[384]{0:T(512)(128)(2,1)S(1)}, bf16[384]{0:T(512)(128)(2,1)S(1)}, u32[]{:S(2)}, u32[]{:S(2)}) collective-permute-start(bf16[384]{0:T(512)(128)(2,1)S(1)} %reduce_sum.60), channel_id=1, source_target_pairs={{0,1},{1,0},{2,3},{3,2},{4,5},{5,4},{6,7},{7,6},{8,9},{9,8},{10,11... | collective-permute-start | bytes 2312 | tf_op jit(solution)/shard_map/ppermute | solution.py:388
  624.7 4.7 copy-start.5
  630.9 1.3 collective-permute-start.6
  638.3 9.6 %collective-permute-start.5 = (bf16[32,1536]{1,0:T(8,128)(2,1)S(1)}, bf16[32,1536]{1,0:T(8,128)(2,1)S(1)}, u32[]{:S(2)}, u32[]{:S(2)}) collective-permute-start(bf16[32,1536]{1,0:T(8,128)(2,1)S(1)} %reduce_sum.61), channel_id=1, source_target_pairs={{0,1},{1,0},{2,3},{3,2},{4,5},{5,4},{6,7},{7,6},{8,9},{9,8},{10,11... | collective-permute-start | bytes 294920 | tf_op jit(solution)/shard_map/ppermute | solution.py:388
  638.8 12.4 %copy-start.1 = (f32[169,16]{0,1:T(8,128)S(1)}, f32[169,16]{0,1:T(8,128)}, u32[]{:S(2)}) copy-start(f32[169,16]{0,1:T(8,128)} %param.35) | copy-start | bytes 32452
  647.7 1.7 collective-permute-start.8
  648.9 1.5 collective-permute-start.7
Sparse Core Ops, SparseCore 0:
  10.8 61.1 all-gather.5
  74.7 60.4 all-gather.9
  138.0 59.2 all-gather.7

commit v2 on v1

--- a/solution.py
+++ b/solution.py
@@ -337,6 +337,273 @@
     )(x, gm, gatt, qkv, prob, g, b, w)
 
 
+DEEP = 4
+
+
+class Place:
+    def __init__(self, inner):
+        self.inner = inner
+        me, core = lax.axis_index("fsdp"), lax.axis_index("win")
+        self.core, self.mate = core, 1 - core
+        self.z = me // (inner * inner)
+        u, v = (me // inner) % inner, me % inner
+        self.a = u * (1 - core) + v * core
+        self.b = v * (1 - core) + u * core
+        self.step_a = inner * (1 - core) + core
+        self.step_b = inner * core + 1 - core
+
+    def at(self, dz=0, da=0, db=0):
+        z = (self.z + dz) % DEEP
+        a = (self.a + da) % self.inner
+        b = (self.b + db) % self.inner
+        return z * self.inner * self.inner + a * self.step_a + b * self.step_b
+
+    def device(self, dz=0, da=0, db=0):
+        return (self.at(dz, da, db), self.core)
+
+    def partner(self):
+        return (self.at(), self.mate)
+
+    def peers(self):
+        near = [self.device(dz=d) for d in range(1, DEEP)]
+        near += [self.device(da=d) for d in range(1, self.inner)]
+        near += [self.device(db=d) for d in range(1, self.inner)]
+        return near + [self.partner()]
+
+
+def meet(place):
+    barrier = pltpu.get_barrier_semaphore()
+    peers = place.peers()
+    for peer in peers:
+        pl.semaphore_signal(barrier, inc=1, device_id=peer, device_id_type=pl.DeviceIdType.MESH)
+    pl.semaphore_wait(barrier, len(peers))
+
+
+def remote(src, dst, send_sem, recv_sem, device):
+    return pltpu.make_async_remote_copy(
+        src_ref=src, dst_ref=dst, send_sem=send_sem, recv_sem=recv_sem, device_id=device,
+        device_id_type=pl.DeviceIdType.MESH,
+    )
+
+
+def gather_kernel(inner, kinds, *refs):
+    ins, outs = refs[:kinds], refs[kinds : 2 * kinds]
+    send_sem, recv_sem, own_sem = refs[2 * kinds :]
+    place = Place(inner)
+    meet(place)
+
+    def piece(k, block, core):
+        half = outs[k].shape[-1] // 2
+        return outs[k].at[block, :, pl.ds(pl.multiple_of(core * half, LANES), half)]
+
+    def mine(k):
+        half = outs[k].shape[-1] // 2
+        return ins[k].at[:, pl.ds(pl.multiple_of(place.core * half, LANES), half)]
+
+    sent = [[] for _ in range(kinds)]
+
+    def send(k, src, block, device):
+        copy = remote(src, piece(k, block, place.core), send_sem.at[k, len(sent[k])],
+                      recv_sem.at[k, place.core, block], device)
+        copy.start()
+        sent[k].append(copy)
+
+    def arrive(k, core, block):
+        at = piece(k, block, core)
+        remote(at, at, send_sem.at[k, 0], recv_sem.at[k, core, block], place.partner()).wait_recv()
+
+    steps = range(1, inner)
+    order_z = (1, 3, 2)
+    own = []
+    for k in range(kinds):
+        for d in order_z:
+            send(k, mine(k), place.at(), place.device(dz=d))
+        for d in steps:
+            send(k, mine(k), place.at(), place.device(da=d))
+        for d in steps:
+            send(k, mine(k), place.at(), place.device(db=d))
+    for k in range(kinds):
+        copy = pltpu.make_async_copy(ins[k], outs[k].at[place.at()], own_sem.at[k])
+        copy.start()
+        own.append(copy)
+
+    def pass_on(k, block, along_a, along_b):
+        arrive(k, place.core, block)
+        src = piece(k, block, place.core)
+        if along_a:
+            for d in steps:
+                send(k, src, block, place.device(da=d))
+        if along_b:
+            for d in steps:
+                send(k, src, block, place.device(db=d))
+        send(k, src, block, place.partner())
+
+    for k in range(kinds):
+        for dz in order_z:
+            pass_on(k, place.at(dz=dz), True, True)
+        for da in steps:
+            for dz in (0,) + order_z:
+                pass_on(k, place.at(dz=dz, da=da), False, True)
+    for k in range(kinds):
+        for db in steps:
+            for da in range(inner):
+                for dz in (0,) + order_z:
+                    pass_on(k, place.at(dz=dz, da=da, db=db), False, False)
+    for k in range(kinds):
+        for db in range(inner):
+            for da in range(inner):
+                for dz in range(DEEP):
+                    if db or da or dz:
+                        arrive(k, place.mate, place.at(dz, da, db))
+        own[k].wait()
+        for copy in sent[k]:
+            copy.wait_send()
+
+
+def inner_of(owners):
+    return int(round((owners // DEEP) ** 0.5))
+
+
+def gathered(shards):
+    owners = lax.axis_size("fsdp")
+    inner, kinds = inner_of(owners), len(shards)
+    sends = (DEEP - 1) + 2 * (inner - 1) + 1 + (DEEP - 1) * (2 * inner - 1) + DEEP * (inner - 1) * inner + DEEP * inner * (inner - 1)
+    anywhere = pl.BlockSpec(memory_space=pl.ANY)
+    return pl.pallas_call(
+        functools.partial(gather_kernel, inner, kinds),
+        in_specs=[anywhere] * kinds,
+        out_specs=[anywhere] * kinds,
+        out_shape=[jax.ShapeDtypeStruct((owners, *s.shape), s.dtype) for s in shards],
+        scratch_shapes=[
+            pltpu.SemaphoreType.DMA((kinds, sends)),
+            pltpu.SemaphoreType.DMA((kinds, 2, owners)),
+            pltpu.SemaphoreType.DMA((kinds,)),
+        ],
+        compiler_params=pltpu.CompilerParams(collective_id=0, has_side_effects=True),
+        name="gather",
+    )(*shards)
+
+
+def deliver_kernel(inner, kinds, *refs):
+    ins, outs = refs[:kinds], refs[kinds : 2 * kinds]
+    at = 2 * kinds
+    own, from_mate, from_b, from_a, from_z, final = (refs[at + i * kinds : at + (i + 1) * kinds] for i in range(6))
+    load_sem, mate_sem, b_sem, a_sem, z_sem, end_sem = refs[at + 6 * kinds :]
+    owners = DEEP * inner * inner
+    place = Place(inner)
+    steps = range(1, inner)
+    meet(place)
+
+    def columns(k, core):
+        half = outs[k].shape[-1] // 2
+        return pl.ds(pl.multiple_of(core * half, LANES), half)
+
+    loads, swaps = [], []
+    for k in range(kinds):
+        swap = remote(ins[k].at[:, :, columns(k, place.mate)], from_mate[k], mate_sem.at[k, 0], mate_sem.at[k, 1],
+                      place.partner())
+        swap.start()
+        load = pltpu.make_async_copy(ins[k].at[:, :, columns(k, place.core)], own[k], load_sem.at[k])
+        load.start()
+        swaps.append(swap)
+        loads.append(load)
+
+    sent = []
+
+    def add(k, block, other):
+        own[k][block] = (own[k][block].astype(F32) + other[...].astype(F32)).astype(BF)
+
+    for k in range(kinds):
+        loads[k].wait()
+        swaps[k].wait()
+        for db in tuple(steps) + (0,):
+            for da in range(inner):
+                for dz in range(DEEP):
+                    block = place.at(dz, da, db)
+                    add(k, block, from_mate[k].at[block])
+                    if db:
+                        slot = (db - 1) * inner * DEEP + da * DEEP + dz
+                        copy = remote(own[k].at[block], from_b[k].at[slot], b_sem.at[k, 0, slot],
+                                      b_sem.at[k, 1, slot], place.device(db=db))
+                        copy.start()
+                        sent.append((k, copy))
+    arrivals_b = list(sent)
+    sent = []
+    for k in range(kinds):
+        for kk, copy in arrivals_b:
+            if kk == k:
+                copy.wait()
+        for da in tuple(steps) + (0,):
+            for dz in range(DEEP):
+                block = place.at(dz, da)
+                for db in steps:
+                    add(k, block, from_b[k].at[(db - 1) * inner * DEEP + da * DEEP + dz])
+                if da:
+                    slot = (da - 1) * DEEP + dz
+                    copy = remote(own[k].at[block], from_a[k].at[slot], a_sem.at[k, 0, slot], a_sem.at[k, 1, slot],
+                                  place.device(da=da))
+                    copy.start()
+                    sent.append((k, copy))
+    arrivals_a = list(sent)
+    sent = []
+    for k in range(kinds):
+        for kk, copy in arrivals_a:
+            if kk == k:
+                copy.wait()
+        for dz in (2, 1, 3, 0):
+            block = place.at(dz)
+            for da in steps:
+                add(k, block, from_a[k].at[(da - 1) * DEEP + dz])
+            if dz:
+                copy = remote(own[k].at[block], from_z[k].at[dz - 1], z_sem.at[k, 0, dz - 1], z_sem.at[k, 1, dz - 1],
+                              place.device(dz=dz))
+                copy.start()
+                sent.append((k, copy))
+    ends = []
+    for k in range(kinds):
+        for kk, copy in sent:
+            if kk == k:
+                copy.wait()
+        total = own[k][place.at()].astype(F32)
+        for dz in range(1, DEEP):
+            total = total + from_z[k][dz - 1].astype(F32)
+        final[k][...] = total
+        there = outs[k].at[:, columns(k, place.core)]
+        far = remote(final[k], there, end_sem.at[k, 0], end_sem.at[k, 1], place.partner())
+        near = pltpu.make_async_copy(final[k], there, end_sem.at[k, 2])
+        far.start()
+        near.start()
+        ends += [far, near]
+    for copy in ends:
+        copy.wait()
+
+
+def delivered(grads):
+    owners = lax.axis_size("fsdp")
+    inner, kinds = inner_of(owners), len(grads)
+    anywhere = pl.BlockSpec(memory_space=pl.ANY)
+    halves = [(g.shape[1], g.shape[2] // 2) for g in grads]
+
+    def room(count, dtype=BF):
+        return [pltpu.VMEM((count, *h), dtype) for h in halves]
+
+    dma = pltpu.SemaphoreType.DMA
+    return pl.pallas_call(
+        functools.partial(deliver_kernel, inner, kinds),
+        in_specs=[anywhere] * kinds,
+        out_specs=[anywhere] * kinds,
+        out_shape=[jax.ShapeDtypeStruct(g.shape[1:], F32) for g in grads],
+        scratch_shapes=[
+            *room(owners), *room(owners), *room((inner - 1) * inner * DEEP), *room((inner - 1) * DEEP),
+            *room(DEEP - 1), *[pltpu.VMEM(h, F32) for h in halves],
+            dma((kinds,)), dma((kinds, 2)), dma((kinds, 2, (inner - 1) * inner * DEEP)),
+            dma((kinds, 2, (inner - 1) * DEEP)), dma((kinds, 2, DEEP - 1)), dma((kinds, 3)),
+        ],
+        compiler_params=pltpu.CompilerParams(collective_id=1, has_side_effects=True, vmem_limit_bytes=60 << 20),
+        name="deliver",
+    )(*grads)
+
+
 def swap_rows(array, rows):
     incoming = lax.ppermute(array[:rows], "win", [(0, 1), (1, 0)])
     return jnp.concatenate([incoming, array[rows:]], axis=0)
@@ -378,15 +645,9 @@
     )
 
 
-def owner_blocks(array, count):
-    return array.reshape(count, array.shape[0] // count, *array.shape[1:])
-
-
-def delivered(blocks):
-    mine = lax.all_to_all(blocks, "fsdp", 0, 0, tiled=True)
-    mine = jnp.sum(mine.astype(F32), axis=0).astype(BF)
-    other = lax.ppermute(mine, "win", [(0, 1), (1, 0)])
-    return mine.astype(F32) + other.astype(F32)
+def packed_row(parts):
+    row = jnp.concatenate(parts, axis=-1)
+    return jnp.pad(row, [(0, 0)] * (row.ndim - 1) + [(0, -row.shape[-1] % (2 * LANES))])
 
 
 def per_device(
@@ -399,14 +660,15 @@
     x = swap_rows(images.transpose(1, 2, 0, 3).reshape(rows * cols, imgs, d), top)
     ct = swap_rows(cotangent.transpose(1, 2, 0, 3).reshape(rows * cols, imgs, d), top)
     vectors = (norm1_gain, norm1_bias, q_bias, v_bias, proj_bias, norm2_gain, norm2_bias, fc2_bias, fc1_bias)
-    packed = lax.all_gather(jnp.concatenate(vectors), "fsdp", axis=0).astype(F32)
+    shards = (packed_row(vectors)[None], qkv_weight, proj_weight, fc1_weight, fc2_weight)
+    packed, *mats = gathered(shards)
+    packed = packed[:, 0].astype(F32)
     at, whole = 0, []
     for v in vectors:
         whole.append(packed[:, at : at + v.shape[0]].reshape(1, -1))
         at += v.shape[0]
     g1, b1, qb, vb, bp, g2, b2, b_out, b_in = whole
-    gather = functools.partial(lax.all_gather, axis_name="fsdp", axis=0, tiled=True)
-    w_qkv, w_proj, w_in, w_out = gather(qkv_weight), gather(proj_weight), gather(fc1_weight), gather(fc2_weight)
+    w_qkv, w_proj, w_in, w_out = (v.reshape(owners * v.shape[1], v.shape[2]) for v in mats)
     onehot, relative = relative_parts(rel_index, bias_table)
     rel = bias_of_pairs(relative, regions)
     qkv_bias = jnp.concatenate([qb, jnp.zeros_like(qb), vb], axis=1)
@@ -419,14 +681,15 @@
     tall = lambda v: v.reshape(rows * cols, imgs, d)
     gin, dwq, small1, bsum, rel_sum = back(x, tall(gm), tall(gatt), qkv, prob, g1, b1, w_qkv)
 
-    dw1, dw2, dwp, dwq = (delivered(owner_blocks(v, owners)) for v in (dw1, dw2, dwp, dwq))
     grads = (
         small1[0], small1[1], bsum[0, :d], bsum[0, 2 * d :], small2[2], small2[0], small2[1], small2[3], db_in[0],
     )
-    sums = delivered(jnp.concatenate([v.reshape(owners, -1) for v in grads], axis=1).astype(BF))
+    row = packed_row([v.reshape(owners, 1, -1) for v in grads]).astype(BF)
+    blocks = lambda v: v.reshape(owners, v.shape[0] // owners, v.shape[1])
+    sums, dwp, dw1, dw2, dwq = delivered((row, blocks(dwp), blocks(dw1), blocks(dw2), blocks(dwq)))
     at, own = 0, []
     for v in vectors:
-        own.append(sums[at : at + v.shape[0]].reshape(-1) if sums.ndim == 1 else sums[0, at : at + v.shape[0]])
+        own.append(sums[0, at : at + v.shape[0]])
         at += v.shape[0]
     dg1, db1, dqb, dvb, dbp, dg2, db2, db_out, db_in = own
     spread = jnp.asarray(spread_matrix())

time: 659 us -> 474 us (0.72)
  blocking collectives: 261 us -> 38.8 us
  Pallas kernels: 288 us -> 380 us
  waiting for transfers between devices: 23.8 us -> 0.01 us
  between operations: 14.1 us -> 1.01 us
  other arithmetic: 28.6 us -> 17.5 us
    all_to_all x4 -> x0, blocking collectives: 118 us -> none  [delivered(): mine = lax.all_to_all(blocks, 'fsdp', 0, 0, tiled=True)]
    pallas_call x0 -> x2, Pallas kernels: none -> 91.6 us  [the longest x1 47.5 us: delivered(): pl.pallas_call(functools.partial(deliver_kernel, inner, kinds), in_specs=...]
    all_gather x2 -> x0, blocking collectives: 84.6 us -> none  [the longest x1 42.8 us: per_device(): lax.all_gather(jnp.concatenate(vectors), 'fsdp', axis=0).astype(F32)]
    all_gather x3 -> x0, waiting for transfers between devices: 21.4 us -> none  [the longest x1 21.4 us: per_device(): gather(fc1_weight)]
    psum x1, blocking collectives: 58.3 us -> 38.8 us  [per_device(): table = lax.psum(table, ('fsdp', 'win'))]
  transfers between devices with their start and end apart: 13 -> 4, of which waited for: 3 -> 0; matrix products, arithmetic and copies ran while one was open for 9% -> 7% of each run, Pallas kernels for 8% -> 31%
where the time goes in v2:
time: 474 us
  Pallas kernels  380 us (80%)
  blocking collectives  38.8 us (8%)
  local copies, waits for them, and re-layouts  29.9 us (6%)
  other arithmetic  17.5 us (4%)
  matrix products  5.74 us (1%)
    pallas_call x1, Pallas kernels, back(): pl.pallas_call(back_kernel, grid=(imgs // NB,), in_specs=[tok, tok, tok,...  152 us
    pallas_call x1, Pallas kernels, mlp(): pl.pallas_call(mlp_kernel, grid=(rows // tile,), in_specs=[row, row, row,...  80.9 us
    pallas_call x1, Pallas kernels, attend(): pl.pallas_call(attend_kernel, grid=(imgs // NB,), in_specs=[pl.BlockSpec(...  55 us
    pallas_call x1, Pallas kernels, delivered(): pl.pallas_call(functools.partial(deliver_kernel, inner, kinds), in_specs=...  47.5 us
    pallas_call x1, Pallas kernels, gathered(): pl.pallas_call(functools.partial(gather_kernel, inner, kinds), in_specs=[...  44.1 us
    psum x1, blocking collectives, per_device(): table = lax.psum(table, ('fsdp', 'win'))  38.8 us
    concatenate x4, other arithmetic, swap_rows(): return jnp.concatenate([incoming, array[rows:]], axis=0)  15.7 us
    slice x4, local copies, waits for them, and re-layouts, swap_rows(): incoming = lax.ppermute(array[:rows], 'win', [(0, 1), (1, 0)])  10.6 us
  transfers between devices with their start and end apart: 4, of which 0 were waited for; matrix products, arithmetic and copies ran while one was open for 7% of the time, Pallas kernels for 31%

profile of v2, /device:TPU:0, one launch (start us, length us, event | category | flops | bytes accessed | tf_op | source)
XLA Modules:
  0.0 473.9 jit_solution(7328949333319472332)
XLA Ops:
  0.7 2.8 slice.231
  3.5 0.5 collective-permute-start.1
  4.0 2.7 slice.225
  6.7 0.1 slice_reduce_fusion.9
  6.8 1.4 slice.226
  8.4 0.2 slice.232
  8.6 0.3 copy-done.22
  9.1 0.1 concatenate.34
  9.2 0.6 broadcast_in_dim.29.refs_0_
  9.7 0.1 slice.188
  10.2 0.1 eq.34
  10.3 44.1 %gather.1 = (bf16[16,1,512]{2,1,0:T(2,128)(2,1)}, bf16[16,32,1536]{2,1,0:T(8,128)(2,1)}, bf16[16,32,512]{2,1,0:T(8,128)(2,1)}, bf16[16,32,2048]{2,1,0:T(8,128)(2,1)}, bf16[16,128,512]{2,1,0:T(8,128)(2,1)}) custom-call(bf16[1,512]{1,0:T(2,128)(2,1)} %broadcast_in_dim.29.refs_0_, bf16[32,1536]{1,0:T(8,128)(2,1)} %refs_1_.1, bf16[32,512]{1,0:T(8,128)(2,1)} %refs_2_.1, ...), custom_call_target="tpu_custom_call" | custom-call | tf_op jit(solution)/shard_map/gather/pallas_call | solution.py:472
  54.4 0.8 copy.47
  55.2 0.6 slice.236
  55.8 1.2 fusion.1
  57.1 0.1 fusion.10
  57.1 0.1 pad_add_fusion.1
  57.3 0.2 reshape.173
  57.5 0.7 reshape.183.b2_ref
  58.2 0.6 reshape.169.b_ref
  58.8 0.7 reshape.168.g_ref
  59.5 0.7 reshape.179.b_ref
  60.1 0.6 reshape.178.g_ref
  60.7 0.7 reshape.177.bp_ref
  61.7 0.9 fusion.7
  62.6 1.5 fusion.2
  64.1 1.0 pad_select_fusion.rel_ref
  65.1 0.6 fusion.9.qb_ref
  65.7 3.3 pad_maximum_fusion.1.x_ref
  69.0 55.0 %attend.1 = (bf16[32,12,112,128]{3,2,1,0:T(8,128)(2,1)}, bf16[98,32,512]{2,1,0:T(8,128)(2,1)}, bf16[32,16,112,112]{3,2,1,0:T(8,128)(2,1)}) custom-call(bf16[98,32,512]{2,1,0:T(8,128)(2,1)} %pad_maximum_fusion.1.x_ref, f32[1,512]{1,0:T(1,128)} %reshape.168.g_ref, f32[1,512]{1,0:T(1,128)} %reshape.169.b_ref, bf16[512,1536]{1,0:T(8,128)(2,1)} %bitcast.77, ...), custom_call_target="tpu_custom_call" | custom-call | tf_op jit(solution)/shard_map/attend/pallas_call | solution.py:120
  124.1 3.3 pad_maximum_fusion.2
  127.4 80.9 %mlp.1 = (bf16[3136,512]{1,0:T(8,128)(2,1)}, f32[3136,512]{1,0:T(8,128)}, bf16[3136,512]{1,0:T(8,128)(2,1)}, bf16[512,512]{1,0:T(8,128)(2,1)}, bf16[512,2048]{1,...) custom-call(bf16[3136,512]{1,0:T(8,128)(2,1)} %bitcast.70, ...), custom_call_target="tpu_custom_call" | custom-call | tf_op jit(solution)/shard_map/mlp/pallas_call | solution.py:213
  208.3 152.4 %back.1 = (f32[98,32,512]{2,1,0:T(8,128)}, bf16[512,1536]{1,0:T(8,128)(2,1)}, f32[8,512]{1,0:T(8,128)}, f32[1,1536]{1,0:T(1,128)}, f32[16,112,112]{2,1,0:T(8,128)}) custom-call(bf16[98,32,512]{2,1,0:T(8,128)(2,1)} %pad_maximum_fusion.1.x_ref, f32[98,32,512]{2,1,0:T(8,128)} %bitcast.76, bf16[98,32,512]{2,1,0:T(8,128)(2,1)} %bitcast.85, ...), custom_call_target="tpu_custom_call" | custom-call | tf_op jit(solution)/shard_map/back/pallas_call | solution.py:311
  360.7 3.9 slice.205
  364.6 0.4 collective-permute-start.3
  365.0 1.2 slice.201
  366.2 0.1 slice.203
  366.3 2.0 copy-done.4
  368.3 2.2 slice.206
  370.6 0.1 reshape_squeeze.51
  370.7 0.1 reshape_squeeze.49
  370.8 0.1 reshape_squeeze.50
  370.9 0.1 reshape_squeeze.48
  371.0 0.1 reshape_squeeze.55
  371.1 0.1 reshape_squeeze.54
  371.2 0.1 reshape_squeeze.53
  371.3 0.1 reshape_squeeze.52
  371.3 0.1 collective-permute-start.2
  371.5 0.2 concatenate.42
  371.7 0.6 pad.20.refs_0_
  372.4 47.5 %deliver.1 = (f32[1,512]{1,0:T(1,128)}, f32[32,512]{1,0:T(8,128)}, f32[32,2048]{1,0:T(8,128)}, f32[128,512]{1,0:T(8,128)}, f32[32,1536]{1,0:T(8,128)}) custom-call(bf16[16,1,512]{2,1,0:T(2,128)(2,1)} %pad.20.refs_0_, bf16[16,32,512]{2,1,0:T(8,128)(2,1)} %bitcast.91, bf16[16,32,2048]{2,1,0:T(8,128)(2,1)} %bitcast.86, bf16[16,128,512]{2,1,0:T(8,128)(2,1)} %bitcast.87, ...), custom_call_target="tpu_custom_call" | custom-call | tf_op jit(solution)/shard_map/deliver/pallas_call | solution.py:591
  419.9 0.7 fusion.5
  420.6 0.5 convolution_bitcast_fusion
  421.1 0.2 reshape.192
  421.3 0.9 fusion
  422.2 38.8 %psum.7 = f32[169,16]{0,1:T(8,128)} all-reduce(f32[169,16]{0,1:T(8,128)S(1)} %fusion), channel_id=1, replica_groups=mesh['fsdp'=16,'win'=2] {'fsdp','win'}, use_global_device_ids=true, to_apply=%region_0.1 | all-reduce | flops 2704 | bytes 21632 | tf_op jit(solution)/shard_map/psum | solution.py:698
  461.0 0.5 slice_bitcast_fusion.1
  461.5 0.6 slice_bitcast_fusion
  462.1 3.5 pad_maximum_fusion.3
  465.6 5.6 %pad_maximum_fusion = f32[98,32,512]{2,1,0:T(8,128)} fusion(f32[56,32,512]{2,1,0:T(8,128)S(1)} %copy-done.2, f32[42,32,512]{2,1,0:T(8,128)} %collective-permute-done.3), kind=kLoop, calls=%fused_computation | loop fusion | flops 1605632 | bytes 12845056 | tf_op jit(solution)/shard_map/concatenate | solution.py:609
  471.2 0.7 copy.52
  471.9 0.6 copy.53
  472.5 0.7 copy.54
  473.2 0.7 copy.55
  (85 shorter events, 1.1 us)
Async XLA Ops:
  0.6 55.2 %copy-start = (f32[169,16]{0,1:T(8,128)S(1)}, f32[169,16]{0,1:T(8,128)}, u32[]{:S(2)}) copy-start(f32[169,16]{0,1:T(8,128)} %param.35) | copy-start | bytes 32452
  0.7 6.0 %copy-start.21 = (s32[1,2,49]{2,1,0:T(2,128)S(1)}, s32[1,2,49]{2,1,0:T(2,128)}, u32[]{:S(2)}) copy-start(s32[1,2,49]{2,1,0:T(2,128)} %param.36) | copy-start | bytes 1180
  0.7 6.2 %copy-start.5 = (bf16[32,7,14,512]{3,0,2,1:T(8,128)(2,1)S(1)}, bf16[32,7,14,512]{3,0,2,1:T(8,128)(2,1)}, u32[]{:S(2)}) copy-start(bf16[32,7,14,512]{3,0,2,1:T(8,128)(2,1)} %param.21) | copy-start | bytes 9633796
  3.5 120.6 %collective-permute-start.1 = (bf16[42,32,512]{2,1,0:T(8,128)(2,1)}, bf16[42,32,512]{2,1,0:T(8,128)(2,1)}, u32[]{:S(2)}, u32[]{:S(2)}) collective-permute-start(bf16[42,32,512]{2,1,0:T(8,128)(2,1)} %bitcast.9), channel_id=1, source_target_pairs={{0,1},{1,0},{2,3},{3,2},{4,5},{5,4},{6,7},{7,6},{8,9},{9,8},{10,11... | collective-permute-start | bytes 4128776 | tf_op jit(solution)/shard_map/ppermute | solution.py:608
  4.0 4.3 copy-start.6
  6.7 59.0 %collective-permute-start = (bf16[42,32,512]{2,1,0:T(8,128)(2,1)}, bf16[42,32,512]{2,1,0:T(8,128)(2,1)}, u32[]{:S(2)}, u32[]{:S(2)}) collective-permute-start(bf16[42,32,512]{2,1,0:T(8,128)(2,1)} %bitcast.1), channel_id=1, source_target_pairs={{0,1},{1,0},{2,3},{3,2},{4,5},{5,4},{6,7},{7,6},{8,9},{9,8},{10,11... | collective-permute-start | bytes 4128776 | tf_op jit(solution)/shard_map/ppermute | solution.py:608
  8.3 0.7 copy-start.22
  8.3 0.7 copy-start.23
  8.3 0.7 copy-start.24
  8.3 0.7 copy-start.25
  8.3 0.7 copy-start.26
  8.3 0.7 copy-start.27
  8.3 0.7 copy-start.28
  8.3 0.7 copy-start.29
  8.3 0.7 copy-start.30
  8.4 1.8 copy-start.14
  8.4 53.3 %copy-start.9 = (f32[98,49,1]{0,1,2:T(8,128)S(1)}, f32[98,49,1]{0,1,2:T(8,128)}, u32[]{:S(2)}) copy-start(f32[98,49,1]{0,1,2:T(8,128)} %constant.29) | copy-start | bytes 57628
  8.4 54.2 %copy-start.17 = (pred[98,98]{1,0:T(8,128)(4,1)S(1)}, pred[98,98]{1,0:T(8,128)(4,1)}, u32[]{:S(2)}) copy-start(pred[98,98]{1,0:T(8,128)(4,1)} %constant.17.clone) | copy-start | bytes 28816
  61.6 4.2 copy-start.3
  360.7 4.3 copy-start.7
  364.6 101.0 %collective-permute-start.3 = (f32[42,32,512]{2,1,0:T(8,128)}, f32[42,32,512]{2,1,0:T(8,128)}, u32[]{:S(2)}, u32[]{:S(2)}) collective-permute-start(f32[42,32,512]{2,1,0:T(8,128)} %slice.205), channel_id=1, source_target_pairs={{0,1},{1,0},{2,3},{3,2},{4,5},{5,4},{6,7},{7,6},{8,9},{9,8},{10,11... | collective-permute-start | bytes 8257544 | tf_op jit(solution)/shard_map/ppermute | solution.py:608
  365.0 3.3 copy-start.4
  368.3 2.2 copy-start.16
  368.3 2.2 copy-start.20
  368.3 2.6 copy-start.15
  368.3 3.1 copy-start.18
  371.3 90.8 %collective-permute-start.2 = (bf16[42,32,512]{2,1,0:T(8,128)(2,1)}, bf16[42,32,512]{2,1,0:T(8,128)(2,1)}, u32[]{:S(2)}, u32[]{:S(2)}) collective-permute-start(bf16[42,32,512]{2,1,0:T(8,128)(2,1)} %bitcast.16), channel_id=1, source_target_pairs={{0,1},{1,0},{2,3},{3,2},{4,5},{5,4},{6,7},{7,6},{8,9},{9,8},{10,11... | collective-permute-start | bytes 4128776 | tf_op jit(solution)/shard_map/ppermute | solution.py:608
  372.4 47.5 %copy-start.8 = (f32[16,112,112]{2,1,0:T(8,128)S(1)}, f32[16,112,112]{2,1,0:T(8,128)}, u32[]{:S(2)}) copy-start(f32[16,112,112]{2,1,0:T(8,128)} %get-tuple-element.67) | copy-start | bytes 2408452
  419.9 41.1 %copy-start.19 = (f32[1,512]{1,0:T(1,128)S(1)}, f32[1,512]{1,0:T(1,128)}, u32[]{:S(2)}) copy-start(f32[1,512]{1,0:T(1,128)} %get-tuple-element.62) | copy-start | bytes 6148
  462.1 3.5 copy-start.2
  465.6 5.6 %copy-start.12 = (f32[32,1536]{1,0:T(8,128)S(1)}, f32[32,1536]{1,0:T(8,128)}, u32[]{:S(2)}) copy-start(f32[32,1536]{1,0:T(8,128)} %get-tuple-element.116) | copy-start | bytes 589828
  465.6 6.3 %copy-start.13 = (f32[32,512]{1,0:T(8,128)S(1)}, f32[32,512]{1,0:T(8,128)}, u32[]{:S(2)}) copy-start(f32[32,512]{1,0:T(8,128)} %get-tuple-element.119) | copy-start | bytes 196612
  465.6 6.9 %copy-start.11 = (f32[32,2048]{1,0:T(8,128)S(1)}, f32[32,2048]{1,0:T(8,128)}, u32[]{:S(2)}) copy-start(f32[32,2048]{1,0:T(8,128)} %get-tuple-element.123) | copy-start | bytes 786436
  465.6 7.6 %copy-start.10 = (f32[128,512]{1,0:T(8,128)S(1)}, f32[128,512]{1,0:T(8,128)}, u32[]{:S(2)}) copy-start(f32[128,512]{1,0:T(8,128)} %get-tuple-element.125) | copy-start | bytes 786436
  465.6 8.3 %copy-start.1 = (f32[169,16]{0,1:T(8,128)S(1)}, f32[169,16]{0,1:T(8,128)}, u32[]{:S(2)}) copy-start(f32[169,16]{0,1:T(8,128)} %param.35) | copy-start | bytes 32452

commit v3 on v2

--- a/solution.py
+++ b/solution.py
@@ -12,6 +12,7 @@
 WIN = 7
 SHIFT = 3
 TOK = 98
+TOP = 42
 PAD = 112
 LANES = 128
 GROUPS = 4
@@ -70,19 +71,35 @@
     return [(lane == h).astype(BF) for h in range(GROUPS)]
 
 
-def attend_kernel(x_ref, g_ref, b_ref, w_ref, qb_ref, rel_ref, qkv_ref, att_ref, prob_ref, wide, joined):
+def shifted_rows(x_ref, halo_ref):
+    x = jnp.concatenate([halo_ref[...], x_ref[TOP:]], axis=0)
+    return x.astype(F32).reshape(x.shape[0] * NB, x.shape[-1])
+
+
+def own_lanes(stack):
+    lane = lax.broadcasted_iota(jnp.int32, (1, LANES), 1) // HD
+    out = stack[:PAD]
+    for h in range(1, GROUPS):
+        out = jnp.where(lane == h, stack[h * PAD : (h + 1) * PAD], out)
+    return out
+
+
+def attend_kernel(x_ref, halo_ref, vec_ref, w_ref, rel_ref, qkv_ref, att_ref, prob_ref, wide, joined):
     d = x_ref.shape[-1]
-    n, _ = normalized(x_ref[...].astype(F32).reshape(TOK * NB, d))
-    normed = (n * g_ref[...] + b_ref[...]).astype(BF)
+    n, _ = normalized(shifted_rows(x_ref, halo_ref))
+    normed = (n * vec_ref[0:1] + vec_ref[1:2]).astype(BF)
     lanes3 = 3 * d // LANES
-    chunk = 512
+    chunk = d
+    biases = (vec_ref[2:3], None, vec_ref[3:4])
 
     @pl.when(pl.program_id(0) == 0)
     def _():
         wide[:, TOK * NB :, :] = jnp.zeros((lanes3, (PAD - TOK) * NB, LANES), F32)
 
     for c in range(3 * d // chunk):
-        part = mm(normed, w_ref[:, c * chunk : (c + 1) * chunk]) + qb_ref[:, c * chunk : (c + 1) * chunk]
+        part = mm(normed, w_ref[:, c * chunk : (c + 1) * chunk])
+        if biases[c] is not None:
+            part = part + biases[c]
         for k in range(chunk // LANES):
             wide[c * (chunk // LANES) + k, : TOK * NB, :] = part[:, k * LANES : (k + 1) * LANES]
     masks = head_masks()
@@ -97,15 +114,16 @@
             qkv_ref[i, g] = q
             qkv_ref[i, per + g] = k
             qkv_ref[i, 2 * per + g] = v
-            total = None
+            scores = mm_nt(jnp.concatenate([k * m for m in masks], axis=0), q)
+            v_t = v.T
+            heads = []
             for h in range(GROUPS):
-                s = mm_nt(q * masks[h], k) * scale + rel_ref[g * GROUPS + h][:, :PAD]
-                e = jnp.exp(s - jnp.max(s, axis=-1, keepdims=True))
-                p = (e / jnp.sum(e, axis=-1, keepdims=True)).astype(BF)
+                s = scores[h * PAD : (h + 1) * PAD] * scale + rel_ref[g * GROUPS + h][:, :PAD]
+                e = jnp.exp(s - jnp.max(s, axis=0, keepdims=True))
+                p = (e * (1.0 / jnp.sum(e, axis=0, keepdims=True))).astype(BF)
                 prob_ref[i, g * GROUPS + h] = p
-                o = mm(p, v * masks[h])
-                total = o if total is None else total + o
-            joined[g, pl.ds(i, PAD, stride=NB), :] = total
+                heads.append(mm(v_t[h * HD : (h + 1) * HD], p))
+            joined[g, pl.ds(i, PAD, stride=NB), :] = jnp.concatenate(heads, axis=0).T
         return carry
 
     lax.fori_loop(0, NB, one, 0)
@@ -113,7 +131,7 @@
         att_ref[:, :, g * LANES : (g + 1) * LANES] = joined[g, : TOK * NB, :].astype(BF).reshape(TOK, NB, LANES)
 
 
-def attend(x, g, b, w, qb, rel):
+def attend(x, halo, vecs, w, rel):
     _, imgs, d = x.shape
     full = lambda *shape: pl.BlockSpec(shape, lambda i: (0,) * len(shape), pipeline_mode=pl.Buffered(1))
     per = d // LANES
@@ -122,7 +140,8 @@
         grid=(imgs // NB,),
         in_specs=[
             pl.BlockSpec((TOK, NB, d), lambda i: (0, i, 0)),
-            full(1, d), full(1, d), full(d, 3 * d), full(1, 3 * d), full(HEADS, PAD, LANES),
+            pl.BlockSpec((TOP, NB, d), lambda i: (0, i, 0)),
+            full(8, d), full(d, 3 * d), full(HEADS, PAD, LANES),
         ],
         out_specs=[
             pl.BlockSpec((NB, 3 * per, PAD, LANES), lambda i: (i, 0, 0, 0)),
@@ -140,11 +159,11 @@
         ],
         compiler_params=pltpu.CompilerParams(vmem_limit_bytes=60 << 20),
         name="attend",
-    )(x, g, b, w, qb, rel)
-
-
-def mlp_kernel(x_ref, att_ref, ct_ref, wp_ref, bp_ref, g_ref, b_ref, w1_ref, b1_ref, w2_ref, b2_ref,
-               out_ref, gm_ref, gatt_ref, dwp_ref, dw1_ref, dw2_ref, db1_ref, small_ref,
+    )(x, halo, vecs, w, rel)
+
+
+def mlp_kernel(tops, x_ref, halo_ref, att_ref, ct_ref, ct_halo_ref, wp_ref, vec_ref, w1_ref, b1_ref, w2_ref,
+               top_ref, rest_ref, gm_ref, gatt_ref, dwp_ref, dw1_ref, dw2_ref, db1_ref, small_ref,
                awp, aw1, aw2, ab1, asm):
     step = pl.program_id(0)
     d = x_ref.shape[-1]
@@ -160,14 +179,15 @@
         asm[...] = jnp.zeros_like(asm)
 
     att = att_ref[...]
-    gb = ct_ref[...]
+    above = step < tops
+    gb = jnp.where(above, ct_halo_ref[...], ct_ref[...])
     grad_out = gb.astype(F32)
-    middle = x_ref[...].astype(F32) + mm(att, wp_ref[...]) + bp_ref[...]
+    middle = jnp.where(above, halo_ref[...], x_ref[...]).astype(F32) + mm(att, wp_ref[...]) + vec_ref[4:5]
     n, r = normalized(middle)
-    normed = (n * g_ref[...] + b_ref[...]).astype(BF)
+    normed = (n * vec_ref[5:6] + vec_ref[6:7]).astype(BF)
     normed_t = normed.T
     gb_t = gb.T
-    out = middle + b2_ref[...]
+    out = middle + vec_ref[7:8]
     m = None
     for c in range(ff // chunk):
         at = slice(c * chunk, (c + 1) * chunk)
@@ -183,8 +203,16 @@
         aw1[:, at] += mm(normed_t, ghb)
         part = mm_nt(ghb, w1_ref[:, at])
         m = part if m is None else m + part
-    out_ref[...] = out.astype(BF)
-    grad_middle = grad_out + norm_back(m * g_ref[...], n, r)
+
+    @pl.when(above)
+    def _():
+        top_ref[...] = out.astype(BF)
+
+    @pl.when(jnp.logical_not(above))
+    def _():
+        rest_ref[...] = out.astype(BF)
+
+    grad_middle = grad_out + norm_back(m * vec_ref[5:6], n, r)
     gm_ref[...] = grad_middle
     gp = grad_middle.astype(BF)
     gatt_ref[...] = mm_nt(gp, wp_ref[...]).astype(BF)
@@ -205,19 +233,24 @@
         small_ref[...] = asm[...]
 
 
-def mlp(x, att, ct, wp, bp, g, b, w1, b1, w2, b2, tile=448):
+def mlp(x, halo, att, ct, ct_halo, wp, vecs, w1, b1, w2):
     rows, d = x.shape
+    tile = halo.shape[0] // 3
+    tops = 3
     ff = w1.shape[-1]
     full = lambda *shape: pl.BlockSpec(shape, lambda i: (0,) * len(shape), pipeline_mode=pl.Buffered(1))
     row = pl.BlockSpec((tile, d), lambda i: (i, 0))
+    own = pl.BlockSpec((tile, d), lambda i: (jnp.maximum(i, tops), 0))
+    top = pl.BlockSpec((tile, d), lambda i: (jnp.minimum(i, tops - 1), 0))
+    rest = pl.BlockSpec((tile, d), lambda i: (jnp.maximum(i - tops, 0), 0))
     return pl.pallas_call(
-        mlp_kernel,
+        functools.partial(mlp_kernel, tops),
         grid=(rows // tile,),
-        in_specs=[row, row, row, full(d, d), full(1, d), full(1, d), full(1, d), full(d, ff), full(1, ff),
-                  full(ff, d), full(1, d)],
-        out_specs=[row, row, row, full(d, d), full(d, ff), full(ff, d), full(1, ff), full(8, d)],
+        in_specs=[own, top, row, own, top, full(d, d), full(8, d), full(d, ff), full(1, ff), full(ff, d)],
+        out_specs=[top, rest, row, row, full(d, d), full(d, ff), full(ff, d), full(1, ff), full(8, d)],
         out_shape=[
-            jax.ShapeDtypeStruct((rows, d), BF),
+            jax.ShapeDtypeStruct((tops * tile, d), BF),
+            jax.ShapeDtypeStruct((rows - tops * tile, d), BF),
             jax.ShapeDtypeStruct((rows, d), F32),
             jax.ShapeDtypeStruct((rows, d), BF),
             jax.ShapeDtypeStruct((d, d), BF),
@@ -232,11 +265,11 @@
         ],
         compiler_params=pltpu.CompilerParams(vmem_limit_bytes=60 << 20),
         name="mlp",
-    )(x, att, ct, wp, bp, g, b, w1, b1, w2, b2)
-
-
-def back_kernel(x_ref, gm_ref, gatt_ref, qkv_ref, prob_ref, g_ref, b_ref, w_ref,
-                gin_ref, dw_ref, small_ref, bsum_ref, rel_ref, wide, grads, aw, asm, abs_):
+    )(x, halo, att, ct, ct_halo, wp, vecs, w1, b1, w2)
+
+
+def back_kernel(x_ref, halo_ref, gm_ref, gatt_ref, qkv_ref, prob_ref, vec_ref, w_ref,
+                top_ref, rest_ref, dw_ref, small_ref, bsum_ref, rel_ref, wide, grads, aw, asm, abs_):
     step = pl.program_id(0)
     d = x_ref.shape[-1]
     per = d // LANES
@@ -260,27 +293,28 @@
             q = qkv_ref[i, g]
             k = qkv_ref[i, per + g]
             v = qkv_ref[i, 2 * per + g]
-            dq = dk = dv = None
+            dps = mm_nt(jnp.concatenate([v * m for m in masks], axis=0), ga)
+            k_t = k.T
+            probs, marks, dq = [], [], []
             for h in range(GROUPS):
                 p = prob_ref[i, g * GROUPS + h]
                 pf = p.astype(F32)
-                gah = ga * masks[h]
-                dp = mm_nt(gah, v)
-                inner = jnp.sum(pf * dp, axis=-1, keepdims=True)
-                ds = (pf * (dp - inner)).astype(BF)
+                dp = dps[h * PAD : (h + 1) * PAD]
+                ds = (pf * (dp - jnp.sum(pf * dp, axis=0, keepdims=True))).astype(BF)
                 rel_ref[g * GROUPS + h] += ds.astype(F32)
-                a, b, c = mm(ds, k * masks[h]), mm_tn(ds, q * masks[h]), mm_tn(p, gah)
-                dq = a if dq is None else dq + a
-                dk = b if dk is None else dk + b
-                dv = c if dv is None else dv + c
-            grads[g, pl.ds(i, PAD, stride=NB), :] = dq * scale
+                dq.append(mm(k_t[h * HD : (h + 1) * HD], ds))
+                probs.append(p)
+                marks.append(ds)
+            dv = own_lanes(mm(jnp.concatenate(probs, axis=0), ga))
+            dk = own_lanes(mm(jnp.concatenate(marks, axis=0), q))
+            grads[g, pl.ds(i, PAD, stride=NB), :] = jnp.concatenate(dq, axis=0).T * scale
             grads[per + g, pl.ds(i, PAD, stride=NB), :] = dk * scale
             grads[2 * per + g, pl.ds(i, PAD, stride=NB), :] = dv
         return carry
 
     lax.fori_loop(0, NB, one, 0)
-    n, r = normalized(x_ref[...].astype(F32).reshape(TOK * NB, d))
-    normed = (n * g_ref[...] + b_ref[...]).astype(BF)
+    n, r = normalized(shifted_rows(x_ref, halo_ref))
+    normed = (n * vec_ref[0:1] + vec_ref[1:2]).astype(BF)
     normed_t = normed.T
     dn = None
     for c in range(3):
@@ -293,8 +327,10 @@
     dn = dn.astype(BF).astype(F32)
     asm[0:1, :] += col_sum(dn * n)
     asm[1:2, :] += col_sum(dn)
-    gin = gm_ref[...].reshape(TOK * NB, d) + norm_back(dn * g_ref[...], n, r)
-    gin_ref[...] = gin.reshape(TOK, NB, d)
+    gin = gm_ref[...].reshape(TOK * NB, d) + norm_back(dn * vec_ref[0:1], n, r)
+    gin = gin.reshape(TOK, NB, d)
+    top_ref[...] = gin[:TOP]
+    rest_ref[...] = gin[TOP:]
 
     @pl.when(step == pl.num_programs(0) - 1)
     def _():
@@ -303,7 +339,7 @@
         bsum_ref[...] = abs_[...]
 
 
-def back(x, gm, gatt, qkv, prob, g, b, w):
+def back(x, halo, gm, gatt, qkv, prob, vecs, w):
     _, imgs, d = x.shape
     per = d // LANES
     full = lambda *shape: pl.BlockSpec(shape, lambda i: (0,) * len(shape), pipeline_mode=pl.Buffered(1))
@@ -312,14 +348,15 @@
         back_kernel,
         grid=(imgs // NB,),
         in_specs=[
-            tok, tok, tok,
+            tok, pl.BlockSpec((TOP, NB, d), lambda i: (0, i, 0)), tok, tok,
             pl.BlockSpec((NB, 3 * per, PAD, LANES), lambda i: (i, 0, 0, 0)),
             pl.BlockSpec((NB, HEADS, PAD, PAD), lambda i: (i, 0, 0, 0)),
-            full(1, d), full(1, d), full(d, 3 * d),
-        ],
-        out_specs=[tok, full(d, 3 * d), full(8, d), full(1, 3 * d), full(HEADS, PAD, PAD)],
+            full(8, d), full(d, 3 * d),
+        ],
+        out_specs=[pl.BlockSpec((TOP, NB, d), lambda i: (0, i, 0)), pl.BlockSpec((TOK - TOP, NB, d), lambda i: (0, i, 0)), full(d, 3 * d), full(8, d), full(1, 3 * d), full(HEADS, PAD, PAD)],
         out_shape=[
-            jax.ShapeDtypeStruct((TOK, imgs, d), F32),
+            jax.ShapeDtypeStruct((TOP, imgs, d), F32),
+            jax.ShapeDtypeStruct((TOK - TOP, imgs, d), F32),
             jax.ShapeDtypeStruct((d, 3 * d), BF),
             jax.ShapeDtypeStruct((8, d), F32),
             jax.ShapeDtypeStruct((1, 3 * d), F32),
@@ -334,7 +371,7 @@
         ],
         compiler_params=pltpu.CompilerParams(vmem_limit_bytes=60 << 20),
         name="back",
-    )(x, gm, gatt, qkv, prob, g, b, w)
+    )(x, halo, gm, gatt, qkv, prob, vecs, w)
 
 
 DEEP = 4
@@ -386,9 +423,10 @@
     )
 
 
-def gather_kernel(inner, kinds, *refs):
-    ins, outs = refs[:kinds], refs[kinds : 2 * kinds]
-    send_sem, recv_sem, own_sem = refs[2 * kinds :]
+def gather_kernel(inner, kinds, fields, *refs):
+    ins, maps = refs[:kinds], refs[kinds : kinds + fields]
+    outs, halos = refs[kinds + fields : 2 * kinds + fields], refs[2 * kinds + fields : 2 * (kinds + fields)]
+    send_sem, recv_sem, own_sem, halo_sem = refs[2 * (kinds + fields) :]
     place = Place(inner)
     meet(place)
 
@@ -422,6 +460,10 @@
             send(k, mine(k), place.at(), place.device(da=d))
         for d in steps:
             send(k, mine(k), place.at(), place.device(db=d))
+    swaps = [remote(maps[f].at[:TOP], halos[f], halo_sem.at[f, 0], halo_sem.at[f, 1], place.partner())
+             for f in range(fields)]
+    for copy in swaps:
+        copy.start()
     for k in range(kinds):
         copy = pltpu.make_async_copy(ins[k], outs[k].at[place.at()], own_sem.at[k])
         copy.start()
@@ -458,37 +500,41 @@
         own[k].wait()
         for copy in sent[k]:
             copy.wait_send()
+    for copy in swaps:
+        copy.wait()
 
 
 def inner_of(owners):
     return int(round((owners // DEEP) ** 0.5))
 
 
-def gathered(shards):
+def gathered(shards, maps):
     owners = lax.axis_size("fsdp")
-    inner, kinds = inner_of(owners), len(shards)
+    inner, kinds, fields = inner_of(owners), len(shards), len(maps)
     sends = (DEEP - 1) + 2 * (inner - 1) + 1 + (DEEP - 1) * (2 * inner - 1) + DEEP * (inner - 1) * inner + DEEP * inner * (inner - 1)
     anywhere = pl.BlockSpec(memory_space=pl.ANY)
     return pl.pallas_call(
-        functools.partial(gather_kernel, inner, kinds),
-        in_specs=[anywhere] * kinds,
-        out_specs=[anywhere] * kinds,
-        out_shape=[jax.ShapeDtypeStruct((owners, *s.shape), s.dtype) for s in shards],
+        functools.partial(gather_kernel, inner, kinds, fields),
+        in_specs=[anywhere] * (kinds + fields),
+        out_specs=[anywhere] * (kinds + fields),
+        out_shape=[jax.ShapeDtypeStruct((owners, *s.shape), s.dtype) for s in shards]
+        + [jax.ShapeDtypeStruct((TOP, *m.shape[1:]), m.dtype) for m in maps],
         scratch_shapes=[
             pltpu.SemaphoreType.DMA((kinds, sends)),
             pltpu.SemaphoreType.DMA((kinds, 2, owners)),
             pltpu.SemaphoreType.DMA((kinds,)),
+            pltpu.SemaphoreType.DMA((fields, 2)),
         ],
         compiler_params=pltpu.CompilerParams(collective_id=0, has_side_effects=True),
         name="gather",
-    )(*shards)
+    )(*shards, *maps)
 
 
 def deliver_kernel(inner, kinds, *refs):
-    ins, outs = refs[:kinds], refs[kinds : 2 * kinds]
-    at = 2 * kinds
+    ins, table_ref, outs, sum_ref = refs[:kinds], refs[kinds], refs[kinds + 1 : 2 * kinds + 1], refs[2 * kinds + 1]
+    at = 2 * kinds + 2
     own, from_mate, from_b, from_a, from_z, final = (refs[at + i * kinds : at + (i + 1) * kinds] for i in range(6))
-    load_sem, mate_sem, b_sem, a_sem, z_sem, end_sem = refs[at + 6 * kinds :]
+    load_sem, mate_sem, b_sem, a_sem, z_sem, end_sem, parts, part_sem = refs[at + 6 * kinds :]
     owners = DEEP * inner * inner
     place = Place(inner)
     steps = range(1, inner)
@@ -497,6 +543,29 @@
     def columns(k, core):
         half = outs[k].shape[-1] // 2
         return pl.ds(pl.multiple_of(core * half, LANES), half)
+
+    def table_stage(stage, value, count, mine, peer):
+        parts[stage, mine] = value
+        copies = [remote(parts.at[stage, mine], parts.at[stage, mine], part_sem.at[stage, 0, d],
+                         part_sem.at[stage, 1, d], peer(d)) for d in range(1, count)]
+        for copy in copies:
+            copy.start()
+        return copies, stage, count
+
+    def table_sum(begun):
+        copies, stage, count = begun
+        for copy in copies:
+            copy.wait()
+        total = parts[stage, 0]
+        for i in range(1, count):
+            total = total + parts[stage, i]
+        return total
+
+    u = place.a * (1 - place.core) + place.b * place.core
+    v = place.b * (1 - place.core) + place.a * place.core
+    along_u = lambda d: (place.at(da=d * (1 - place.core), db=d * place.core), place.core)
+    along_v = lambda d: (place.at(da=d * place.core, db=d * (1 - place.core)), place.core)
+    begun = table_stage(0, table_ref[...], 2, place.core, lambda d: place.partner())
 
     loads, swaps = [], []
     for k in range(kinds):
@@ -527,6 +596,7 @@
                                       b_sem.at[k, 1, slot], place.device(db=db))
                         copy.start()
                         sent.append((k, copy))
+    begun = table_stage(1, table_sum(begun), inner, u, along_u)
     arrivals_b = list(sent)
     sent = []
     for k in range(kinds):
@@ -544,6 +614,7 @@
                                   place.device(da=da))
                     copy.start()
                     sent.append((k, copy))
+    begun = table_stage(2, table_sum(begun), inner, v, along_v)
     arrivals_a = list(sent)
     sent = []
     for k in range(kinds):
@@ -559,6 +630,7 @@
                               place.device(dz=dz))
                 copy.start()
                 sent.append((k, copy))
+    begun = table_stage(3, table_sum(begun), DEEP, place.z, lambda d: place.device(dz=d))
     ends = []
     for k in range(kinds):
         for kk, copy in sent:
@@ -574,11 +646,12 @@
         far.start()
         near.start()
         ends += [far, near]
+    sum_ref[...] = table_sum(begun)
     for copy in ends:
         copy.wait()
 
 
-def delivered(grads):
+def delivered(grads, table):
     owners = lax.axis_size("fsdp")
     inner, kinds = inner_of(owners), len(grads)
     anywhere = pl.BlockSpec(memory_space=pl.ANY)
@@ -590,23 +663,20 @@
     dma = pltpu.SemaphoreType.DMA
     return pl.pallas_call(
         functools.partial(deliver_kernel, inner, kinds),
-        in_specs=[anywhere] * kinds,
-        out_specs=[anywhere] * kinds,
-        out_shape=[jax.ShapeDtypeStruct(g.shape[1:], F32) for g in grads],
+        in_specs=[anywhere] * kinds + [pl.BlockSpec(memory_space=pltpu.VMEM)],
+        out_specs=[anywhere] * kinds + [pl.BlockSpec(memory_space=pltpu.VMEM)],
+        out_shape=[jax.ShapeDtypeStruct(g.shape[1:], F32) for g in grads]
+        + [jax.ShapeDtypeStruct(table.shape, F32)],
         scratch_shapes=[
             *room(owners), *room(owners), *room((inner - 1) * inner * DEEP), *room((inner - 1) * DEEP),
             *room(DEEP - 1), *[pltpu.VMEM(h, F32) for h in halves],
             dma((kinds,)), dma((kinds, 2)), dma((kinds, 2, (inner - 1) * inner * DEEP)),
             dma((kinds, 2, (inner - 1) * DEEP)), dma((kinds, 2, DEEP - 1)), dma((kinds, 3)),
+            pltpu.VMEM((4, DEEP, *table.shape), F32), dma((4, 2, DEEP)),
         ],
         compiler_params=pltpu.CompilerParams(collective_id=1, has_side_effects=True, vmem_limit_bytes=60 << 20),
         name="deliver",
-    )(*grads)
-
-
-def swap_rows(array, rows):
-    incoming = lax.ppermute(array[:rows], "win", [(0, 1), (1, 0)])
-    return jnp.concatenate([incoming, array[rows:]], axis=0)
+    )(*grads, table)
 
 
 def window_of_tokens():
@@ -630,7 +700,7 @@
 def bias_of_pairs(relative, regions):
     side, place = window_of_tokens()
     spread = jnp.asarray(spread_matrix())
-    wide = jnp.einsum("at,hts,bs->hab", spread, relative, spread, precision=HIGHEST)
+    wide = jnp.einsum("at,hts,bs->hba", spread, relative, spread, precision=HIGHEST)
     region = regions.reshape(2, WIN * WIN)
     region = jnp.concatenate(
         [jnp.roll(region[s].reshape(WIN, WIN), SHIFT, axis=0)[:, c] for s, c in ((1, slice(4, 7)), (0, slice(0, 7)), (1, slice(0, 4)))],
@@ -640,8 +710,8 @@
     same = jnp.asarray(side[:, None] == side[None, :])
     bias = jnp.where(same[None], wide + mask[None], FAR)
     return jnp.pad(
-        jnp.pad(bias, ((0, 0), (0, 0), (0, LANES - TOK)), constant_values=FAR),
-        ((0, 0), (0, PAD - TOK), (0, 0)),
+        jnp.pad(bias, ((0, 0), (0, PAD - TOK), (0, 0)), constant_values=FAR),
+        ((0, 0), (0, 0), (0, LANES - TOK)),
     )
 
 
@@ -655,50 +725,51 @@
     fc1_weight, fc1_bias, fc2_weight, fc2_bias, bias_table, regions, rel_index, cotangent,
 ):
     imgs, rows, cols, d = images.shape
-    top = SHIFT * cols
     owners = lax.axis_size("fsdp")
-    x = swap_rows(images.transpose(1, 2, 0, 3).reshape(rows * cols, imgs, d), top)
-    ct = swap_rows(cotangent.transpose(1, 2, 0, 3).reshape(rows * cols, imgs, d), top)
+    x = images.transpose(1, 2, 0, 3).reshape(rows * cols, imgs, d)
+    ct = cotangent.transpose(1, 2, 0, 3).reshape(rows * cols, imgs, d)
     vectors = (norm1_gain, norm1_bias, q_bias, v_bias, proj_bias, norm2_gain, norm2_bias, fc2_bias, fc1_bias)
     shards = (packed_row(vectors)[None], qkv_weight, proj_weight, fc1_weight, fc2_weight)
-    packed, *mats = gathered(shards)
+    packed, *mats, halo, ct_halo = gathered(shards, (x, ct))
     packed = packed[:, 0].astype(F32)
-    at, whole = 0, []
-    for v in vectors:
-        whole.append(packed[:, at : at + v.shape[0]].reshape(1, -1))
-        at += v.shape[0]
-    g1, b1, qb, vb, bp, g2, b2, b_out, b_in = whole
+    part = d // owners
+    vecs = packed[:, : 8 * part].reshape(owners, 8, part).transpose(1, 0, 2).reshape(8, d)
+    b_in = packed[:, 8 * part : 8 * part + fc1_bias.shape[0]].reshape(1, -1)
     w_qkv, w_proj, w_in, w_out = (v.reshape(owners * v.shape[1], v.shape[2]) for v in mats)
     onehot, relative = relative_parts(rel_index, bias_table)
     rel = bias_of_pairs(relative, regions)
-    qkv_bias = jnp.concatenate([qb, jnp.zeros_like(qb), vb], axis=1)
-
-    qkv, att, prob = attend(x, g1, b1, w_qkv, qkv_bias, rel)
-    flat = lambda v: v.reshape(rows * cols * imgs, d)
-    out, gm, gatt, dwp, dw1, dw2, db_in, small2 = mlp(
-        flat(x), flat(att), flat(ct), w_proj, bp, g2, b2, w_in, b_in, w_out, b_out
+
+    qkv, att, prob = attend(x, halo, vecs, w_qkv, rel)
+    flat = lambda v: v.reshape(v.shape[0] * imgs, d)
+    tall = lambda v: v.reshape(v.shape[0] // imgs, imgs, d)
+    out_top, out_rest, gm, gatt, dwp, dw1, dw2, db_in, small2 = mlp(
+        flat(x), flat(halo), flat(att), flat(ct), flat(ct_halo), w_proj, vecs, w_in, b_in, w_out
     )
-    tall = lambda v: v.reshape(rows * cols, imgs, d)
-    gin, dwq, small1, bsum, rel_sum = back(x, tall(gm), tall(gatt), qkv, prob, g1, b1, w_qkv)
-
+    swapped = lambda v: lax.ppermute(v, "win", [(0, 1), (1, 0)])
+    out_top = swapped(out_top)
+    gin_top, gin_rest, dwq, small1, bsum, rel_sum = back(x, halo, tall(gm), tall(gatt), qkv, prob, vecs, w_qkv)
+    gin_top = swapped(gin_top)
+    spread = jnp.asarray(spread_matrix())
+    pairs = jnp.einsum("at,hba,bs->tsh", spread, rel_sum[:, :TOK, :TOK], spread, precision=HIGHEST)
+    table = jnp.dot(onehot.T, pairs.reshape(WIN**4, -1), precision=HIGHEST)
+    flat_table = jnp.pad(table.reshape(-1), (0, -table.size % (8 * LANES))).reshape(-1, LANES)
     grads = (
         small1[0], small1[1], bsum[0, :d], bsum[0, 2 * d :], small2[2], small2[0], small2[1], small2[3], db_in[0],
     )
     row = packed_row([v.reshape(owners, 1, -1) for v in grads]).astype(BF)
     blocks = lambda v: v.reshape(owners, v.shape[0] // owners, v.shape[1])
-    sums, dwp, dw1, dw2, dwq = delivered((row, blocks(dwp), blocks(dw1), blocks(dw2), blocks(dwq)))
+    sums, dwp, dw1, dw2, dwq, table_sum = delivered(
+        (row, blocks(dwp), blocks(dw1), blocks(dw2), blocks(dwq)), flat_table
+    )
     at, own = 0, []
     for v in vectors:
         own.append(sums[0, at : at + v.shape[0]])
         at += v.shape[0]
     dg1, db1, dqb, dvb, dbp, dg2, db2, db_out, db_in = own
-    spread = jnp.asarray(spread_matrix())
-    pairs = jnp.einsum("at,hab,bs->tsh", spread, rel_sum[:, :TOK, :TOK], spread, precision=HIGHEST)
-    table = jnp.dot(onehot.T, pairs.reshape(WIN**4, -1), precision=HIGHEST)
-    table = lax.psum(table, ("fsdp", "win"))
-    back_to_images = lambda v: swap_rows(v, top).reshape(rows, cols, imgs, d).transpose(2, 0, 1, 3)
+    table = table_sum.reshape(-1)[: table.size].reshape(table.shape)
+    joined = lambda top, rest: jnp.concatenate([top, rest], axis=0).reshape(rows, cols, imgs, d).transpose(2, 0, 1, 3)
     return (
-        back_to_images(tall(out)), back_to_images(gin), dg1, db1, dwq, dqb, dvb, dwp, dbp, dg2, db2, dw1, db_in, dw2,
+        joined(tall(out_top), tall(out_rest)), joined(gin_top, gin_rest), dg1, db1, dwq, dqb, dvb, dwp, dbp, dg2, db2, dw1, db_in, dw2,
         db_out, table,
     )
 

time: 474 us -> 316 us (0.67)
  Pallas kernels: 380 us -> 275 us
  blocking collectives: 38.8 us -> 0 us
  local copies, waits for them, and re-layouts: 29.9 us -> 20.6 us
  other arithmetic: 17.5 us -> 10.2 us
    pallas_call x3, Pallas kernels: 277 us -> 185 us  [the longest x1 83.7 us: mlp(): pl.pallas_call(functools.partial(mlp_kernel, tops), grid=(rows // tile,),...]
    psum x1 -> x0, blocking collectives: 38.8 us -> none  [per_device(): table = lax.psum(table, ('fsdp', 'win'))]
    pallas_call x1, Pallas kernels: 55 us -> 39.6 us  [attend(): pl.pallas_call(attend_kernel, grid=(imgs // NB,), in_specs=[pl.BlockSpec(...]
    slice x10 -> x4, local copies, waits for them, and re-layouts: 15.2 us -> 1.4 us  [the longest x2 0.8 us: per_device(): table = table_sum.reshape(-1)[:table.size].reshape(table.shape)]
    concatenate x5 -> x2, other arithmetic: 16.3 us -> 7.54 us  [per_device(): jnp.concatenate([top, rest], axis=0).reshape(rows, cols, imgs, d)]
    concatenate x2, local copies, waits for them, and re-layouts: 0.34 us -> 6.34 us  [packed_row(): row = jnp.concatenate(parts, axis=-1)]
  transfers between devices with their start and end apart: 4 -> 2, of which waited for: 0 -> 0; matrix products, arithmetic and copies ran while one was open for 7% -> 6% of each run, Pallas kernels for 31% -> 16%
where the time goes in v3:
time: 316 us
  Pallas kernels  275 us (87%)
  local copies, waits for them, and re-layouts  20.6 us (7%)
  other arithmetic  10.2 us (3%)
  matrix products  8.45 us (3%)
    pallas_call x1, Pallas kernels, mlp(): pl.pallas_call(functools.partial(mlp_kernel, tops), grid=(rows // tile,),...  83.7 us
    pallas_call x1, Pallas kernels, back(): pl.pallas_call(back_kernel, grid=(imgs // NB,), in_specs=[tok, pl.BlockSp...  57.3 us
    pallas_call x1, Pallas kernels, delivered(): pl.pallas_call(functools.partial(deliver_kernel, inner, kinds), in_specs=...  50.7 us
    pallas_call x1, Pallas kernels, gathered(): pl.pallas_call(functools.partial(gather_kernel, inner, kinds, fields), in...  43.7 us
    pallas_call x1, Pallas kernels, attend(): pl.pallas_call(attend_kernel, grid=(imgs // NB,), in_specs=[pl.BlockSpec(...  39.6 us
    concatenate x2, other arithmetic, per_device(): jnp.concatenate([top, rest], axis=0).reshape(rows, cols, imgs, d)  7.54 us
    concatenate x2, local copies, waits for them, and re-layouts, packed_row(): row = jnp.concatenate(parts, axis=-1)  6.34 us
  transfers between devices with their start and end apart: 2, of which 0 were waited for; matrix products, arithmetic and copies ran while one was open for 6% of the time, Pallas kernels for 16%

profile of v3, /device:TPU:0, one launch (start us, length us, event | category | flops | bytes accessed | tf_op | source)
XLA Modules:
  0.0 315.6 jit_solution(3012455454827968788)
XLA Ops:
  0.6 0.0 copy-start
  0.7 0.8 slice_reduce_fusion.8
  1.4 0.8 slice_reduce_fusion.9
  2.3 6.1 %concatenate.24 = bf16[384]{0:T(512)(128)(2,1)S(1)} concatenate(bf16[32]{0:T(256)(128)(2,1)} %param.22, bf16[32]{0:T(256)(128)(2,1)} %param.23, bf16[32]{0:T(256)(128)(2,1)} %param.25, bf16[32]{0:T(256)(128)(2,1)} %param.26, bf16[32]{0:T(256)(128)(2,1)} %param.28, bf16[32]{0:T(256)(128)(2,1)} %param.29, bf16[32]{0:T(256)(128)(2,1)} %param.30, bf16[32]{0:T(256)(128)(2,1)} %param.34, ...), dimensions={0} | concatenate | bytes 1536 | tf_op jit(solution)/shard_map/concatenate | solution.py:719
  8.4 0.6 broadcast_in_dim.26.refs_0_
  9.0 43.7 %gather.1 = (bf16[16,1,512]{2,1,0:T(2,128)(2,1)}, bf16[16,32,1536]{2,1,0:T(8,128)(2,1)}, bf16[16,32,512]{2,1,0:T(8,128)(2,1)}, bf16[16,32,2048]{2,1,0:T(8,128)(2...) custom-call(bf16[1,512]{1,0:T(2,128)(2,1)} %broadcast_in_dim.26.refs_0_, ...), custom_call_target="tpu_custom_call" | custom-call | tf_op jit(solution)/shard_map/gather/pallas_call | solution.py:516
  52.6 0.8 copy.58
  53.4 0.6 slice.150
  54.0 0.1 slice.124
  54.1 0.1 slice.126
  54.2 0.1 slice.119
  54.3 0.1 slice.121
  54.4 0.1 slice.122
  54.4 0.1 pad_add_fusion.1
  54.5 0.1 eq.38
  54.6 0.1 eq.34
  54.7 0.1 compare_select_fusion
  54.8 0.0 copy-done
  54.8 1.2 fusion.1
  56.1 0.2 reshape.168
  56.3 0.9 fusion.10
  57.2 0.9 fusion.3
  58.1 1.0 pad_select_fusion.rel_ref
  59.1 0.1 reshape.165
  59.2 0.7 reshape.166.vec_ref
  59.9 39.6 %attend.1 = (bf16[32,12,112,128]{3,2,1,0:T(8,128)(2,1)}, bf16[98,32,512]{2,1,0:T(8,128)(2,1)}, bf16[32,16,112,112]{3,2,1,0:T(8,128)(2,1)}) custom-call(bf16[98,32,512]{2,1,0:T(8,128)(2,1)} %bitcast.86, bf16[42,32,512]{2,1,0:T(8,128)(2,1)} %get-tuple-element.47.halo_ref, f32[8,512]{1,0:T(8,128)} %reshape.166.vec_ref, bf16[512,1536]{1,0:T(8,128)(2,1)} %bitcast.94, ...), custom_call_target="tpu_custom_call" | custom-call | tf_op jit(solution)/shard_map/attend/pallas_call | solution.py:138
  99.5 83.7 %mlp.1 = (bf16[1344,512]{1,0:T(8,128)(2,1)}, bf16[1792,512]{1,0:T(8,128)(2,1)}, f32[3136,512]{1,0:T(8,128)}, bf16[3136,512]{1,0:T(8,128)(2,1)}, bf16[512,512]{1,...) custom-call(bf16[3136,512]{1,0:T(8,128)(2,1)} %bitcast.87, ...), custom_call_target="tpu_custom_call" | custom-call | tf_op jit(solution)/shard_map/mlp/pallas_call | solution.py:246
  183.2 0.0 copy-start.9
  183.2 0.0 copy-start.11
  183.2 57.3 %back.1 = (f32[42,32,512]{2,1,0:T(8,128)}, f32[56,32,512]{2,1,0:T(8,128)}, bf16[512,1536]{1,0:T(8,128)(2,1)}, f32[8,512]{1,0:T(8,128)}, f32[1,1536]{1,0:T(1,128)}, /*index=5*/f32[16,112,112]{2,1,0:T(8,128)}) custom-call(bf16[98,32,512]{2,1,0:T(8,128)(2,1)} %bitcast.88, bf16[42,32,512]{2,1,0:T(8,128)(2,1)} %get-tuple-element.47.halo_ref, ...), custom_call_target="tpu_custom_call" | custom-call | tf_op jit(solution)/shard_map/back/pallas_call | solution.py:347
  240.5 0.5 collective-permute-start.1
  241.0 0.1 collective-permute-start
  241.1 0.7 convert.38
  241.8 0.1 reshape_squeeze.51
  241.9 0.1 reshape_squeeze.50
  242.0 0.7 convert.37
  242.7 0.1 reshape_squeeze.49
  242.8 0.1 reshape_squeeze.48
  243.0 0.1 reshape_squeeze.55
  243.0 0.1 reshape_squeeze.54
  243.1 0.1 reshape_squeeze.53
  243.2 0.1 reshape_squeeze.52
  243.3 0.2 concatenate.30
  243.5 0.6 pad.24.refs_0_
  244.2 3.0 fusion.8
  247.2 0.5 convolution_bitcast_fusion.1
  247.7 0.2 reshape.185
  247.9 1.9 fusion.4
  249.8 0.1 reshape.186
  249.9 0.6 pad_bitcast_fusion.refs_5_
  250.5 50.7 %deliver.1 = (f32[1,512]{1,0:T(1,128)}, f32[32,512]{1,0:T(8,128)}, f32[32,2048]{1,0:T(8,128)}, f32[128,512]{1,0:T(8,128)}, f32[32,1536]{1,0:T(8,128)}, /*index=5*/f32[24,128]{1,0:T(8,128)}) custom-call(bf16[16,1,512]{2,1,0:T(2,128)(2,1)} %pad.24.refs_0_, bf16[16,32,512]{2,1,0:T(8,128)(2,1)} %bitcast.107, bf16[16,32,2048]{2,1,0:T(8,128)(2,1)} %bitcast.101, ...), custom_call_target="tpu_custom_call" | custom-call | tf_op jit(solution)/shard_map/deliver/pallas_call | solution.py:664
  301.2 0.8 slice.147
  302.0 0.7 copy.51
  302.7 1.2 slice_bitcast_fusion.1
  303.9 1.4 slice_bitcast_fusion
  305.3 0.0 collective-permute-done
  305.3 4.0 %pad_maximum_fusion.1 = bf16[98,32,512]{2,1,0:T(8,128)(2,1)} fusion(bf16[56,32,512]{2,1,0:T(8,128)(2,1)} %bitcast.103, bf16[42,32,512]{2,1,0:T(8,128)(2,1)} %bitcast.19), kind=kLoop, calls=%fused_computation.1 | loop fusion | flops 1605632 | bytes 6422528 | tf_op jit(solution)/shard_map/concatenate | solution.py:770
  309.3 0.0 collective-permute-done.1
  309.4 0.0 copy-start.1
  309.4 3.5 %pad_maximum_fusion = f32[98,32,512]{2,1,0:T(8,128)} fusion(f32[56,32,512]{2,1,0:T(8,128)S(1)} %copy-done.2, f32[42,32,512]{2,1,0:T(8,128)S(1)} %collective-permute-done.1), kind=kLoop, calls=%fused_computation | loop fusion | flops 1605632 | bytes 12845056 | tf_op jit(solution)/shard_map/concatenate | solution.py:770
  312.9 0.7 copy.63
  313.6 0.6 copy.64
  314.2 0.7 copy.65
  314.9 0.7 copy.66
  (29 shorter events, 0.2 us)
Async XLA Ops:
  0.6 54.2 %copy-start = (f32[169,16]{0,1:T(8,128)S(1)}, f32[169,16]{0,1:T(8,128)}, u32[]{:S(2)}) copy-start(f32[169,16]{0,1:T(8,128)} %param.35) | copy-start | bytes 32452
  9.0 45.6 %copy-start.8 = (s32[49,49]{1,0:T(8,128)S(1)}, s32[49,49]{1,0:T(8,128)}, u32[]{:S(2)}) copy-start(s32[49,49]{1,0:T(8,128)} %param.37) | copy-start | bytes 28816
  9.0 47.3 %copy-start.3 = (f32[98,49,1]{0,1,2:T(8,128)S(1)}, f32[98,49,1]{0,1,2:T(8,128)}, u32[]{:S(2)}) copy-start(f32[98,49,1]{0,1,2:T(8,128)} %constant.30) | copy-start | bytes 57628
  9.0 48.2 %copy-start.10 = (pred[98,98]{1,0:T(8,128)(4,1)S(1)}, pred[98,98]{1,0:T(8,128)(4,1)}, u32[]{:S(2)}) copy-start(pred[98,98]{1,0:T(8,128)(4,1)} %constant.16.clone) | copy-start | bytes 28816
  183.2 59.7 %copy-start.9 = (f32[8,512]{1,0:T(8,128)S(1)}, f32[8,512]{1,0:T(8,128)}, u32[]{:S(2)}) copy-start(f32[8,512]{1,0:T(8,128)} %get-tuple-element.65) | copy-start | bytes 49156
  183.2 59.7 %copy-start.11 = (f32[1,2048]{1,0:T(1,128)S(1)}, f32[1,2048]{1,0:T(1,128)}, u32[]{:S(2)}) copy-start(f32[1,2048]{1,0:T(1,128)} %get-tuple-element.66) | copy-start | bytes 24580
  240.5 68.8 %collective-permute-start.1 = (f32[42,32,512]{2,1,0:T(8,128)}, f32[42,32,512]{2,1,0:T(8,128)S(1)}, u32[]{:S(2)}, u32[]{:S(2)}) collective-permute-start(f32[42,32,512]{2,1,0:T(8,128)} %get-tuple-element.61), channel_id=1, source_target_pairs={{0,1},{1,0},{2,3},{3,2},{4,5},{5,4},{6,7},{7,6},{8,9},{9,8},{10,11... | collective-permute-start | bytes 8257544 | tf_op jit(solution)/shard_map/ppermute | solution.py:748
  241.0 64.3 %collective-permute-start = (bf16[1344,512]{1,0:T(8,128)(2,1)}, bf16[1344,512]{1,0:T(8,128)(2,1)}, u32[]{:S(2)}, u32[]{:S(2)}) collective-permute-start(bf16[1344,512]{1,0:T(8,128)(2,1)} %get-tuple-element.55), channel_id=1, source_target_pairs={{0,1},{1,0},{2,3},{3,2},{4,5},{5,4},{6,7},{7,6},{8,9},{9,8},{10,11... | collective-permute-start | bytes 4128776 | tf_op jit(solution)/shard_map/ppermute | solution.py:748
  305.3 4.0 %copy-start.2 = (f32[56,32,512]{2,1,0:T(8,128)S(1)}, f32[56,32,512]{2,1,0:T(8,128)}, u32[]{:S(2)}) copy-start(f32[56,32,512]{2,1,0:T(8,128)} %get-tuple-element.62) | copy-start | bytes 11010052
  309.3 3.6 %copy-start.6 = (f32[32,1536]{1,0:T(8,128)S(1)}, f32[32,1536]{1,0:T(8,128)}, u32[]{:S(2)}) copy-start(f32[32,1536]{1,0:T(8,128)} %get-tuple-element.134) | copy-start | bytes 589828
  309.3 4.3 %copy-start.7 = (f32[32,512]{1,0:T(8,128)S(1)}, f32[32,512]{1,0:T(8,128)}, u32[]{:S(2)}) copy-start(f32[32,512]{1,0:T(8,128)} %get-tuple-element.137) | copy-start | bytes 196612
  309.3 4.9 %copy-start.5 = (f32[32,2048]{1,0:T(8,128)S(1)}, f32[32,2048]{1,0:T(8,128)}, u32[]{:S(2)}) copy-start(f32[32,2048]{1,0:T(8,128)} %get-tuple-element.141) | copy-start | bytes 786436
  309.3 5.6 %copy-start.4 = (f32[128,512]{1,0:T(8,128)S(1)}, f32[128,512]{1,0:T(8,128)}, u32[]{:S(2)}) copy-start(f32[128,512]{1,0:T(8,128)} %get-tuple-element.143) | copy-start | bytes 786436
  309.4 6.3 %copy-start.1 = (f32[169,16]{0,1:T(8,128)S(1)}, f32[169,16]{0,1:T(8,128)}, u32[]{:S(2)}) copy-start(f32[169,16]{0,1:T(8,128)} %param.35) | copy-start | bytes 32452

commit v4 on v3

--- a/solution.py
+++ b/solution.py
@@ -84,7 +84,26 @@
     return out
 
 
-def attend_kernel(x_ref, halo_ref, vec_ref, w_ref, rel_ref, qkv_ref, att_ref, prob_ref, wide, joined):
+def at_step(step, action):
+    @pl.when(pl.program_id(0) == step)
+    def _():
+        action()
+
+
+def attend_kernel(inner, kinds, fields, x_ref, halo_ref, vec_ref, w_ref, rel_ref, *refs):
+    ins, maps = refs[:kinds], refs[kinds : kinds + fields]
+    qkv_ref, att_ref, prob_ref = refs[kinds + fields : kinds + fields + 3]
+    outs, halos = refs[kinds + fields + 3 : 2 * kinds + fields + 3], refs[2 * kinds + fields + 3 : 2 * (kinds + fields) + 3]
+    wide, joined, *sems = refs[2 * (kinds + fields) + 3 :]
+    moves = Spread(inner, ins, maps, outs, halos, *sems)
+
+    def begin():
+        meet(Place(inner))
+        moves.run(0)
+
+    at_step(0, begin)
+    for stage in (1, 2, 3):
+        at_step(stage, functools.partial(moves.run, stage))
     d = x_ref.shape[-1]
     n, _ = normalized(shifted_rows(x_ref, halo_ref))
     normed = (n * vec_ref[0:1] + vec_ref[1:2]).astype(BF)
@@ -129,37 +148,44 @@
     lax.fori_loop(0, NB, one, 0)
     for g in range(per):
         att_ref[:, :, g * LANES : (g + 1) * LANES] = joined[g, : TOK * NB, :].astype(BF).reshape(TOK, NB, LANES)
-
-
-def attend(x, halo, vecs, w, rel):
+    at_step(3, moves.finish)
+
+
+def attend(x, halo, vecs, w, rel, shards, maps):
     _, imgs, d = x.shape
+    owners = lax.axis_size("fsdp")
+    inner, kinds, fields = inner_of(owners), len(shards), len(maps)
+    anywhere = [pl.BlockSpec(memory_space=pl.ANY)] * (kinds + fields)
     full = lambda *shape: pl.BlockSpec(shape, lambda i: (0,) * len(shape), pipeline_mode=pl.Buffered(1))
     per = d // LANES
     return pl.pallas_call(
-        attend_kernel,
+        functools.partial(attend_kernel, inner, kinds, fields),
         grid=(imgs // NB,),
         in_specs=[
             pl.BlockSpec((TOK, NB, d), lambda i: (0, i, 0)),
             pl.BlockSpec((TOP, NB, d), lambda i: (0, i, 0)),
-            full(8, d), full(d, 3 * d), full(HEADS, PAD, LANES),
+            full(8, d), full(d, 3 * d), full(HEADS, PAD, LANES), *anywhere,
         ],
         out_specs=[
             pl.BlockSpec((NB, 3 * per, PAD, LANES), lambda i: (i, 0, 0, 0)),
             pl.BlockSpec((TOK, NB, d), lambda i: (0, i, 0)),
             pl.BlockSpec((NB, HEADS, PAD, PAD), lambda i: (i, 0, 0, 0)),
+            *anywhere,
         ],
         out_shape=[
             jax.ShapeDtypeStruct((imgs, 3 * per, PAD, LANES), BF),
             jax.ShapeDtypeStruct((TOK, imgs, d), BF),
             jax.ShapeDtypeStruct((imgs, HEADS, PAD, PAD), BF),
+            *spread_shapes(owners, shards, maps),
         ],
         scratch_shapes=[
             pltpu.VMEM((3 * per, PAD * NB, LANES), F32),
             pltpu.VMEM((per, PAD * NB, LANES), F32),
-        ],
-        compiler_params=pltpu.CompilerParams(vmem_limit_bytes=60 << 20),
+            *spread_scratch(owners, kinds, fields),
+        ],
+        compiler_params=pltpu.CompilerParams(collective_id=2, has_side_effects=True, vmem_limit_bytes=60 << 20),
         name="attend",
-    )(x, halo, vecs, w, rel)
+    )(x, halo, vecs, w, rel, *shards, *maps)
 
 
 def mlp_kernel(tops, x_ref, halo_ref, att_ref, ct_ref, ct_halo_ref, wp_ref, vec_ref, w1_ref, b1_ref, w2_ref,
@@ -268,8 +294,19 @@
     )(x, halo, att, ct, ct_halo, wp, vecs, w1, b1, w2)
 
 
-def back_kernel(x_ref, halo_ref, gm_ref, gatt_ref, qkv_ref, prob_ref, vec_ref, w_ref,
-                top_ref, rest_ref, dw_ref, small_ref, bsum_ref, rel_ref, wide, grads, aw, asm, abs_):
+def back_kernel(inner, kinds, x_ref, halo_ref, gm_ref, gatt_ref, qkv_ref, prob_ref, vec_ref, w_ref, *refs):
+    ins, (top_ref, rest_ref, dw_ref, small_ref, bsum_ref, rel_ref) = refs[:kinds], refs[kinds : kinds + 6]
+    outs, (wide, grads, aw, asm, abs_), room = refs[kinds + 6 : 2 * kinds + 6], refs[2 * kinds + 6 : 2 * kinds + 11], refs[2 * kinds + 11 :]
+    moves = Delivery(inner, ins, outs, room)
+
+    def begin():
+        meet(Place(inner))
+        moves.start()
+
+    at_step(0, begin)
+    at_step(1, moves.pass_b)
+    at_step(2, moves.pass_a)
+    at_step(3, moves.pass_z)
     step = pl.program_id(0)
     d = x_ref.shape[-1]
     per = d // LANES
@@ -332,6 +369,12 @@
     top_ref[...] = gin[:TOP]
     rest_ref[...] = gin[TOP:]
 
+    def end():
+        moves.hand_over()
+        moves.finish()
+
+    at_step(3, end)
+
     @pl.when(step == pl.num_programs(0) - 1)
     def _():
         dw_ref[...] = aw[...].astype(BF)
@@ -339,21 +382,23 @@
         bsum_ref[...] = abs_[...]
 
 
-def back(x, halo, gm, gatt, qkv, prob, vecs, w):
+def back(x, halo, gm, gatt, qkv, prob, vecs, w, grads):
     _, imgs, d = x.shape
+    owners, kinds = lax.axis_size("fsdp"), len(grads)
+    anywhere = [pl.BlockSpec(memory_space=pl.ANY)] * kinds
     per = d // LANES
     full = lambda *shape: pl.BlockSpec(shape, lambda i: (0,) * len(shape), pipeline_mode=pl.Buffered(1))
     tok = pl.BlockSpec((TOK, NB, d), lambda i: (0, i, 0))
     return pl.pallas_call(
-        back_kernel,
+        functools.partial(back_kernel, inner_of(owners), kinds),
         grid=(imgs // NB,),
         in_specs=[
             tok, pl.BlockSpec((TOP, NB, d), lambda i: (0, i, 0)), tok, tok,
             pl.BlockSpec((NB, 3 * per, PAD, LANES), lambda i: (i, 0, 0, 0)),
             pl.BlockSpec((NB, HEADS, PAD, PAD), lambda i: (i, 0, 0, 0)),
-            full(8, d), full(d, 3 * d),
-        ],
-        out_specs=[pl.BlockSpec((TOP, NB, d), lambda i: (0, i, 0)), pl.BlockSpec((TOK - TOP, NB, d), lambda i: (0, i, 0)), full(d, 3 * d), full(8, d), full(1, 3 * d), full(HEADS, PAD, PAD)],
+            full(8, d), full(d, 3 * d), *anywhere,
+        ],
+        out_specs=[pl.BlockSpec((TOP, NB, d), lambda i: (0, i, 0)), pl.BlockSpec((TOK - TOP, NB, d), lambda i: (0, i, 0)), full(d, 3 * d), full(8, d), full(1, 3 * d), full(HEADS, PAD, PAD), *anywhere],
         out_shape=[
             jax.ShapeDtypeStruct((TOP, imgs, d), F32),
             jax.ShapeDtypeStruct((TOK - TOP, imgs, d), F32),
@@ -361,6 +406,7 @@
             jax.ShapeDtypeStruct((8, d), F32),
             jax.ShapeDtypeStruct((1, 3 * d), F32),
             jax.ShapeDtypeStruct((HEADS, PAD, PAD), F32),
+            *[jax.ShapeDtypeStruct(g.shape[1:], F32) for g in grads],
         ],
         scratch_shapes=[
             pltpu.VMEM((per, PAD * NB, LANES), F32),
@@ -368,10 +414,11 @@
             pltpu.VMEM((d, 3 * d), F32),
             pltpu.VMEM((8, d), F32),
             pltpu.VMEM((1, 3 * d), F32),
-        ],
-        compiler_params=pltpu.CompilerParams(vmem_limit_bytes=60 << 20),
+            *delivery_scratch(owners, grads),
+        ],
+        compiler_params=pltpu.CompilerParams(collective_id=3, has_side_effects=True, vmem_limit_bytes=62 << 20),
         name="back",
-    )(x, halo, gm, gatt, qkv, prob, vecs, w)
+    )(x, halo, gm, gatt, qkv, prob, vecs, w, *grads)
 
 
 DEEP = 4
@@ -423,85 +470,99 @@
     )
 
 
+class Spread:
+    def __init__(self, inner, ins, maps, outs, halos, send_sem, recv_sem, own_sem, halo_sem):
+        self.inner, self.ins, self.maps, self.outs, self.halos = inner, ins, maps, outs, halos
+        self.send_sem, self.recv_sem, self.own_sem, self.halo_sem = send_sem, recv_sem, own_sem, halo_sem
+        steps = [("a", d) for d in range(1, inner)], [("b", d) for d in range(1, inner)]
+        order_z, mate = (1, 3, 2), [("m", 0)]
+        plan = [[((0, 0, 0), [("z", d) for d in order_z] + steps[0] + steps[1])]]
+        plan.append([((dz, 0, 0), steps[0] + steps[1] + mate) for dz in order_z])
+        plan.append([((dz, da, 0), steps[1] + mate) for da in range(1, inner) for dz in (0,) + order_z])
+        plan.append([((dz, da, db), mate) for db in range(1, inner) for da in range(inner) for dz in (0,) + order_z])
+        self.plan, count = [], 0
+        for stage in plan:
+            rows = []
+            for block, targets in stage:
+                rows.append((block, [(t, count + i) for i, t in enumerate(targets)]))
+                count += len(targets)
+            self.plan.append(rows)
+
+    def piece(self, k, block, core):
+        half = self.outs[k].shape[-1] // 2
+        return self.outs[k].at[block, :, pl.ds(pl.multiple_of(core * half, LANES), half)]
+
+    def copy(self, place, k, stage, block, target, index):
+        (axis, d), where = target, place.at(*block)
+        device = {"z": place.device(dz=d), "a": place.device(da=d), "b": place.device(db=d), "m": place.partner()}[axis]
+        half = self.outs[k].shape[-1] // 2
+        src = self.piece(k, where, place.core)
+        if stage == 0:
+            src = self.ins[k].at[:, pl.ds(pl.multiple_of(place.core * half, LANES), half)]
+        return remote(src, self.piece(k, where, place.core), self.send_sem.at[k, index],
+                      self.recv_sem.at[k, place.core, where], device)
+
+    def arrive(self, place, k, block, core):
+        at = self.piece(k, place.at(*block), core)
+        remote(at, at, self.send_sem.at[k, 0], self.recv_sem.at[k, core, place.at(*block)], place.partner()).wait_recv()
+
+    def local(self, place):
+        copies = [remote(self.maps[f].at[:TOP], self.halos[f], self.halo_sem.at[f, 0], self.halo_sem.at[f, 1],
+                         place.partner()) for f in range(len(self.maps))]
+        copies += [pltpu.make_async_copy(self.ins[k], self.outs[k].at[place.at()], self.own_sem.at[k])
+                   for k in range(len(self.ins))]
+        return copies
+
+    def run(self, stage, kinds=None):
+        place = Place(self.inner)
+        for k in range(len(self.ins)) if kinds is None else kinds:
+            for block, targets in self.plan[stage]:
+                if stage:
+                    self.arrive(place, k, block, place.core)
+                for target, index in targets:
+                    self.copy(place, k, stage, block, target, index).start()
+        if stage == 0:
+            for copy in self.local(place):
+                copy.start()
+
+    def finish(self):
+        place = Place(self.inner)
+        for k in range(len(self.ins)):
+            for stage in self.plan[1:]:
+                for block, _ in stage:
+                    self.arrive(place, k, block, place.mate)
+            for stage, rows in enumerate(self.plan):
+                for block, targets in rows:
+                    for target, index in targets:
+                        self.copy(place, k, stage, block, target, index).wait_send()
+        for copy in self.local(place):
+            copy.wait()
+
+
+def spread_scratch(owners, kinds, fields):
+    inner = inner_of(owners)
+    sends = 3 + 2 * (inner - 1) + 3 * (2 * inner - 1) + 2 * DEEP * (inner - 1) * inner
+    dma = pltpu.SemaphoreType.DMA
+    return [dma((kinds, sends)), dma((kinds, 2, owners)), dma((kinds,)), dma((fields, 2))]
+
+
+def spread_shapes(owners, shards, maps):
+    return [jax.ShapeDtypeStruct((owners, *s.shape), s.dtype) for s in shards] + [
+        jax.ShapeDtypeStruct((TOP, *m.shape[1:]), m.dtype) for m in maps
+    ]
+
+
 def gather_kernel(inner, kinds, fields, *refs):
     ins, maps = refs[:kinds], refs[kinds : kinds + fields]
     outs, halos = refs[kinds + fields : 2 * kinds + fields], refs[2 * kinds + fields : 2 * (kinds + fields)]
-    send_sem, recv_sem, own_sem, halo_sem = refs[2 * (kinds + fields) :]
-    place = Place(inner)
-    meet(place)
-
-    def piece(k, block, core):
-        half = outs[k].shape[-1] // 2
-        return outs[k].at[block, :, pl.ds(pl.multiple_of(core * half, LANES), half)]
-
-    def mine(k):
-        half = outs[k].shape[-1] // 2
-        return ins[k].at[:, pl.ds(pl.multiple_of(place.core * half, LANES), half)]
-
-    sent = [[] for _ in range(kinds)]
-
-    def send(k, src, block, device):
-        copy = remote(src, piece(k, block, place.core), send_sem.at[k, len(sent[k])],
-                      recv_sem.at[k, place.core, block], device)
-        copy.start()
-        sent[k].append(copy)
-
-    def arrive(k, core, block):
-        at = piece(k, block, core)
-        remote(at, at, send_sem.at[k, 0], recv_sem.at[k, core, block], place.partner()).wait_recv()
-
-    steps = range(1, inner)
-    order_z = (1, 3, 2)
-    own = []
+    meet(Place(inner))
+    moves = Spread(inner, ins, maps, outs, halos, *refs[2 * (kinds + fields) :])
+    moves.run(0)
     for k in range(kinds):
-        for d in order_z:
-            send(k, mine(k), place.at(), place.device(dz=d))
-        for d in steps:
-            send(k, mine(k), place.at(), place.device(da=d))
-        for d in steps:
-            send(k, mine(k), place.at(), place.device(db=d))
-    swaps = [remote(maps[f].at[:TOP], halos[f], halo_sem.at[f, 0], halo_sem.at[f, 1], place.partner())
-             for f in range(fields)]
-    for copy in swaps:
-        copy.start()
-    for k in range(kinds):
-        copy = pltpu.make_async_copy(ins[k], outs[k].at[place.at()], own_sem.at[k])
-        copy.start()
-        own.append(copy)
-
-    def pass_on(k, block, along_a, along_b):
-        arrive(k, place.core, block)
-        src = piece(k, block, place.core)
-        if along_a:
-            for d in steps:
-                send(k, src, block, place.device(da=d))
-        if along_b:
-            for d in steps:
-                send(k, src, block, place.device(db=d))
-        send(k, src, block, place.partner())
-
-    for k in range(kinds):
-        for dz in order_z:
-            pass_on(k, place.at(dz=dz), True, True)
-        for da in steps:
-            for dz in (0,) + order_z:
-                pass_on(k, place.at(dz=dz, da=da), False, True)
-    for k in range(kinds):
-        for db in steps:
-            for da in range(inner):
-                for dz in (0,) + order_z:
-                    pass_on(k, place.at(dz=dz, da=da, db=db), False, False)
-    for k in range(kinds):
-        for db in range(inner):
-            for da in range(inner):
-                for dz in range(DEEP):
-                    if db or da or dz:
-                        arrive(k, place.mate, place.at(dz, da, db))
-        own[k].wait()
-        for copy in sent[k]:
-            copy.wait_send()
-    for copy in swaps:
-        copy.wait()
+        moves.run(1, (k,))
+        moves.run(2, (k,))
+    moves.run(3)
+    moves.finish()
 
 
 def inner_of(owners):
@@ -511,38 +572,147 @@
 def gathered(shards, maps):
     owners = lax.axis_size("fsdp")
     inner, kinds, fields = inner_of(owners), len(shards), len(maps)
-    sends = (DEEP - 1) + 2 * (inner - 1) + 1 + (DEEP - 1) * (2 * inner - 1) + DEEP * (inner - 1) * inner + DEEP * inner * (inner - 1)
     anywhere = pl.BlockSpec(memory_space=pl.ANY)
     return pl.pallas_call(
         functools.partial(gather_kernel, inner, kinds, fields),
         in_specs=[anywhere] * (kinds + fields),
         out_specs=[anywhere] * (kinds + fields),
-        out_shape=[jax.ShapeDtypeStruct((owners, *s.shape), s.dtype) for s in shards]
-        + [jax.ShapeDtypeStruct((TOP, *m.shape[1:]), m.dtype) for m in maps],
-        scratch_shapes=[
-            pltpu.SemaphoreType.DMA((kinds, sends)),
-            pltpu.SemaphoreType.DMA((kinds, 2, owners)),
-            pltpu.SemaphoreType.DMA((kinds,)),
-            pltpu.SemaphoreType.DMA((fields, 2)),
-        ],
+        out_shape=spread_shapes(owners, shards, maps),
+        scratch_shapes=spread_scratch(owners, kinds, fields),
         compiler_params=pltpu.CompilerParams(collective_id=0, has_side_effects=True),
         name="gather",
     )(*shards, *maps)
 
 
+class Delivery:
+    def __init__(self, inner, ins, outs, refs):
+        self.inner, self.ins, self.outs, kinds = inner, ins, outs, len(ins)
+        self.kinds = range(kinds)
+        self.own, self.from_mate, self.from_b, self.from_a, self.from_z, self.final = (
+            refs[i * kinds : (i + 1) * kinds] for i in range(6)
+        )
+        self.load_sem, self.mate_sem, self.b_sem, self.a_sem, self.z_sem, self.end_sem = refs[6 * kinds : 6 * kinds + 6]
+        self.steps = range(1, inner)
+
+    def columns(self, k, core):
+        half = self.outs[k].shape[-1] // 2
+        return pl.ds(pl.multiple_of(core * half, LANES), half)
+
+    def add(self, k, block, other):
+        self.own[k][block] = (self.own[k][block].astype(F32) + other[...].astype(F32)).astype(BF)
+
+    def loads(self, place, k):
+        return (
+            remote(self.ins[k].at[:, :, self.columns(k, place.mate)], self.from_mate[k], self.mate_sem.at[k, 0],
+                   self.mate_sem.at[k, 1], place.partner()),
+            pltpu.make_async_copy(self.ins[k].at[:, :, self.columns(k, place.core)], self.own[k], self.load_sem.at[k]),
+        )
+
+    def to_b(self, place, k, dz, da, db):
+        slot = (db - 1) * self.inner * DEEP + da * DEEP + dz
+        return remote(self.own[k].at[place.at(dz, da, db)], self.from_b[k].at[slot], self.b_sem.at[k, 0, slot],
+                      self.b_sem.at[k, 1, slot], place.device(db=db))
+
+    def to_a(self, place, k, dz, da):
+        slot = (da - 1) * DEEP + dz
+        return remote(self.own[k].at[place.at(dz, da)], self.from_a[k].at[slot], self.a_sem.at[k, 0, slot],
+                      self.a_sem.at[k, 1, slot], place.device(da=da))
+
+    def to_z(self, place, k, dz):
+        return remote(self.own[k].at[place.at(dz)], self.from_z[k].at[dz - 1], self.z_sem.at[k, 0, dz - 1],
+                      self.z_sem.at[k, 1, dz - 1], place.device(dz=dz))
+
+    def ends(self, place, k):
+        there = self.outs[k].at[:, self.columns(k, place.core)]
+        return (remote(self.final[k], there, self.end_sem.at[k, 0], self.end_sem.at[k, 1], place.partner()),
+                pltpu.make_async_copy(self.final[k], there, self.end_sem.at[k, 2]))
+
+    def start(self):
+        place = Place(self.inner)
+        for k in self.kinds:
+            for copy in self.loads(place, k):
+                copy.start()
+
+    def pass_b(self):
+        place = Place(self.inner)
+        for k in self.kinds:
+            for copy in self.loads(place, k):
+                copy.wait()
+            for db in tuple(self.steps) + (0,):
+                for da in range(self.inner):
+                    for dz in range(DEEP):
+                        block = place.at(dz, da, db)
+                        self.add(k, block, self.from_mate[k].at[block])
+                        if db:
+                            self.to_b(place, k, dz, da, db).start()
+
+    def pass_a(self):
+        place = Place(self.inner)
+        for k in self.kinds:
+            for db in self.steps:
+                for da in range(self.inner):
+                    for dz in range(DEEP):
+                        self.to_b(place, k, dz, da, db).wait()
+            for da in tuple(self.steps) + (0,):
+                for dz in range(DEEP):
+                    for db in self.steps:
+                        self.add(k, place.at(dz, da), self.from_b[k].at[(db - 1) * self.inner * DEEP + da * DEEP + dz])
+                    if da:
+                        self.to_a(place, k, dz, da).start()
+
+    def pass_z(self):
+        place = Place(self.inner)
+        for k in self.kinds:
+            for da in self.steps:
+                for dz in range(DEEP):
+                    self.to_a(place, k, dz, da).wait()
+            for dz in (2, 1, 3, 0):
+                for da in self.steps:
+                    self.add(k, place.at(dz), self.from_a[k].at[(da - 1) * DEEP + dz])
+                if dz:
+                    self.to_z(place, k, dz).start()
+
+    def hand_over(self):
+        place = Place(self.inner)
+        for k in self.kinds:
+            for dz in (2, 1, 3):
+                self.to_z(place, k, dz).wait()
+            total = self.own[k][place.at()].astype(F32)
+            for dz in range(1, DEEP):
+                total = total + self.from_z[k][dz - 1].astype(F32)
+            self.final[k][...] = total
+            for copy in self.ends(place, k):
+                copy.start()
+
+    def finish(self):
+        place = Place(self.inner)
+        for k in self.kinds:
+            for copy in self.ends(place, k):
+                copy.wait()
+
+
+def delivery_scratch(owners, grads):
+    inner, kinds = inner_of(owners), len(grads)
+    halves = [(g.shape[1], g.shape[2] // 2) for g in grads]
+    dma = pltpu.SemaphoreType.DMA
+
+    def room(count):
+        return [pltpu.VMEM((count, *h), BF) for h in halves]
+
+    return [
+        *room(owners), *room(owners), *room((inner - 1) * inner * DEEP), *room((inner - 1) * DEEP),
+        *room(DEEP - 1), *[pltpu.VMEM(h, F32) for h in halves],
+        dma((kinds,)), dma((kinds, 2)), dma((kinds, 2, (inner - 1) * inner * DEEP)),
+        dma((kinds, 2, (inner - 1) * DEEP)), dma((kinds, 2, DEEP - 1)), dma((kinds, 3)),
+    ]
+
+
 def deliver_kernel(inner, kinds, *refs):
     ins, table_ref, outs, sum_ref = refs[:kinds], refs[kinds], refs[kinds + 1 : 2 * kinds + 1], refs[2 * kinds + 1]
-    at = 2 * kinds + 2
-    own, from_mate, from_b, from_a, from_z, final = (refs[at + i * kinds : at + (i + 1) * kinds] for i in range(6))
-    load_sem, mate_sem, b_sem, a_sem, z_sem, end_sem, parts, part_sem = refs[at + 6 * kinds :]
-    owners = DEEP * inner * inner
+    parts, part_sem = refs[-2:]
     place = Place(inner)
-    steps = range(1, inner)
     meet(place)
-
-    def columns(k, core):
-        half = outs[k].shape[-1] // 2
-        return pl.ds(pl.multiple_of(core * half, LANES), half)
+    moves = Delivery(inner, ins, outs, refs[2 * kinds + 2 :])
 
     def table_stage(stage, value, count, mine, peer):
         parts[stage, mine] = value
@@ -566,100 +736,22 @@
     along_u = lambda d: (place.at(da=d * (1 - place.core), db=d * place.core), place.core)
     along_v = lambda d: (place.at(da=d * place.core, db=d * (1 - place.core)), place.core)
     begun = table_stage(0, table_ref[...], 2, place.core, lambda d: place.partner())
-
-    loads, swaps = [], []
-    for k in range(kinds):
-        swap = remote(ins[k].at[:, :, columns(k, place.mate)], from_mate[k], mate_sem.at[k, 0], mate_sem.at[k, 1],
-                      place.partner())
-        swap.start()
-        load = pltpu.make_async_copy(ins[k].at[:, :, columns(k, place.core)], own[k], load_sem.at[k])
-        load.start()
-        swaps.append(swap)
-        loads.append(load)
-
-    sent = []
-
-    def add(k, block, other):
-        own[k][block] = (own[k][block].astype(F32) + other[...].astype(F32)).astype(BF)
-
-    for k in range(kinds):
-        loads[k].wait()
-        swaps[k].wait()
-        for db in tuple(steps) + (0,):
-            for da in range(inner):
-                for dz in range(DEEP):
-                    block = place.at(dz, da, db)
-                    add(k, block, from_mate[k].at[block])
-                    if db:
-                        slot = (db - 1) * inner * DEEP + da * DEEP + dz
-                        copy = remote(own[k].at[block], from_b[k].at[slot], b_sem.at[k, 0, slot],
-                                      b_sem.at[k, 1, slot], place.device(db=db))
-                        copy.start()
-                        sent.append((k, copy))
+    moves.start()
+    moves.pass_b()
     begun = table_stage(1, table_sum(begun), inner, u, along_u)
-    arrivals_b = list(sent)
-    sent = []
-    for k in range(kinds):
-        for kk, copy in arrivals_b:
-            if kk == k:
-                copy.wait()
-        for da in tuple(steps) + (0,):
-            for dz in range(DEEP):
-                block = place.at(dz, da)
-                for db in steps:
-                    add(k, block, from_b[k].at[(db - 1) * inner * DEEP + da * DEEP + dz])
-                if da:
-                    slot = (da - 1) * DEEP + dz
-                    copy = remote(own[k].at[block], from_a[k].at[slot], a_sem.at[k, 0, slot], a_sem.at[k, 1, slot],
-                                  place.device(da=da))
-                    copy.start()
-                    sent.append((k, copy))
+    moves.pass_a()
     begun = table_stage(2, table_sum(begun), inner, v, along_v)
-    arrivals_a = list(sent)
-    sent = []
-    for k in range(kinds):
-        for kk, copy in arrivals_a:
-            if kk == k:
-                copy.wait()
-        for dz in (2, 1, 3, 0):
-            block = place.at(dz)
-            for da in steps:
-                add(k, block, from_a[k].at[(da - 1) * DEEP + dz])
-            if dz:
-                copy = remote(own[k].at[block], from_z[k].at[dz - 1], z_sem.at[k, 0, dz - 1], z_sem.at[k, 1, dz - 1],
-                              place.device(dz=dz))
-                copy.start()
-                sent.append((k, copy))
+    moves.pass_z()
     begun = table_stage(3, table_sum(begun), DEEP, place.z, lambda d: place.device(dz=d))
-    ends = []
-    for k in range(kinds):
-        for kk, copy in sent:
-            if kk == k:
-                copy.wait()
-        total = own[k][place.at()].astype(F32)
-        for dz in range(1, DEEP):
-            total = total + from_z[k][dz - 1].astype(F32)
-        final[k][...] = total
-        there = outs[k].at[:, columns(k, place.core)]
-        far = remote(final[k], there, end_sem.at[k, 0], end_sem.at[k, 1], place.partner())
-        near = pltpu.make_async_copy(final[k], there, end_sem.at[k, 2])
-        far.start()
-        near.start()
-        ends += [far, near]
+    moves.hand_over()
+    moves.finish()
     sum_ref[...] = table_sum(begun)
-    for copy in ends:
-        copy.wait()
 
 
 def delivered(grads, table):
     owners = lax.axis_size("fsdp")
     inner, kinds = inner_of(owners), len(grads)
     anywhere = pl.BlockSpec(memory_space=pl.ANY)
-    halves = [(g.shape[1], g.shape[2] // 2) for g in grads]
-
-    def room(count, dtype=BF):
-        return [pltpu.VMEM((count, *h), dtype) for h in halves]
-
     dma = pltpu.SemaphoreType.DMA
     return pl.pallas_call(
         functools.partial(deliver_kernel, inner, kinds),
@@ -668,11 +760,7 @@
         out_shape=[jax.ShapeDtypeStruct(g.shape[1:], F32) for g in grads]
         + [jax.ShapeDtypeStruct(table.shape, F32)],
         scratch_shapes=[
-            *room(owners), *room(owners), *room((inner - 1) * inner * DEEP), *room((inner - 1) * DEEP),
-            *room(DEEP - 1), *[pltpu.VMEM(h, F32) for h in halves],
-            dma((kinds,)), dma((kinds, 2)), dma((kinds, 2, (inner - 1) * inner * DEEP)),
-            dma((kinds, 2, (inner - 1) * DEEP)), dma((kinds, 2, DEEP - 1)), dma((kinds, 3)),
-            pltpu.VMEM((4, DEEP, *table.shape), F32), dma((4, 2, DEEP)),
+            *delivery_scratch(owners, grads), pltpu.VMEM((4, DEEP, *table.shape), F32), dma((4, 2, DEEP)),
         ],
         compiler_params=pltpu.CompilerParams(collective_id=1, has_side_effects=True, vmem_limit_bytes=60 << 20),
         name="deliver",
@@ -729,17 +817,20 @@
     x = images.transpose(1, 2, 0, 3).reshape(rows * cols, imgs, d)
     ct = cotangent.transpose(1, 2, 0, 3).reshape(rows * cols, imgs, d)
     vectors = (norm1_gain, norm1_bias, q_bias, v_bias, proj_bias, norm2_gain, norm2_bias, fc2_bias, fc1_bias)
-    shards = (packed_row(vectors)[None], qkv_weight, proj_weight, fc1_weight, fc2_weight)
-    packed, *mats, halo, ct_halo = gathered(shards, (x, ct))
+    packed, w_qkv, halo = gathered((packed_row(vectors)[None], qkv_weight), (x,))
     packed = packed[:, 0].astype(F32)
     part = d // owners
     vecs = packed[:, : 8 * part].reshape(owners, 8, part).transpose(1, 0, 2).reshape(8, d)
     b_in = packed[:, 8 * part : 8 * part + fc1_bias.shape[0]].reshape(1, -1)
-    w_qkv, w_proj, w_in, w_out = (v.reshape(owners * v.shape[1], v.shape[2]) for v in mats)
+    whole = lambda v: v.reshape(owners * v.shape[1], v.shape[2])
+    w_qkv = whole(w_qkv)
     onehot, relative = relative_parts(rel_index, bias_table)
     rel = bias_of_pairs(relative, regions)
 
-    qkv, att, prob = attend(x, halo, vecs, w_qkv, rel)
+    qkv, att, prob, *mats, ct_halo = attend(
+        x, halo, vecs, w_qkv, rel, (proj_weight, fc1_weight, fc2_weight), (ct,)
+    )
+    w_proj, w_in, w_out = (whole(v) for v in mats)
     flat = lambda v: v.reshape(v.shape[0] * imgs, d)
     tall = lambda v: v.reshape(v.shape[0] // imgs, imgs, d)
     out_top, out_rest, gm, gatt, dwp, dw1, dw2, db_in, small2 = mlp(
@@ -747,7 +838,10 @@
     )
     swapped = lambda v: lax.ppermute(v, "win", [(0, 1), (1, 0)])
     out_top = swapped(out_top)
-    gin_top, gin_rest, dwq, small1, bsum, rel_sum = back(x, halo, tall(gm), tall(gatt), qkv, prob, vecs, w_qkv)
+    blocks = lambda v: v.reshape(owners, v.shape[0] // owners, v.shape[1])
+    gin_top, gin_rest, dwq, small1, bsum, rel_sum, dwp, dw1, dw2 = back(
+        x, halo, tall(gm), tall(gatt), qkv, prob, vecs, w_qkv, (blocks(dwp), blocks(dw1), blocks(dw2))
+    )
     gin_top = swapped(gin_top)
     spread = jnp.asarray(spread_matrix())
     pairs = jnp.einsum("at,hba,bs->tsh", spread, rel_sum[:, :TOK, :TOK], spread, precision=HIGHEST)
@@ -757,10 +851,7 @@
         small1[0], small1[1], bsum[0, :d], bsum[0, 2 * d :], small2[2], small2[0], small2[1], small2[3], db_in[0],
     )
     row = packed_row([v.reshape(owners, 1, -1) for v in grads]).astype(BF)
-    blocks = lambda v: v.reshape(owners, v.shape[0] // owners, v.shape[1])
-    sums, dwp, dw1, dw2, dwq, table_sum = delivered(
-        (row, blocks(dwp), blocks(dw1), blocks(dw2), blocks(dwq)), flat_table
-    )
+    sums, dwq, table_sum = delivered((row, blocks(dwq)), flat_table)
     at, own = 0, []
     for v in vectors:
         own.append(sums[0, at : at + v.shape[0]])

time: 316 us -> 291 us (0.921)
  Pallas kernels: 275 us -> 248 us
    pallas_call x1, Pallas kernels: 50.7 us -> 24.2 us  [delivered(): pl.pallas_call(functools.partial(deliver_kernel, inner, kinds), in_specs=...]
    pallas_call x1, Pallas kernels: 43.7 us -> 23.5 us  [gathered(): pl.pallas_call(functools.partial(gather_kernel, inner, kinds, fields), in...]
    pallas_call x2, Pallas kernels: 96.8 us -> 117 us  [the longest x1 66.5 us: back(): pl.pallas_call(functools.partial(back_kernel, inner_of(owners), kinds), g...]
  transfers between devices with their start and end apart: 2 -> 2, of which waited for: 0 -> 0; matrix products, arithmetic and copies ran while one was open for 6% -> 6% of each run, Pallas kernels for 16% -> 8%
where the time goes in v4:
time: 291 us
  Pallas kernels  248 us (85%)
  local copies, waits for them, and re-layouts  20.6 us (7%)
  other arithmetic  11.8 us (4%)
  matrix products  8.58 us (3%)
    pallas_call x1, Pallas kernels, mlp(): pl.pallas_call(functools.partial(mlp_kernel, tops), grid=(rows // tile,),...  83.8 us
    pallas_call x1, Pallas kernels, back(): pl.pallas_call(functools.partial(back_kernel, inner_of(owners), kinds), g...  66.5 us
    pallas_call x1, Pallas kernels, attend(): pl.pallas_call(functools.partial(attend_kernel, inner, kinds, fields), gr...  50.3 us
    pallas_call x1, Pallas kernels, delivered(): pl.pallas_call(functools.partial(deliver_kernel, inner, kinds), in_specs=...  24.2 us
    pallas_call x1, Pallas kernels, gathered(): pl.pallas_call(functools.partial(gather_kernel, inner, kinds, fields), in...  23.5 us
    concatenate x2, other arithmetic, per_device(): jnp.concatenate([top, rest], axis=0).reshape(rows, cols, imgs, d)  9.13 us
    concatenate x2, local copies, waits for them, and re-layouts, packed_row(): row = jnp.concatenate(parts, axis=-1)  6.33 us
  transfers between devices with their start and end apart: 2, of which 0 were waited for; matrix products, arithmetic and copies ran while one was open for 6% of the time, Pallas kernels for 8%

profile of v4, /device:TPU:0, one launch (start us, length us, event | category | flops | bytes accessed | tf_op | source)
XLA Modules:
  0.0 290.7 jit_solution(18038326356457030986)
XLA Ops:
  0.6 0.0 copy-start
  0.7 0.0 copy-start.4
  0.7 0.8 slice_reduce_fusion.8
  1.5 0.8 slice_reduce_fusion.9
  2.3 6.1 %concatenate.24 = bf16[384]{0:T(512)(128)(2,1)S(1)} concatenate(bf16[32]{0:T(256)(128)(2,1)} %param.22, bf16[32]{0:T(256)(128)(2,1)} %param.23, bf16[32]{0:T(256)(128)(2,1)} %param.25, bf16[32]{0:T(256)(128)(2,1)} %param.26, bf16[32]{0:T(256)(128)(2,1)} %param.28, bf16[32]{0:T(256)(128)(2,1)} %param.29, bf16[32]{0:T(256)(128)(2,1)} %param.30, bf16[32]{0:T(256)(128)(2,1)} %param.34, ...), dimensions={0} | concatenate | bytes 1536 | tf_op jit(solution)/shard_map/concatenate | solution.py:807
  8.4 0.6 broadcast_in_dim.26.refs_0_
  9.0 23.5 %gather.1 = (bf16[16,1,512]{2,1,0:T(2,128)(2,1)}, bf16[16,32,1536]{2,1,0:T(8,128)(2,1)}, bf16[42,32,512]{2,1,0:T(8,128)(2,1)}) custom-call(bf16[1,512]{1,0:T(2,128)(2,1)} %broadcast_in_dim.26.refs_0_, bf16[32,1536]{1,0:T(8,128)(2,1)} %refs_1_.2, bf16[98,32,512]{2,1,0:T(8,128)(2,1)} %bitcast.85), custom_call_target="tpu_custom_call" | custom-call | tf_op jit(solution)/shard_map/gather/pallas_call | solution.py:576
  32.5 0.8 copy.58
  33.3 0.6 slice.150
  33.9 0.1 slice.124
  34.0 0.1 slice.126
  34.0 0.1 slice.119
  34.1 0.1 slice.121
  34.2 0.1 slice.122
  34.3 0.1 pad_add_fusion.1
  34.4 0.1 eq.38
  34.5 0.1 eq.34
  34.6 0.1 compare_select_fusion
  34.7 1.2 fusion.1
  35.9 0.2 reshape.167
  36.2 0.9 fusion.10
  37.1 0.9 fusion.3
  38.0 1.0 pad_select_fusion.rel_ref
  39.0 0.1 reshape.164
  39.1 0.7 reshape.165.vec_ref
  39.8 50.3 %attend.1 = (bf16[32,12,112,128]{3,2,1,0:T(8,128)(2,1)}, bf16[98,32,512]{2,1,0:T(8,128)(2,1)}, bf16[32,16,112,112]{3,2,1,0:T(8,128)(2,1)}, bf16[16,32,512]{2,1,0...) custom-call(bf16[98,32,512]{2,1,0:T(8,128)(2,1)} %bitcast.86, ...), custom_call_target="tpu_custom_call" | custom-call | tf_op jit(solution)/shard_map/attend/pallas_call | solution.py:161
  90.1 83.8 %mlp.1 = (bf16[1344,512]{1,0:T(8,128)(2,1)}, bf16[1792,512]{1,0:T(8,128)(2,1)}, f32[3136,512]{1,0:T(8,128)}, bf16[3136,512]{1,0:T(8,128)(2,1)}, bf16[512,512]{1,...) custom-call(bf16[3136,512]{1,0:T(8,128)(2,1)} %bitcast.87, ...), custom_call_target="tpu_custom_call" | custom-call | tf_op jit(solution)/shard_map/mlp/pallas_call | solution.py:272
  173.8 0.0 copy-start.10
  173.9 0.0 copy-start.12
  173.9 66.5 %back.1 = (f32[42,32,512]{2,1,0:T(8,128)}, f32[56,32,512]{2,1,0:T(8,128)}, bf16[512,1536]{1,0:T(8,128)(2,1)}, f32[8,512]{1,0:T(8,128)}, f32[1,1536]{1,0:T(1,128)...) custom-call(bf16[98,32,512]{2,1,0:T(8,128)(2,1)} %bitcast.88, ...), custom_call_target="tpu_custom_call" | custom-call | tf_op jit(solution)/shard_map/back/pallas_call | solution.py:392
  240.3 0.4 collective-permute-start.1
  240.8 0.1 collective-permute-start
  240.9 0.7 convert.38
  241.6 0.1 reshape_squeeze.51
  241.7 0.1 reshape_squeeze.50
  241.8 0.7 convert.37
  242.6 0.1 reshape_squeeze.49
  242.6 0.1 reshape_squeeze.48
  242.8 0.1 reshape_squeeze.55
  242.9 0.1 reshape_squeeze.54
  243.0 0.1 reshape_squeeze.53
  243.1 0.1 reshape_squeeze.52
  243.1 0.2 concatenate.30
  243.4 0.6 pad.24.refs_0_
  244.0 3.1 %fusion.8 = f32[16,98,49]{1,2,0:T(8,128)S(1)} fusion(f32[98,49,1]{0,1,2:T(8,128)S(1)} %copy-done.4, f32[16,112,112]{2,1,0:T(8,128)} %get-tuple-element.71), kind=kOutput, calls=%fused_computation.14 | convolution fusion | flops 90354432 | bytes 1178504 | tf_op jit(solution)/shard_map/at,hba,bs->tsh/dot_general | solution.py:847
  247.2 0.5 convolution_bitcast_fusion.1
  247.7 0.2 reshape.185
  247.9 1.9 fusion.4
  249.8 0.1 reshape.186
  249.9 0.6 pad_bitcast_fusion.refs_2_
  250.5 24.2 %deliver.1 = (f32[1,512]{1,0:T(1,128)}, f32[32,1536]{1,0:T(8,128)}, f32[24,128]{1,0:T(8,128)}) custom-call(bf16[16,1,512]{2,1,0:T(2,128)(2,1)} %pad.24.refs_0_, bf16[16,32,1536]{2,1,0:T(8,128)(2,1)} %bitcast.104, f32[24,128]{1,0:T(8,128)} %pad_bitcast_fusion.refs_2_), custom_call_target="tpu_custom_call" | custom-call | tf_op jit(solution)/shard_map/deliver/pallas_call | solution.py:756
  274.7 0.8 slice.147
  275.5 0.7 copy.51
  276.2 1.1 slice_bitcast_fusion.1
  277.3 1.4 slice_bitcast_fusion
  278.7 0.0 collective-permute-done
  278.8 3.5 %pad_maximum_fusion.1 = bf16[98,32,512]{2,1,0:T(8,128)(2,1)} fusion(bf16[56,32,512]{2,1,0:T(8,128)(2,1)S(1)} %bitcast.103, bf16[42,32,512]{2,1,0:T(8,128)(2,1)} %bitcast.19), kind=kLoop, calls=%fused_computation.1 | loop fusion | flops 1605632 | bytes 6422528 | tf_op jit(solution)/shard_map/concatenate | solution.py:861
  282.2 0.0 collective-permute-done.1
  282.3 0.0 copy-start.1
  282.3 5.7 %pad_maximum_fusion = f32[98,32,512]{2,1,0:T(8,128)} fusion(f32[56,32,512]{2,1,0:T(8,128)S(1)} %copy-done.2, f32[42,32,512]{2,1,0:T(8,128)} %collective-permute-done.1), kind=kLoop, calls=%fused_computation | loop fusion | flops 1605632 | bytes 12845056 | tf_op jit(solution)/shard_map/concatenate | solution.py:861
  288.0 0.7 copy.63
  288.6 0.6 copy.64
  289.3 0.7 copy.65
  290.0 0.7 copy.66
  (31 shorter events, 0.2 us)
Async XLA Ops:
  0.6 34.0 %copy-start = (f32[169,16]{0,1:T(8,128)S(1)}, f32[169,16]{0,1:T(8,128)}, u32[]{:S(2)}) copy-start(f32[169,16]{0,1:T(8,128)} %param.35) | copy-start | bytes 32452
  0.7 35.5 %copy-start.4 = (f32[98,49,1]{0,1,2:T(8,128)S(1)}, f32[98,49,1]{0,1,2:T(8,128)}, u32[]{:S(2)}) copy-start(f32[98,49,1]{0,1,2:T(8,128)} %constant.30) | copy-start | bytes 57628
  0.7 33.8 %copy-start.9 = (s32[49,49]{1,0:T(8,128)S(1)}, s32[49,49]{1,0:T(8,128)}, u32[]{:S(2)}) copy-start(s32[49,49]{1,0:T(8,128)} %param.37) | copy-start | bytes 28816
  9.0 28.1 %copy-start.11 = (pred[98,98]{1,0:T(8,128)(4,1)S(1)}, pred[98,98]{1,0:T(8,128)(4,1)}, u32[]{:S(2)}) copy-start(pred[98,98]{1,0:T(8,128)(4,1)} %constant.16.clone) | copy-start | bytes 28816
  173.8 68.9 %copy-start.10 = (f32[8,512]{1,0:T(8,128)S(1)}, f32[8,512]{1,0:T(8,128)}, u32[]{:S(2)}) copy-start(f32[8,512]{1,0:T(8,128)} %get-tuple-element.68) | copy-start | bytes 49156
  173.9 68.9 %copy-start.12 = (f32[1,2048]{1,0:T(1,128)S(1)}, f32[1,2048]{1,0:T(1,128)}, u32[]{:S(2)}) copy-start(f32[1,2048]{1,0:T(1,128)} %get-tuple-element.69) | copy-start | bytes 24580
  240.3 41.9 %collective-permute-start.1 = (f32[42,32,512]{2,1,0:T(8,128)}, f32[42,32,512]{2,1,0:T(8,128)}, u32[]{:S(2)}, u32[]{:S(2)}) collective-permute-start(f32[42,32,512]{2,1,0:T(8,128)} %get-tuple-element.64), channel_id=1, source_target_pairs={{0,1},{1,0},{2,3},{3,2},{4,5},{5,4},{6,7},{7,6},{8,9},{9,8},{10,11... | collective-permute-start | bytes 8257544 | tf_op jit(solution)/shard_map/ppermute | solution.py:839
  240.8 38.0 %collective-permute-start = (bf16[1344,512]{1,0:T(8,128)(2,1)}, bf16[1344,512]{1,0:T(8,128)(2,1)}, u32[]{:S(2)}, u32[]{:S(2)}) collective-permute-start(bf16[1344,512]{1,0:T(8,128)(2,1)} %get-tuple-element.55), channel_id=1, source_target_pairs={{0,1},{1,0},{2,3},{3,2},{4,5},{5,4},{6,7},{7,6},{8,9},{9,8},{10,11... | collective-permute-start | bytes 4128776 | tf_op jit(solution)/shard_map/ppermute | solution.py:839
  244.0 34.7 %copy-start.3 = (bf16[1792,512]{1,0:T(8,128)(2,1)S(1)}, bf16[1792,512]{1,0:T(8,128)(2,1)}, u32[]{:S(2)}) copy-start(bf16[1792,512]{1,0:T(8,128)(2,1)} %get-tuple-element.56) | copy-start | bytes 5505028
  278.8 3.5 %copy-start.2 = (f32[56,32,512]{2,1,0:T(8,128)S(1)}, f32[56,32,512]{2,1,0:T(8,128)}, u32[]{:S(2)}) copy-start(f32[56,32,512]{2,1,0:T(8,128)} %get-tuple-element.65) | copy-start | bytes 11010052
  282.2 5.7 %copy-start.7 = (f32[32,1536]{1,0:T(8,128)S(1)}, f32[32,1536]{1,0:T(8,128)}, u32[]{:S(2)}) copy-start(f32[32,1536]{1,0:T(8,128)} %get-tuple-element.134) | copy-start | bytes 589828
  282.2 6.4 %copy-start.8 = (f32[32,512]{1,0:T(8,128)S(1)}, f32[32,512]{1,0:T(8,128)}, u32[]{:S(2)}) copy-start(f32[32,512]{1,0:T(8,128)} %get-tuple-element.137) | copy-start | bytes 196612
  282.2 7.0 %copy-start.6 = (f32[32,2048]{1,0:T(8,128)S(1)}, f32[32,2048]{1,0:T(8,128)}, u32[]{:S(2)}) copy-start(f32[32,2048]{1,0:T(8,128)} %get-tuple-element.141) | copy-start | bytes 786436
  282.3 7.7 %copy-start.5 = (f32[128,512]{1,0:T(8,128)S(1)}, f32[128,512]{1,0:T(8,128)}, u32[]{:S(2)}) copy-start(f32[128,512]{1,0:T(8,128)} %get-tuple-element.143) | copy-start | bytes 786436
  282.3 8.4 %copy-start.1 = (f32[169,16]{0,1:T(8,128)S(1)}, f32[169,16]{0,1:T(8,128)}, u32[]{:S(2)}) copy-start(f32[169,16]{0,1:T(8,128)} %param.35) | copy-start | bytes 32452

commit v5 on v4

--- a/solution.py
+++ b/solution.py
@@ -90,20 +90,35 @@
         action()
 
 
+def at_images(events, i):
+    images = pl.program_id(0) * NB + i
+    for share, action in events:
+        @pl.when(images == share)
+        def _(action=action):
+            action()
+
+
+def whole_cuts(count):
+    return tuple((i, 0, 1) for i in range(count))
+
+
 def attend_kernel(inner, kinds, fields, x_ref, halo_ref, vec_ref, w_ref, rel_ref, *refs):
     ins, maps = refs[:kinds], refs[kinds : kinds + fields]
     qkv_ref, att_ref, prob_ref = refs[kinds + fields : kinds + fields + 3]
     outs, halos = refs[kinds + fields + 3 : 2 * kinds + fields + 3], refs[2 * kinds + fields + 3 : 2 * (kinds + fields) + 3]
     wide, joined, *sems = refs[2 * (kinds + fields) + 3 :]
-    moves = Spread(inner, ins, maps, outs, halos, *sems)
+    moves = Spread(inner, whole_cuts(kinds), ins, maps, outs, halos, *sems)
 
     def begin():
         meet(Place(inner))
         moves.run(0)
 
     at_step(0, begin)
-    for stage in (1, 2, 3):
-        at_step(stage, functools.partial(moves.run, stage))
+    early, late = tuple(range(kinds - 1)), (kinds - 1,)
+    events = [
+        (share, functools.partial(moves.run, stage, which))
+        for share, stage, which in ((8, 1, early), (13, 1, late), (15, 2, early), (19, 2, late), (23, 3, early), (28, 3, late))
+    ]
     d = x_ref.shape[-1]
     n, _ = normalized(shifted_rows(x_ref, halo_ref))
     normed = (n * vec_ref[0:1] + vec_ref[1:2]).astype(BF)
@@ -126,6 +141,7 @@
     scale = HD ** (-0.5)
 
     def one(i, carry):
+        at_images(events, i)
         for g in range(per):
             q = wide[g, pl.ds(i, PAD, stride=NB), :].astype(BF)
             k = wide[per + g, pl.ds(i, PAD, stride=NB), :].astype(BF)
@@ -181,7 +197,7 @@
         scratch_shapes=[
             pltpu.VMEM((3 * per, PAD * NB, LANES), F32),
             pltpu.VMEM((per, PAD * NB, LANES), F32),
-            *spread_scratch(owners, kinds, fields),
+            *spread_scratch(owners, kinds, kinds, fields),
         ],
         compiler_params=pltpu.CompilerParams(collective_id=2, has_side_effects=True, vmem_limit_bytes=60 << 20),
         name="attend",
@@ -215,20 +231,27 @@
     gb_t = gb.T
     out = middle + vec_ref[7:8]
     m = None
+    def begin(c):
+        at = slice(c * chunk, (c + 1) * chunk)
+        return mm(normed, w1_ref[:, at]), mm_nt(gb, w2_ref[at, :])
+
+    now = begin(0)
     for c in range(ff // chunk):
         at = slice(c * chunk, (c + 1) * chunk)
-        hidden = mm(normed, w1_ref[:, at]) + b1_ref[:, at]
+        later = begin(c + 1) if c + 1 < ff // chunk else None
+        hidden = now[0] + b1_ref[:, at]
         cdf = 0.5 * (1.0 + erf(hidden * 0.7071067811865476))
         slope = cdf + hidden * (0.3989422804014327 * jnp.exp(-0.5 * hidden * hidden))
         active = (hidden * cdf).astype(BF)
-        out = out + mm(active, w2_ref[at, :])
-        gh = mm_nt(gb, w2_ref[at, :]) * slope
+        gh = now[1] * slope
         ghb = gh.astype(BF)
         ab1[:, at] += col_sum(ghb.astype(F32))
+        out = out + mm(active, w2_ref[at, :])
+        part = mm_nt(ghb, w1_ref[:, at])
+        m = part if m is None else m + part
         aw2[:, at] += mm(gb_t, active)
         aw1[:, at] += mm(normed_t, ghb)
-        part = mm_nt(ghb, w1_ref[:, at])
-        m = part if m is None else m + part
+        now = later
 
     @pl.when(above)
     def _():
@@ -297,16 +320,14 @@
 def back_kernel(inner, kinds, x_ref, halo_ref, gm_ref, gatt_ref, qkv_ref, prob_ref, vec_ref, w_ref, *refs):
     ins, (top_ref, rest_ref, dw_ref, small_ref, bsum_ref, rel_ref) = refs[:kinds], refs[kinds : kinds + 6]
     outs, (wide, grads, aw, asm, abs_), room = refs[kinds + 6 : 2 * kinds + 6], refs[2 * kinds + 6 : 2 * kinds + 11], refs[2 * kinds + 11 :]
-    moves = Delivery(inner, ins, outs, room)
+    moves = Delivery(inner, whole_cuts(kinds), ins, outs, room)
 
     def begin():
         meet(Place(inner))
         moves.start()
 
     at_step(0, begin)
-    at_step(1, moves.pass_b)
-    at_step(2, moves.pass_a)
-    at_step(3, moves.pass_z)
+    events = [(6, moves.pass_b), (15, moves.pass_a), (20, moves.pass_z), (29, moves.hand_over)]
     step = pl.program_id(0)
     d = x_ref.shape[-1]
     per = d // LANES
@@ -325,6 +346,7 @@
     masks = head_masks()
 
     def one(i, carry):
+        at_images(events, i)
         for g in range(per):
             ga = wide[g, pl.ds(i, PAD, stride=NB), :].astype(BF)
             q = qkv_ref[i, g]
@@ -369,11 +391,7 @@
     top_ref[...] = gin[:TOP]
     rest_ref[...] = gin[TOP:]
 
-    def end():
-        moves.hand_over()
-        moves.finish()
-
-    at_step(3, end)
+    at_step(3, moves.finish)
 
     @pl.when(step == pl.num_programs(0) - 1)
     def _():
@@ -414,7 +432,7 @@
             pltpu.VMEM((d, 3 * d), F32),
             pltpu.VMEM((8, d), F32),
             pltpu.VMEM((1, 3 * d), F32),
-            *delivery_scratch(owners, grads),
+            *delivery_scratch(owners, grads, whole_cuts(kinds)),
         ],
         compiler_params=pltpu.CompilerParams(collective_id=3, has_side_effects=True, vmem_limit_bytes=62 << 20),
         name="back",
@@ -470,8 +488,15 @@
     )
 
 
+def cut_columns(array, cut, core):
+    half = array.shape[-1] // 2
+    width = half // cut[2]
+    return pl.ds(pl.multiple_of(core * half + cut[1] * width, LANES), width)
+
+
 class Spread:
-    def __init__(self, inner, ins, maps, outs, halos, send_sem, recv_sem, own_sem, halo_sem):
+    def __init__(self, inner, cuts, ins, maps, outs, halos, send_sem, recv_sem, own_sem, halo_sem):
+        self.cuts = cuts
         self.inner, self.ins, self.maps, self.outs, self.halos = inner, ins, maps, outs, halos
         self.send_sem, self.recv_sem, self.own_sem, self.halo_sem = send_sem, recv_sem, own_sem, halo_sem
         steps = [("a", d) for d in range(1, inner)], [("b", d) for d in range(1, inner)]
@@ -489,16 +514,16 @@
             self.plan.append(rows)
 
     def piece(self, k, block, core):
-        half = self.outs[k].shape[-1] // 2
-        return self.outs[k].at[block, :, pl.ds(pl.multiple_of(core * half, LANES), half)]
+        out = self.outs[self.cuts[k][0]]
+        return out.at[block, :, cut_columns(out, self.cuts[k], core)]
 
     def copy(self, place, k, stage, block, target, index):
         (axis, d), where = target, place.at(*block)
         device = {"z": place.device(dz=d), "a": place.device(da=d), "b": place.device(db=d), "m": place.partner()}[axis]
-        half = self.outs[k].shape[-1] // 2
         src = self.piece(k, where, place.core)
         if stage == 0:
-            src = self.ins[k].at[:, pl.ds(pl.multiple_of(place.core * half, LANES), half)]
+            shard = self.ins[self.cuts[k][0]]
+            src = shard.at[:, cut_columns(shard, self.cuts[k], place.core)]
         return remote(src, self.piece(k, where, place.core), self.send_sem.at[k, index],
                       self.recv_sem.at[k, place.core, where], device)
 
@@ -515,7 +540,7 @@
 
     def run(self, stage, kinds=None):
         place = Place(self.inner)
-        for k in range(len(self.ins)) if kinds is None else kinds:
+        for k in range(len(self.cuts)) if kinds is None else kinds:
             for block, targets in self.plan[stage]:
                 if stage:
                     self.arrive(place, k, block, place.core)
@@ -527,7 +552,7 @@
 
     def finish(self):
         place = Place(self.inner)
-        for k in range(len(self.ins)):
+        for k in range(len(self.cuts)):
             for stage in self.plan[1:]:
                 for block, _ in stage:
                     self.arrive(place, k, block, place.mate)
@@ -539,11 +564,11 @@
             copy.wait()
 
 
-def spread_scratch(owners, kinds, fields):
+def spread_scratch(owners, kinds, arrays, fields):
     inner = inner_of(owners)
     sends = 3 + 2 * (inner - 1) + 3 * (2 * inner - 1) + 2 * DEEP * (inner - 1) * inner
     dma = pltpu.SemaphoreType.DMA
-    return [dma((kinds, sends)), dma((kinds, 2, owners)), dma((kinds,)), dma((fields, 2))]
+    return [dma((kinds, sends)), dma((kinds, 2, owners)), dma((arrays,)), dma((fields, 2))]
 
 
 def spread_shapes(owners, shards, maps):
@@ -552,13 +577,13 @@
     ]
 
 
-def gather_kernel(inner, kinds, fields, *refs):
+def gather_kernel(inner, cuts, kinds, fields, *refs):
     ins, maps = refs[:kinds], refs[kinds : kinds + fields]
     outs, halos = refs[kinds + fields : 2 * kinds + fields], refs[2 * kinds + fields : 2 * (kinds + fields)]
     meet(Place(inner))
-    moves = Spread(inner, ins, maps, outs, halos, *refs[2 * (kinds + fields) :])
+    moves = Spread(inner, cuts, ins, maps, outs, halos, *refs[2 * (kinds + fields) :])
     moves.run(0)
-    for k in range(kinds):
+    for k in range(len(cuts)):
         moves.run(1, (k,))
         moves.run(2, (k,))
     moves.run(3)
@@ -569,24 +594,24 @@
     return int(round((owners // DEEP) ** 0.5))
 
 
-def gathered(shards, maps):
+def gathered(shards, maps, cuts):
     owners = lax.axis_size("fsdp")
     inner, kinds, fields = inner_of(owners), len(shards), len(maps)
     anywhere = pl.BlockSpec(memory_space=pl.ANY)
     return pl.pallas_call(
-        functools.partial(gather_kernel, inner, kinds, fields),
+        functools.partial(gather_kernel, inner, cuts, kinds, fields),
         in_specs=[anywhere] * (kinds + fields),
         out_specs=[anywhere] * (kinds + fields),
         out_shape=spread_shapes(owners, shards, maps),
-        scratch_shapes=spread_scratch(owners, kinds, fields),
+        scratch_shapes=spread_scratch(owners, len(cuts), kinds, fields),
         compiler_params=pltpu.CompilerParams(collective_id=0, has_side_effects=True),
         name="gather",
     )(*shards, *maps)
 
 
 class Delivery:
-    def __init__(self, inner, ins, outs, refs):
-        self.inner, self.ins, self.outs, kinds = inner, ins, outs, len(ins)
+    def __init__(self, inner, cuts, ins, outs, refs):
+        self.inner, self.cuts, self.ins, self.outs, kinds = inner, cuts, ins, outs, len(cuts)
         self.kinds = range(kinds)
         self.own, self.from_mate, self.from_b, self.from_a, self.from_z, self.final = (
             refs[i * kinds : (i + 1) * kinds] for i in range(6)
@@ -595,17 +620,16 @@
         self.steps = range(1, inner)
 
     def columns(self, k, core):
-        half = self.outs[k].shape[-1] // 2
-        return pl.ds(pl.multiple_of(core * half, LANES), half)
+        return cut_columns(self.outs[self.cuts[k][0]], self.cuts[k], core)
 
     def add(self, k, block, other):
         self.own[k][block] = (self.own[k][block].astype(F32) + other[...].astype(F32)).astype(BF)
 
     def loads(self, place, k):
         return (
-            remote(self.ins[k].at[:, :, self.columns(k, place.mate)], self.from_mate[k], self.mate_sem.at[k, 0],
+            remote(self.ins[self.cuts[k][0]].at[:, :, self.columns(k, place.mate)], self.from_mate[k], self.mate_sem.at[k, 0],
                    self.mate_sem.at[k, 1], place.partner()),
-            pltpu.make_async_copy(self.ins[k].at[:, :, self.columns(k, place.core)], self.own[k], self.load_sem.at[k]),
+            pltpu.make_async_copy(self.ins[self.cuts[k][0]].at[:, :, self.columns(k, place.core)], self.own[k], self.load_sem.at[k]),
         )
 
     def to_b(self, place, k, dz, da, db):
@@ -623,7 +647,7 @@
                       self.z_sem.at[k, 1, dz - 1], place.device(dz=dz))
 
     def ends(self, place, k):
-        there = self.outs[k].at[:, self.columns(k, place.core)]
+        there = self.outs[self.cuts[k][0]].at[:, self.columns(k, place.core)]
         return (remote(self.final[k], there, self.end_sem.at[k, 0], self.end_sem.at[k, 1], place.partner()),
                 pltpu.make_async_copy(self.final[k], there, self.end_sem.at[k, 2]))
 
@@ -691,9 +715,9 @@
                 copy.wait()
 
 
-def delivery_scratch(owners, grads):
-    inner, kinds = inner_of(owners), len(grads)
-    halves = [(g.shape[1], g.shape[2] // 2) for g in grads]
+def delivery_scratch(owners, grads, cuts):
+    inner, kinds = inner_of(owners), len(cuts)
+    halves = [(grads[i].shape[1], grads[i].shape[2] // 2 // parts) for i, _, parts in cuts]
     dma = pltpu.SemaphoreType.DMA
 
     def room(count):
@@ -707,12 +731,12 @@
     ]
 
 
-def deliver_kernel(inner, kinds, *refs):
+def deliver_kernel(inner, cuts, kinds, *refs):
     ins, table_ref, outs, sum_ref = refs[:kinds], refs[kinds], refs[kinds + 1 : 2 * kinds + 1], refs[2 * kinds + 1]
     parts, part_sem = refs[-2:]
     place = Place(inner)
     meet(place)
-    moves = Delivery(inner, ins, outs, refs[2 * kinds + 2 :])
+    moves = Delivery(inner, cuts, ins, outs, refs[2 * kinds + 2 :])
 
     def table_stage(stage, value, count, mine, peer):
         parts[stage, mine] = value
@@ -748,19 +772,19 @@
     sum_ref[...] = table_sum(begun)
 
 
-def delivered(grads, table):
+def delivered(grads, table, cuts):
     owners = lax.axis_size("fsdp")
     inner, kinds = inner_of(owners), len(grads)
     anywhere = pl.BlockSpec(memory_space=pl.ANY)
     dma = pltpu.SemaphoreType.DMA
     return pl.pallas_call(
-        functools.partial(deliver_kernel, inner, kinds),
+        functools.partial(deliver_kernel, inner, cuts, kinds),
         in_specs=[anywhere] * kinds + [pl.BlockSpec(memory_space=pltpu.VMEM)],
         out_specs=[anywhere] * kinds + [pl.BlockSpec(memory_space=pltpu.VMEM)],
         out_shape=[jax.ShapeDtypeStruct(g.shape[1:], F32) for g in grads]
         + [jax.ShapeDtypeStruct(table.shape, F32)],
         scratch_shapes=[
-            *delivery_scratch(owners, grads), pltpu.VMEM((4, DEEP, *table.shape), F32), dma((4, 2, DEEP)),
+            *delivery_scratch(owners, grads, cuts), pltpu.VMEM((4, DEEP, *table.shape), F32), dma((4, 2, DEEP)),
         ],
         compiler_params=pltpu.CompilerParams(collective_id=1, has_side_effects=True, vmem_limit_bytes=60 << 20),
         name="deliver",
@@ -804,8 +828,18 @@
 
 
 def packed_row(parts):
-    row = jnp.concatenate(parts, axis=-1)
-    return jnp.pad(row, [(0, 0)] * (row.ndim - 1) + [(0, -row.shape[-1] % (2 * LANES))])
+    width = sum(p.shape[-1] for p in parts)
+    width += -width % (2 * LANES)
+    at, row = 0, None
+    for p in parts:
+        edges = [(0, 0)] * (p.ndim - 1) + [(at, width - at - p.shape[-1])]
+        row = jnp.pad(p, edges) if row is None else row + jnp.pad(p, edges)
+        at += p.shape[-1]
+    return row
+
+
+def qkv_cuts():
+    return ((0, 0, 1),) + tuple((1, part, 3) for part in range(3))
 
 
 def per_device(
@@ -817,7 +851,7 @@
     x = images.transpose(1, 2, 0, 3).reshape(rows * cols, imgs, d)
     ct = cotangent.transpose(1, 2, 0, 3).reshape(rows * cols, imgs, d)
     vectors = (norm1_gain, norm1_bias, q_bias, v_bias, proj_bias, norm2_gain, norm2_bias, fc2_bias, fc1_bias)
-    packed, w_qkv, halo = gathered((packed_row(vectors)[None], qkv_weight), (x,))
+    packed, w_qkv, halo = gathered((packed_row(vectors)[None], qkv_weight), (x,), qkv_cuts())
     packed = packed[:, 0].astype(F32)
     part = d // owners
     vecs = packed[:, : 8 * part].reshape(owners, 8, part).transpose(1, 0, 2).reshape(8, d)
@@ -851,7 +885,7 @@
         small1[0], small1[1], bsum[0, :d], bsum[0, 2 * d :], small2[2], small2[0], small2[1], small2[3], db_in[0],
     )
     row = packed_row([v.reshape(owners, 1, -1) for v in grads]).astype(BF)
-    sums, dwq, table_sum = delivered((row, blocks(dwq)), flat_table)
+    sums, dwq, table_sum = delivered((row, blocks(dwq)), flat_table, qkv_cuts())
     at, own = 0, []
     for v in vectors:
         own.append(sums[0, at : at + v.shape[0]])

time: 291 us -> 288 us (0.990)
  local copies, waits for them, and re-layouts: 20.6 us -> 14.4 us
  Pallas kernels: 248 us -> 251 us
    concatenate x2 -> x0, local copies, waits for them, and re-layouts: 6.33 us -> none  [packed_row(): row = jnp.concatenate(parts, axis=-1)]
    pallas_call x1, Pallas kernels: 83.8 us -> 88.6 us  [mlp(): pl.pallas_call(functools.partial(mlp_kernel, tops), grid=(rows // tile,),...]
    pallas_call x2, Pallas kernels: 47.7 us -> 52 us  [the longest x1 29.1 us: gathered(): pl.pallas_call(functools.partial(gather_kernel, inner, cuts, kinds, field...]
    pallas_call x1, Pallas kernels: 66.5 us -> 62.5 us  [back(): pl.pallas_call(functools.partial(back_kernel, inner_of(owners), kinds), g...]
where the time goes in v5:
time: 288 us
  Pallas kernels  251 us (87%)
  local copies, waits for them, and re-layouts  14.4 us (5%)
  other arithmetic  12 us (4%)
  matrix products  8.44 us (3%)
    pallas_call x1, Pallas kernels, mlp(): pl.pallas_call(functools.partial(mlp_kernel, tops), grid=(rows // tile,),...  88.6 us
    pallas_call x1, Pallas kernels, back(): pl.pallas_call(functools.partial(back_kernel, inner_of(owners), kinds), g...  62.5 us
    pallas_call x1, Pallas kernels, attend(): pl.pallas_call(functools.partial(attend_kernel, inner, kinds, fields), gr...  48.2 us
    pallas_call x1, Pallas kernels, gathered(): pl.pallas_call(functools.partial(gather_kernel, inner, cuts, kinds, field...  29.1 us
    pallas_call x1, Pallas kernels, delivered(): pl.pallas_call(functools.partial(deliver_kernel, inner, cuts, kinds), in_...  22.9 us
    concatenate x2, other arithmetic, per_device(): jnp.concatenate([top, rest], axis=0).reshape(rows, cols, imgs, d)  9.02 us
  transfers between devices with their start and end apart: 2, of which 0 were waited for; matrix products, arithmetic and copies ran while one was open for 6% of the time, Pallas kernels for 8%

profile of v5, /device:TPU:0, one launch (start us, length us, event | category | flops | bytes accessed | tf_op | source)
XLA Modules:
  0.0 287.7 jit_solution(5820709018683403193)
XLA Ops:
  0.6 0.0 copy-start
  0.7 0.0 copy-start.4
  0.7 0.8 slice_reduce_fusion.8
  1.5 0.8 slice_reduce_fusion.9
  2.3 0.9 pad_add_fusion.2
  3.2 0.6 broadcast_in_dim.26.refs_0_
  3.8 29.1 %gather.1 = (bf16[16,1,512]{2,1,0:T(2,128)(2,1)}, bf16[16,32,1536]{2,1,0:T(8,128)(2,1)}, bf16[42,32,512]{2,1,0:T(8,128)(2,1)}) custom-call(bf16[1,512]{1,0:T(2,128)(2,1)} %broadcast_in_dim.26.refs_0_, bf16[32,1536]{1,0:T(8,128)(2,1)} %refs_1_.2, bf16[98,32,512]{2,1,0:T(8,128)(2,1)} %bitcast.84), custom_call_target="tpu_custom_call" | custom-call | tf_op jit(solution)/shard_map/gather/pallas_call | solution.py:601
  32.9 0.8 copy.50
  33.6 0.6 slice.142
  34.2 0.1 slice.116
  34.3 0.1 slice.118
  34.4 0.1 slice.111
  34.5 0.1 slice.113
  34.6 0.1 slice.114
  34.6 0.1 pad_add_fusion.1
  34.7 0.1 eq.38
  34.8 0.1 eq.34
  34.9 0.1 compare_select_fusion
  35.0 1.2 fusion.1
  36.3 0.2 reshape.167
  36.5 0.9 fusion.10
  37.4 0.0 copy-done.10
  37.4 0.9 fusion.3
  38.3 1.0 pad_select_fusion.rel_ref
  39.3 0.1 reshape.164
  39.4 0.7 reshape.165.vec_ref
  40.1 48.2 %attend.1 = (bf16[32,12,112,128]{3,2,1,0:T(8,128)(2,1)}, bf16[98,32,512]{2,1,0:T(8,128)(2,1)}, bf16[32,16,112,112]{3,2,1,0:T(8,128)(2,1)}, bf16[16,32,512]{2,1,0...) custom-call(bf16[98,32,512]{2,1,0:T(8,128)(2,1)} %bitcast.85, ...), custom_call_target="tpu_custom_call" | custom-call | tf_op jit(solution)/shard_map/attend/pallas_call | solution.py:177
  88.3 88.6 %mlp.1 = (bf16[1344,512]{1,0:T(8,128)(2,1)}, bf16[1792,512]{1,0:T(8,128)(2,1)}, f32[3136,512]{1,0:T(8,128)}, bf16[3136,512]{1,0:T(8,128)(2,1)}, bf16[512,512]{1,...) custom-call(bf16[3136,512]{1,0:T(8,128)(2,1)} %bitcast.86, ...), custom_call_target="tpu_custom_call" | custom-call | tf_op jit(solution)/shard_map/mlp/pallas_call | solution.py:295
  176.9 0.0 copy-start.12
  176.9 62.5 %back.1 = (f32[42,32,512]{2,1,0:T(8,128)}, f32[56,32,512]{2,1,0:T(8,128)}, bf16[512,1536]{1,0:T(8,128)(2,1)}, f32[8,512]{1,0:T(8,128)}, f32[1,1536]{1,0:T(1,128)...) custom-call(bf16[98,32,512]{2,1,0:T(8,128)(2,1)} %bitcast.87, ...), custom_call_target="tpu_custom_call" | custom-call | tf_op jit(solution)/shard_map/back/pallas_call | solution.py:410
  239.5 0.0 copy-start.11
  239.5 0.1 collective-permute-start.1
  239.6 0.5 collective-permute-start
  240.1 0.8 slice_reduce_fusion.5
  240.9 0.1 reshape_squeeze.32
  241.0 0.1 reshape_squeeze.33
  241.1 0.1 reshape_squeeze.31
  241.2 0.1 reshape_squeeze.30
  241.3 0.1 reshape_squeeze.34
  241.4 0.1 reshape_squeeze.37
  241.4 0.1 reshape_squeeze.36
  241.5 0.1 reshape_squeeze.35
  241.6 3.0 %fusion.8 = f32[16,98,49]{1,2,0:T(8,128)S(1)} fusion(f32[98,49,1]{0,1,2:T(8,128)S(1)} %copy-done.4, f32[16,112,112]{2,1,0:T(8,128)} %get-tuple-element.71), kind=kOutput, calls=%fused_computation.14 | convolution fusion | flops 90354432 | bytes 1178504 | tf_op jit(solution)/shard_map/at,hba,bs->tsh/dot_general | solution.py:881
  244.6 0.0 copy-start.3
  244.6 0.5 convolution_bitcast_fusion.1
  245.2 0.2 reshape.185
  245.3 1.9 fusion.4
  247.2 0.1 reshape.186
  247.3 0.6 pad_bitcast_fusion.refs_2_
  247.9 0.9 add_convert_fusion.refs_0_
  248.8 22.9 %deliver.1 = (f32[1,512]{1,0:T(1,128)}, f32[32,1536]{1,0:T(8,128)}, f32[24,128]{1,0:T(8,128)}) custom-call(bf16[16,1,512]{2,1,0:T(2,128)(2,1)} %add_convert_fusion.refs_0_, bf16[16,32,1536]{2,1,0:T(8,128)(2,1)} %bitcast.103, f32[24,128]{1,0:T(8,128)} %pad_bitcast_fusion.refs_2_), custom_call_target="tpu_custom_call" | custom-call | tf_op jit(solution)/shard_map/deliver/pallas_call | solution.py:780
  271.8 0.8 slice.139
  272.6 0.7 copy.43
  273.2 1.1 slice_bitcast_fusion.1
  274.4 1.4 slice_bitcast_fusion
  275.8 0.0 collective-permute-done
  275.8 3.5 %pad_maximum_fusion.1 = bf16[98,32,512]{2,1,0:T(8,128)(2,1)} fusion(bf16[56,32,512]{2,1,0:T(8,128)(2,1)S(1)} %bitcast.102, bf16[42,32,512]{2,1,0:T(8,128)(2,1)} %bitcast.19), kind=kLoop, calls=%fused_computation.1 | loop fusion | flops 1605632 | bytes 6422528 | tf_op jit(solution)/shard_map/concatenate | solution.py:895
  279.3 0.0 collective-permute-done.1
  279.3 0.0 copy-start.1
  279.4 5.6 %pad_maximum_fusion = f32[98,32,512]{2,1,0:T(8,128)} fusion(f32[56,32,512]{2,1,0:T(8,128)S(1)} %copy-done.2, f32[42,32,512]{2,1,0:T(8,128)} %collective-permute-done.1), kind=kLoop, calls=%fused_computation | loop fusion | flops 1605632 | bytes 12845056 | tf_op jit(solution)/shard_map/concatenate | solution.py:895
  284.9 0.7 copy.55
  285.6 0.6 copy.56
  286.2 0.7 copy.57
  286.9 0.7 copy.58
  (24 shorter events, 0.1 us)
Async XLA Ops:
  0.6 34.4 %copy-start = (f32[169,16]{0,1:T(8,128)S(1)}, f32[169,16]{0,1:T(8,128)}, u32[]{:S(2)}) copy-start(f32[169,16]{0,1:T(8,128)} %param.35) | copy-start | bytes 32452
  0.7 35.8 %copy-start.4 = (f32[98,49,1]{0,1,2:T(8,128)S(1)}, f32[98,49,1]{0,1,2:T(8,128)}, u32[]{:S(2)}) copy-start(f32[98,49,1]{0,1,2:T(8,128)} %constant.61) | copy-start | bytes 57628
  0.7 34.1 %copy-start.9 = (s32[49,49]{1,0:T(8,128)S(1)}, s32[49,49]{1,0:T(8,128)}, u32[]{:S(2)}) copy-start(s32[49,49]{1,0:T(8,128)} %param.37) | copy-start | bytes 28816
  3.8 33.7 %copy-start.10 = (pred[98,98]{1,0:T(8,128)(4,1)S(1)}, pred[98,98]{1,0:T(8,128)(4,1)}, u32[]{:S(2)}) copy-start(pred[98,98]{1,0:T(8,128)(4,1)} %constant.15.clone) | copy-start | bytes 28816
  176.9 64.3 %copy-start.12 = (f32[8,512]{1,0:T(8,128)S(1)}, f32[8,512]{1,0:T(8,128)}, u32[]{:S(2)}) copy-start(f32[8,512]{1,0:T(8,128)} %get-tuple-element.68) | copy-start | bytes 49156
  239.5 8.5 %copy-start.11 = (f32[1,2048]{1,0:T(1,128)S(1)}, f32[1,2048]{1,0:T(1,128)}, u32[]{:S(2)}) copy-start(f32[1,2048]{1,0:T(1,128)} %get-tuple-element.69) | copy-start | bytes 24580
  239.5 39.8 %collective-permute-start.1 = (f32[42,32,512]{2,1,0:T(8,128)}, f32[42,32,512]{2,1,0:T(8,128)}, u32[]{:S(2)}, u32[]{:S(2)}) collective-permute-start(f32[42,32,512]{2,1,0:T(8,128)} %get-tuple-element.64), channel_id=1, source_target_pairs={{0,1},{1,0},{2,3},{3,2},{4,5},{5,4},{6,7},{7,6},{8,9},{9,8},{10,11... | collective-permute-start | bytes 8257544 | tf_op jit(solution)/shard_map/ppermute | solution.py:873
  239.6 36.3 %collective-permute-start = (bf16[1344,512]{1,0:T(8,128)(2,1)}, bf16[1344,512]{1,0:T(8,128)(2,1)}, u32[]{:S(2)}, u32[]{:S(2)}) collective-permute-start(bf16[1344,512]{1,0:T(8,128)(2,1)} %get-tuple-element.55), channel_id=1, source_target_pairs={{0,1},{1,0},{2,3},{3,2},{4,5},{5,4},{6,7},{7,6},{8,9},{9,8},{10,11... | collective-permute-start | bytes 4128776 | tf_op jit(solution)/shard_map/ppermute | solution.py:873
  244.6 31.2 %copy-start.3 = (bf16[1792,512]{1,0:T(8,128)(2,1)S(1)}, bf16[1792,512]{1,0:T(8,128)(2,1)}, u32[]{:S(2)}) copy-start(bf16[1792,512]{1,0:T(8,128)(2,1)} %get-tuple-element.56) | copy-start | bytes 5505028
  275.8 3.5 %copy-start.2 = (f32[56,32,512]{2,1,0:T(8,128)S(1)}, f32[56,32,512]{2,1,0:T(8,128)}, u32[]{:S(2)}) copy-start(f32[56,32,512]{2,1,0:T(8,128)} %get-tuple-element.65) | copy-start | bytes 11010052
  279.3 5.6 %copy-start.7 = (f32[32,1536]{1,0:T(8,128)S(1)}, f32[32,1536]{1,0:T(8,128)}, u32[]{:S(2)}) copy-start(f32[32,1536]{1,0:T(8,128)} %get-tuple-element.136) | copy-start | bytes 589828
  279.3 6.3 %copy-start.8 = (f32[32,512]{1,0:T(8,128)S(1)}, f32[32,512]{1,0:T(8,128)}, u32[]{:S(2)}) copy-start(f32[32,512]{1,0:T(8,128)} %get-tuple-element.139) | copy-start | bytes 196612
  279.3 6.9 %copy-start.6 = (f32[32,2048]{1,0:T(8,128)S(1)}, f32[32,2048]{1,0:T(8,128)}, u32[]{:S(2)}) copy-start(f32[32,2048]{1,0:T(8,128)} %get-tuple-element.143) | copy-start | bytes 786436
  279.3 7.6 %copy-start.5 = (f32[128,512]{1,0:T(8,128)S(1)}, f32[128,512]{1,0:T(8,128)}, u32[]{:S(2)}) copy-start(f32[128,512]{1,0:T(8,128)} %get-tuple-element.145) | copy-start | bytes 786436
  279.3 8.3 %copy-start.1 = (f32[169,16]{0,1:T(8,128)S(1)}, f32[169,16]{0,1:T(8,128)}, u32[]{:S(2)}) copy-start(f32[169,16]{0,1:T(8,128)} %param.35) | copy-start | bytes 32452

commit v6 on v5

--- a/solution.py
+++ b/solution.py
@@ -52,18 +52,20 @@
     return jnp.sum(v, axis=0, keepdims=True)
 
 
-def erf(x):
-    x = jnp.clip(x, -3.7439211627767994, 3.7439211627767994)
-    s = x * x
+def half_erf(h):
+    h = jnp.clip(h, -5.2947041, 5.2947041)
+    s = h * h
     a = (0.00022905065861350646, 0.0034082910107109506, 0.050955695062380861, 0.18520832239976145, 1.128379143519084)
     b = (-1.1791602954361697e-7, 0.000023547966471313185, 0.0010179625278914885, 0.014070470171167667, 0.11098505178285362, 0.49746925110067538, 1.0)
+    a = [c * 0.5 ** (4 - i) * 0.5 * 0.7071067811865476 for i, c in enumerate(a)]
+    b = [c * 0.5 ** (6 - i) for i, c in enumerate(b)]
     p = a[0]
     for c in a[1:]:
         p = p * s + c
     q = b[0]
     for c in b[1:]:
         q = q * s + c
-    return x * p / q
+    return h * p / q
 
 
 def head_masks():
@@ -107,17 +109,17 @@
     qkv_ref, att_ref, prob_ref = refs[kinds + fields : kinds + fields + 3]
     outs, halos = refs[kinds + fields + 3 : 2 * kinds + fields + 3], refs[2 * kinds + fields + 3 : 2 * (kinds + fields) + 3]
     wide, joined, *sems = refs[2 * (kinds + fields) + 3 :]
-    moves = Spread(inner, whole_cuts(kinds), ins, maps, outs, halos, *sems)
+    moves = ColumnSpread(inner, ins, maps, outs, halos, *sems)
 
     def begin():
         meet(Place(inner))
-        moves.run(0)
+        moves.start()
 
     at_step(0, begin)
     early, late = tuple(range(kinds - 1)), (kinds - 1,)
     events = [
         (share, functools.partial(moves.run, stage, which))
-        for share, stage, which in ((8, 1, early), (13, 1, late), (15, 2, early), (19, 2, late), (23, 3, early), (28, 3, late))
+        for share, stage, which in ((6, 0, early), (11, 0, late), (13, 1, early), (19, 1, late), (22, 2, early), (28, 2, late))
     ]
     d = x_ref.shape[-1]
     n, _ = normalized(shifted_rows(x_ref, halo_ref))
@@ -192,12 +194,12 @@
             jax.ShapeDtypeStruct((imgs, 3 * per, PAD, LANES), BF),
             jax.ShapeDtypeStruct((TOK, imgs, d), BF),
             jax.ShapeDtypeStruct((imgs, HEADS, PAD, PAD), BF),
-            *spread_shapes(owners, shards, maps),
+            *column_shapes(owners, shards, maps),
         ],
         scratch_shapes=[
             pltpu.VMEM((3 * per, PAD * NB, LANES), F32),
             pltpu.VMEM((per, PAD * NB, LANES), F32),
-            *spread_scratch(owners, kinds, kinds, fields),
+            *column_scratch(owners, kinds, fields),
         ],
         compiler_params=pltpu.CompilerParams(collective_id=2, has_side_effects=True, vmem_limit_bytes=60 << 20),
         name="attend",
@@ -231,27 +233,20 @@
     gb_t = gb.T
     out = middle + vec_ref[7:8]
     m = None
-    def begin(c):
-        at = slice(c * chunk, (c + 1) * chunk)
-        return mm(normed, w1_ref[:, at]), mm_nt(gb, w2_ref[at, :])
-
-    now = begin(0)
     for c in range(ff // chunk):
         at = slice(c * chunk, (c + 1) * chunk)
-        later = begin(c + 1) if c + 1 < ff // chunk else None
-        hidden = now[0] + b1_ref[:, at]
-        cdf = 0.5 * (1.0 + erf(hidden * 0.7071067811865476))
+        hidden = mm(normed, w1_ref[:, at]) + b1_ref[:, at]
+        cdf = 0.5 + half_erf(hidden)
         slope = cdf + hidden * (0.3989422804014327 * jnp.exp(-0.5 * hidden * hidden))
         active = (hidden * cdf).astype(BF)
-        gh = now[1] * slope
+        out = out + mm(active, w2_ref[at, :])
+        gh = mm_nt(gb, w2_ref[at, :]) * slope
         ghb = gh.astype(BF)
-        ab1[:, at] += col_sum(ghb.astype(F32))
-        out = out + mm(active, w2_ref[at, :])
+        ab1[:, at] += col_sum(gh)
+        aw2[:, at] += mm(gb_t, active)
+        aw1[:, at] += mm(normed_t, ghb)
         part = mm_nt(ghb, w1_ref[:, at])
         m = part if m is None else m + part
-        aw2[:, at] += mm(gb_t, active)
-        aw1[:, at] += mm(normed_t, ghb)
-        now = later
 
     @pl.when(above)
     def _():
@@ -424,7 +419,7 @@
             jax.ShapeDtypeStruct((8, d), F32),
             jax.ShapeDtypeStruct((1, 3 * d), F32),
             jax.ShapeDtypeStruct((HEADS, PAD, PAD), F32),
-            *[jax.ShapeDtypeStruct(g.shape[1:], F32) for g in grads],
+            *[jax.ShapeDtypeStruct(g.shape[2:], F32) for g in grads],
         ],
         scratch_shapes=[
             pltpu.VMEM((per, PAD * NB, LANES), F32),
@@ -459,6 +454,12 @@
         a = (self.a + da) % self.inner
         b = (self.b + db) % self.inner
         return z * self.inner * self.inner + a * self.step_a + b * self.step_b
+
+    def column(self, da=0, db=0):
+        return ((self.a + da) % self.inner) * self.step_a + ((self.b + db) % self.inner) * self.step_b
+
+    def depth(self, dz=0):
+        return (self.z + dz) % DEEP
 
     def device(self, dz=0, da=0, db=0):
         return (self.at(dz, da, db), self.core)
@@ -564,6 +565,101 @@
             copy.wait()
 
 
+class ColumnSpread:
+    def __init__(self, inner, ins, maps, outs, halos, send_sem, z_sem, column_sem, own_sem, halo_sem):
+        self.inner, self.ins, self.maps, self.outs, self.halos = inner, ins, maps, outs, halos
+        self.send_sem, self.z_sem, self.column_sem, self.own_sem, self.halo_sem = send_sem, z_sem, column_sem, own_sem, halo_sem
+        steps = range(1, inner)
+        along_a, along_b, mate = [("a", d) for d in steps], [("b", d) for d in steps], [("m", 0)]
+        plan = [[((0, 0), along_a + along_b + mate)]]
+        plan.append([((da, 0), along_b + mate) for da in steps])
+        plan.append([((da, db), mate) for db in steps for da in range(inner)])
+        self.plan, count = [], DEEP - 1
+        for stage in plan:
+            rows = []
+            for block, targets in stage:
+                rows.append((block, [(t, count + i) for i, t in enumerate(targets)]))
+                count += len(targets)
+            self.plan.append(rows)
+
+    def cut(self, k, core):
+        return cut_columns(self.outs[k], (k, 0, 1), core)
+
+    def along_z(self, place, k, d):
+        mine = self.outs[k].at[place.depth(), place.column(), :, self.cut(k, place.core)]
+        return remote(self.ins[k].at[:, self.cut(k, place.core)], mine, self.send_sem.at[k, d - 1],
+                      self.z_sem.at[k, d - 1], place.device(dz=d))
+
+    def move(self, place, k, block, target, index):
+        (axis, d), column = target, place.column(*block)
+        device = {"a": place.device(da=d), "b": place.device(db=d), "m": place.partner()}[axis]
+        part = self.outs[k].at[:, column, :, self.cut(k, place.core)]
+        return remote(part, part, self.send_sem.at[k, index], self.column_sem.at[k, place.core, column], device)
+
+    def arrive(self, place, k, block, core):
+        column = place.column(*block)
+        part = self.outs[k].at[:, column, :, self.cut(k, core)]
+        remote(part, part, self.send_sem.at[k, 0], self.column_sem.at[k, core, column], place.partner()).wait_recv()
+
+    def local(self, place, k):
+        cut = self.cut(k, place.core)
+        return pltpu.make_async_copy(self.ins[k].at[:, cut], self.outs[k].at[place.depth(), place.column(), :, cut],
+                                     self.own_sem.at[k])
+
+    def swaps(self, place):
+        return [remote(self.maps[f].at[:TOP], self.halos[f], self.halo_sem.at[f, 0], self.halo_sem.at[f, 1],
+                       place.partner()) for f in range(len(self.maps))]
+
+    def start(self):
+        place = Place(self.inner)
+        for k in range(len(self.ins)):
+            for d in (1, 3, 2):
+                self.along_z(place, k, d).start()
+            self.local(place, k).start()
+        for copy in self.swaps(place):
+            copy.start()
+
+    def run(self, stage, kinds):
+        place = Place(self.inner)
+        for k in kinds:
+            if stage == 0:
+                self.local(place, k).wait()
+                for d in (1, 3, 2):
+                    self.along_z(place, k, d).wait_recv()
+            for block, targets in self.plan[stage]:
+                if stage:
+                    self.arrive(place, k, block, place.core)
+                for target, index in targets:
+                    self.move(place, k, block, target, index).start()
+
+    def finish(self):
+        place = Place(self.inner)
+        for k in range(len(self.ins)):
+            for da in range(self.inner):
+                for db in range(self.inner):
+                    self.arrive(place, k, (da, db), place.mate)
+            for d in range(1, DEEP):
+                self.along_z(place, k, d).wait_send()
+            for rows in self.plan:
+                for block, targets in rows:
+                    for target, index in targets:
+                        self.move(place, k, block, target, index).wait_send()
+        for copy in self.swaps(place):
+            copy.wait()
+
+
+def column_scratch(owners, kinds, fields):
+    inner, dma = inner_of(owners), pltpu.SemaphoreType.DMA
+    sends = DEEP - 1 + 2 * (inner - 1) + 1 + (inner - 1) * inner + (inner - 1) * inner
+    return [dma((kinds, sends)), dma((kinds, DEEP - 1)), dma((kinds, 2, inner * inner)), dma((kinds,)), dma((fields, 2))]
+
+
+def column_shapes(owners, shards, maps):
+    return [jax.ShapeDtypeStruct((DEEP, owners // DEEP, *s.shape), s.dtype) for s in shards] + [
+        jax.ShapeDtypeStruct((TOP, *m.shape[1:]), m.dtype) for m in maps
+    ]
+
+
 def spread_scratch(owners, kinds, arrays, fields):
     inner = inner_of(owners)
     sends = 3 + 2 * (inner - 1) + 3 * (2 * inner - 1) + 2 * DEEP * (inner - 1) * inner
@@ -622,29 +718,29 @@
     def columns(self, k, core):
         return cut_columns(self.outs[self.cuts[k][0]], self.cuts[k], core)
 
-    def add(self, k, block, other):
-        self.own[k][block] = (self.own[k][block].astype(F32) + other[...].astype(F32)).astype(BF)
+    def add(self, k, column, other):
+        self.own[k][:, column] = (self.own[k][:, column].astype(F32) + other[...].astype(F32)).astype(BF)
 
     def loads(self, place, k):
+        array = self.ins[self.cuts[k][0]]
         return (
-            remote(self.ins[self.cuts[k][0]].at[:, :, self.columns(k, place.mate)], self.from_mate[k], self.mate_sem.at[k, 0],
+            remote(array.at[:, :, :, self.columns(k, place.mate)], self.from_mate[k], self.mate_sem.at[k, 0],
                    self.mate_sem.at[k, 1], place.partner()),
-            pltpu.make_async_copy(self.ins[self.cuts[k][0]].at[:, :, self.columns(k, place.core)], self.own[k], self.load_sem.at[k]),
+            pltpu.make_async_copy(array.at[:, :, :, self.columns(k, place.core)], self.own[k], self.load_sem.at[k]),
         )
 
-    def to_b(self, place, k, dz, da, db):
-        slot = (db - 1) * self.inner * DEEP + da * DEEP + dz
-        return remote(self.own[k].at[place.at(dz, da, db)], self.from_b[k].at[slot], self.b_sem.at[k, 0, slot],
+    def to_b(self, place, k, da, db):
+        slot = (db - 1) * self.inner + da
+        return remote(self.own[k].at[:, place.column(da, db)], self.from_b[k].at[slot], self.b_sem.at[k, 0, slot],
                       self.b_sem.at[k, 1, slot], place.device(db=db))
 
-    def to_a(self, place, k, dz, da):
-        slot = (da - 1) * DEEP + dz
-        return remote(self.own[k].at[place.at(dz, da)], self.from_a[k].at[slot], self.a_sem.at[k, 0, slot],
-                      self.a_sem.at[k, 1, slot], place.device(da=da))
+    def to_a(self, place, k, da):
+        return remote(self.own[k].at[:, place.column(da)], self.from_a[k].at[da - 1], self.a_sem.at[k, 0, da - 1],
+                      self.a_sem.at[k, 1, da - 1], place.device(da=da))
 
     def to_z(self, place, k, dz):
-        return remote(self.own[k].at[place.at(dz)], self.from_z[k].at[dz - 1], self.z_sem.at[k, 0, dz - 1],
-                      self.z_sem.at[k, 1, dz - 1], place.device(dz=dz))
+        return remote(self.own[k].at[place.depth(dz), place.column()], self.from_z[k].at[dz - 1],
+                      self.z_sem.at[k, 0, dz - 1], self.z_sem.at[k, 1, dz - 1], place.device(dz=dz))
 
     def ends(self, place, k):
         there = self.outs[self.cuts[k][0]].at[:, self.columns(k, place.core)]
@@ -664,44 +760,39 @@
                 copy.wait()
             for db in tuple(self.steps) + (0,):
                 for da in range(self.inner):
-                    for dz in range(DEEP):
-                        block = place.at(dz, da, db)
-                        self.add(k, block, self.from_mate[k].at[block])
-                        if db:
-                            self.to_b(place, k, dz, da, db).start()
+                    column = place.column(da, db)
+                    self.add(k, column, self.from_mate[k].at[:, column])
+                    if db:
+                        self.to_b(place, k, da, db).start()
 
     def pass_a(self):
         place = Place(self.inner)
         for k in self.kinds:
             for db in self.steps:
                 for da in range(self.inner):
-                    for dz in range(DEEP):
-                        self.to_b(place, k, dz, da, db).wait()
+                    self.to_b(place, k, da, db).wait()
             for da in tuple(self.steps) + (0,):
-                for dz in range(DEEP):
-                    for db in self.steps:
-                        self.add(k, place.at(dz, da), self.from_b[k].at[(db - 1) * self.inner * DEEP + da * DEEP + dz])
-                    if da:
-                        self.to_a(place, k, dz, da).start()
+                for db in self.steps:
+                    self.add(k, place.column(da), self.from_b[k].at[(db - 1) * self.inner + da])
+                if da:
+                    self.to_a(place, k, da).start()
 
     def pass_z(self):
         place = Place(self.inner)
         for k in self.kinds:
             for da in self.steps:
-                for dz in range(DEEP):
-                    self.to_a(place, k, dz, da).wait()
-            for dz in (2, 1, 3, 0):
-                for da in self.steps:
-                    self.add(k, place.at(dz), self.from_a[k].at[(da - 1) * DEEP + dz])
-                if dz:
-                    self.to_z(place, k, dz).start()
+                self.to_a(place, k, da).wait()
+            for da in self.steps:
+                self.add(k, place.column(), self.from_a[k].at[da - 1])
+            for dz in (2, 1, 3):
+                self.to_z(place, k, dz).start()
 
     def hand_over(self):
         place = Place(self.inner)
         for k in self.kinds:
             for dz in (2, 1, 3):
                 self.to_z(place, k, dz).wait()
-            total = self.own[k][place.at()].astype(F32)
+            total = self.own[k][place.depth(), place.column()].astype(F32)
             for dz in range(1, DEEP):
                 total = total + self.from_z[k][dz - 1].astype(F32)
             self.final[k][...] = total
@@ -717,17 +808,17 @@
 
 def delivery_scratch(owners, grads, cuts):
     inner, kinds = inner_of(owners), len(cuts)
-    halves = [(grads[i].shape[1], grads[i].shape[2] // 2 // parts) for i, _, parts in cuts]
+    halves = [(grads[i].shape[2], grads[i].shape[3] // 2 // parts) for i, _, parts in cuts]
     dma = pltpu.SemaphoreType.DMA
 
-    def room(count):
-        return [pltpu.VMEM((count, *h), BF) for h in halves]
+    def room(*count):
+        return [pltpu.VMEM((*count, *h), BF) for h in halves]
 
     return [
-        *room(owners), *room(owners), *room((inner - 1) * inner * DEEP), *room((inner - 1) * DEEP),
-        *room(DEEP - 1), *[pltpu.VMEM(h, F32) for h in halves],
-        dma((kinds,)), dma((kinds, 2)), dma((kinds, 2, (inner - 1) * inner * DEEP)),
-        dma((kinds, 2, (inner - 1) * DEEP)), dma((kinds, 2, DEEP - 1)), dma((kinds, 3)),
+        *room(DEEP, owners // DEEP), *room(DEEP, owners // DEEP), *room((inner - 1) * inner, DEEP),
+        *room(inner - 1, DEEP), *room(DEEP - 1), *[pltpu.VMEM(h, F32) for h in halves],
+        dma((kinds,)), dma((kinds, 2)), dma((kinds, 2, (inner - 1) * inner)),
+        dma((kinds, 2, inner - 1)), dma((kinds, 2, DEEP - 1)), dma((kinds, 3)),
     ]
 
 
@@ -781,7 +872,7 @@
         functools.partial(deliver_kernel, inner, cuts, kinds),
         in_specs=[anywhere] * kinds + [pl.BlockSpec(memory_space=pltpu.VMEM)],
         out_specs=[anywhere] * kinds + [pl.BlockSpec(memory_space=pltpu.VMEM)],
-        out_shape=[jax.ShapeDtypeStruct(g.shape[1:], F32) for g in grads]
+        out_shape=[jax.ShapeDtypeStruct(g.shape[2:], F32) for g in grads]
         + [jax.ShapeDtypeStruct(table.shape, F32)],
         scratch_shapes=[
             *delivery_scratch(owners, grads, cuts), pltpu.VMEM((4, DEEP, *table.shape), F32), dma((4, 2, DEEP)),
@@ -851,12 +942,12 @@
     x = images.transpose(1, 2, 0, 3).reshape(rows * cols, imgs, d)
     ct = cotangent.transpose(1, 2, 0, 3).reshape(rows * cols, imgs, d)
     vectors = (norm1_gain, norm1_bias, q_bias, v_bias, proj_bias, norm2_gain, norm2_bias, fc2_bias, fc1_bias)
-    packed, w_qkv, halo = gathered((packed_row(vectors)[None], qkv_weight), (x,), qkv_cuts())
+    packed, w_qkv, halo = gathered((packed_row(vectors)[None], qkv_weight), (x,), whole_cuts(2))
     packed = packed[:, 0].astype(F32)
     part = d // owners
     vecs = packed[:, : 8 * part].reshape(owners, 8, part).transpose(1, 0, 2).reshape(8, d)
     b_in = packed[:, 8 * part : 8 * part + fc1_bias.shape[0]].reshape(1, -1)
-    whole = lambda v: v.reshape(owners * v.shape[1], v.shape[2])
+    whole = lambda v: v.reshape(-1, v.shape[-1])
     w_qkv = whole(w_qkv)
     onehot, relative = relative_parts(rel_index, bias_table)
     rel = bias_of_pairs(relative, regions)
@@ -872,7 +963,7 @@
     )
     swapped = lambda v: lax.ppermute(v, "win", [(0, 1), (1, 0)])
     out_top = swapped(out_top)
-    blocks = lambda v: v.reshape(owners, v.shape[0] // owners, v.shape[1])
+    blocks = lambda v: v.reshape(DEEP, owners // DEEP, v.shape[0] // owners, v.shape[1])
     gin_top, gin_rest, dwq, small1, bsum, rel_sum, dwp, dw1, dw2 = back(
         x, halo, tall(gm), tall(gatt), qkv, prob, vecs, w_qkv, (blocks(dwp), blocks(dw1), blocks(dw2))
     )
@@ -885,7 +976,7 @@
         small1[0], small1[1], bsum[0, :d], bsum[0, 2 * d :], small2[2], small2[0], small2[1], small2[3], db_in[0],
     )
     row = packed_row([v.reshape(owners, 1, -1) for v in grads]).astype(BF)
-    sums, dwq, table_sum = delivered((row, blocks(dwq)), flat_table, qkv_cuts())
+    sums, dwq, table_sum = delivered((row.reshape(DEEP, owners // DEEP, 1, -1), blocks(dwq)), flat_table, qkv_cuts())
     at, own = 0, []
     for v in vectors:
         own.append(sums[0, at : at + v.shape[0]])

time: 288 us -> 278 us (0.965)
  Pallas kernels: 251 us -> 241 us
    pallas_call x1, Pallas kernels: 29.1 us -> 23.5 us  [gathered(): pl.pallas_call(functools.partial(gather_kernel, inner, cuts, kinds, field...]
    pallas_call x1, Pallas kernels: 88.6 us -> 83.2 us  [mlp(): pl.pallas_call(functools.partial(mlp_kernel, tops), grid=(rows // tile,),...]
where the time goes in v6:
time: 278 us
  Pallas kernels  241 us (87%)
  local copies, waits for them, and re-layouts  15 us (5%)
  other arithmetic  11.3 us (4%)
  matrix products  8.59 us (3%)
    pallas_call x1, Pallas kernels, mlp(): pl.pallas_call(functools.partial(mlp_kernel, tops), grid=(rows // tile,),...  83.2 us
    pallas_call x1, Pallas kernels, back(): pl.pallas_call(functools.partial(back_kernel, inner_of(owners), kinds), g...  62.9 us
    pallas_call x1, Pallas kernels, attend(): pl.pallas_call(functools.partial(attend_kernel, inner, kinds, fields), gr...  49.5 us
    pallas_call x1, Pallas kernels, gathered(): pl.pallas_call(functools.partial(gather_kernel, inner, cuts, kinds, field...  23.5 us
    pallas_call x1, Pallas kernels, delivered(): pl.pallas_call(functools.partial(deliver_kernel, inner, cuts, kinds), in_...  22.1 us
    concatenate x2, other arithmetic, per_device(): jnp.concatenate([top, rest], axis=0).reshape(rows, cols, imgs, d)  9.13 us
  transfers between devices with their start and end apart: 2, of which 0 were waited for; matrix products, arithmetic and copies ran while one was open for 6% of the time, Pallas kernels for 8%

profile of v6, /device:TPU:0, one launch (start us, length us, event | category | flops | bytes accessed | tf_op | source)
XLA Modules:
  0.0 277.6 jit_solution(18206284496491654372)
XLA Ops:
  0.6 0.0 copy-start
  0.7 0.0 copy-start.4
  0.7 0.8 slice_reduce_fusion.8
  1.5 0.8 slice_reduce_fusion.9
  2.3 0.9 pad_add_fusion.2
  3.2 0.6 broadcast_in_dim.26.refs_0_
  3.8 23.5 %gather.1 = (bf16[16,1,512]{2,1,0:T(2,128)(2,1)}, bf16[16,32,1536]{2,1,0:T(8,128)(2,1)}, bf16[42,32,512]{2,1,0:T(8,128)(2,1)}) custom-call(bf16[1,512]{1,0:T(2,128)(2,1)} %broadcast_in_dim.26.refs_0_, bf16[32,1536]{1,0:T(8,128)(2,1)} %refs_1_.2, bf16[98,32,512]{2,1,0:T(8,128)(2,1)} %bitcast.86), custom_call_target="tpu_custom_call" | custom-call | tf_op jit(solution)/shard_map/gather/pallas_call | solution.py:697
  27.3 0.8 copy.51
  28.0 0.6 slice.142
  28.6 0.1 slice.116
  28.7 0.1 slice.118
  28.8 0.1 slice.111
  28.9 0.1 slice.113
  29.0 0.1 slice.114
  29.1 0.1 pad_add_fusion.1
  29.1 0.1 eq.38
  29.2 0.1 eq.34
  29.4 0.1 compare_select_fusion
  29.4 0.0 copy-done
  29.5 1.2 fusion.1
  30.7 0.2 reshape.170
  30.9 0.9 fusion.10
  31.8 0.9 fusion.3
  32.7 1.0 pad_select_fusion.rel_ref
  33.8 0.1 reshape.167
  33.9 0.7 reshape.168.vec_ref
  34.6 49.5 %attend.1 = (bf16[32,12,112,128]{3,2,1,0:T(8,128)(2,1)}, bf16[98,32,512]{2,1,0:T(8,128)(2,1)}, bf16[32,16,112,112]{3,2,1,0:T(8,128)(2,1)}, bf16[4,4,32,512]{3,2,...) custom-call(bf16[98,32,512]{2,1,0:T(8,128)(2,1)} %bitcast.87, ...), custom_call_target="tpu_custom_call" | custom-call | tf_op jit(solution)/shard_map/attend/pallas_call | solution.py:179
  84.1 83.2 %mlp.1 = (bf16[1344,512]{1,0:T(8,128)(2,1)}, bf16[1792,512]{1,0:T(8,128)(2,1)}, f32[3136,512]{1,0:T(8,128)}, bf16[3136,512]{1,0:T(8,128)(2,1)}, bf16[512,512]{1,...) custom-call(bf16[3136,512]{1,0:T(8,128)(2,1)} %bitcast.88, ...), custom_call_target="tpu_custom_call" | custom-call | tf_op jit(solution)/shard_map/mlp/pallas_call | solution.py:290
  167.3 0.0 copy-start.12
  167.3 0.0 copy-start.11
  167.3 62.9 %back.1 = (f32[42,32,512]{2,1,0:T(8,128)}, f32[56,32,512]{2,1,0:T(8,128)}, bf16[512,1536]{1,0:T(8,128)(2,1)}, f32[8,512]{1,0:T(8,128)}, f32[1,1536]{1,0:T(1,128)...) custom-call(bf16[98,32,512]{2,1,0:T(8,128)(2,1)} %bitcast.89, ...), custom_call_target="tpu_custom_call" | custom-call | tf_op jit(solution)/shard_map/back/pallas_call | solution.py:405
  230.2 0.1 collective-permute-start.1
  230.3 0.5 collective-permute-start
  230.8 0.8 slice_reduce_fusion.5
  231.6 0.1 reshape_squeeze.32
  231.7 0.1 reshape_squeeze.33
  231.7 0.1 reshape_squeeze.31
  231.8 0.1 reshape_squeeze.30
  231.9 0.1 reshape_squeeze.34
  232.0 0.1 reshape_squeeze.37
  232.1 0.1 reshape_squeeze.36
  232.2 0.1 reshape_squeeze.35
  232.2 0.1 add_convert_fusion
  232.3 0.6 reshape.194.refs_0_
  233.0 3.1 %fusion.8 = f32[16,98,49]{1,2,0:T(8,128)S(1)} fusion(f32[98,49,1]{0,1,2:T(8,128)S(1)} %copy-done.4, f32[16,112,112]{2,1,0:T(8,128)} %get-tuple-element.71), kind=kOutput, calls=%fused_computation.14 | convolution fusion | flops 90354432 | bytes 1178504 | tf_op jit(solution)/shard_map/at,hba,bs->tsh/dot_general | solution.py:972
  236.1 0.5 convolution_bitcast_fusion.1
  236.6 0.2 reshape.189
  236.8 1.9 fusion.4
  238.7 0.1 reshape.190
  238.8 0.6 pad_bitcast_fusion.refs_2_
  239.4 22.1 %deliver.1 = (f32[1,512]{1,0:T(1,128)}, f32[32,1536]{1,0:T(8,128)}, f32[24,128]{1,0:T(8,128)}) custom-call(bf16[4,4,1,512]{3,2,1,0:T(2,128)(2,1)} %reshape.194.refs_0_, bf16[4,4,32,1536]{3,2,1,0:T(8,128)(2,1)} %bitcast.105, f32[24,128]{1,0:T(8,128)} %pad_bitcast_fusion.refs_2_), custom_call_target="tpu_custom_call" | custom-call | tf_op jit(solution)/shard_map/deliver/pallas_call | solution.py:871
  261.6 0.8 slice.139
  262.4 0.7 copy.44
  263.1 1.1 slice_bitcast_fusion.1
  264.2 1.4 slice_bitcast_fusion
  265.6 0.0 collective-permute-done
  265.7 3.5 %pad_maximum_fusion.1 = bf16[98,32,512]{2,1,0:T(8,128)(2,1)} fusion(bf16[56,32,512]{2,1,0:T(8,128)(2,1)S(1)} %bitcast.104, bf16[42,32,512]{2,1,0:T(8,128)(2,1)} %bitcast.19), kind=kLoop, calls=%fused_computation.1 | loop fusion | flops 1605632 | bytes 6422528 | tf_op jit(solution)/shard_map/concatenate | solution.py:986
  269.1 0.0 collective-permute-done.1
  269.2 0.0 copy-start.1
  269.2 5.7 %pad_maximum_fusion = f32[98,32,512]{2,1,0:T(8,128)} fusion(f32[56,32,512]{2,1,0:T(8,128)S(1)} %copy-done.2, f32[42,32,512]{2,1,0:T(8,128)} %collective-permute-done.1), kind=kLoop, calls=%fused_computation | loop fusion | flops 1605632 | bytes 12845056 | tf_op jit(solution)/shard_map/concatenate | solution.py:986
  274.9 0.7 copy.56
  275.5 0.6 copy.57
  276.2 0.7 copy.58
  276.9 0.7 copy.59
  (25 shorter events, 0.1 us)
Async XLA Ops:
  0.6 28.8 %copy-start = (f32[169,16]{0,1:T(8,128)S(1)}, f32[169,16]{0,1:T(8,128)}, u32[]{:S(2)}) copy-start(f32[169,16]{0,1:T(8,128)} %param.35) | copy-start | bytes 32452
  0.7 30.3 %copy-start.4 = (f32[98,49,1]{0,1,2:T(8,128)S(1)}, f32[98,49,1]{0,1,2:T(8,128)}, u32[]{:S(2)}) copy-start(f32[98,49,1]{0,1,2:T(8,128)} %constant.61) | copy-start | bytes 57628
  0.7 28.6 %copy-start.9 = (s32[49,49]{1,0:T(8,128)S(1)}, s32[49,49]{1,0:T(8,128)}, u32[]{:S(2)}) copy-start(s32[49,49]{1,0:T(8,128)} %param.37) | copy-start | bytes 28816
  3.8 28.1 %copy-start.10 = (pred[98,98]{1,0:T(8,128)(4,1)S(1)}, pred[98,98]{1,0:T(8,128)(4,1)}, u32[]{:S(2)}) copy-start(pred[98,98]{1,0:T(8,128)(4,1)} %constant.15.clone) | copy-start | bytes 28816
  167.3 64.6 %copy-start.12 = (f32[8,512]{1,0:T(8,128)S(1)}, f32[8,512]{1,0:T(8,128)}, u32[]{:S(2)}) copy-start(f32[8,512]{1,0:T(8,128)} %get-tuple-element.68) | copy-start | bytes 49156
  167.3 64.9 %copy-start.11 = (f32[1,2048]{1,0:T(1,128)S(1)}, f32[1,2048]{1,0:T(1,128)}, u32[]{:S(2)}) copy-start(f32[1,2048]{1,0:T(1,128)} %get-tuple-element.69) | copy-start | bytes 24580
  230.2 38.9 %collective-permute-start.1 = (f32[42,32,512]{2,1,0:T(8,128)}, f32[42,32,512]{2,1,0:T(8,128)}, u32[]{:S(2)}, u32[]{:S(2)}) collective-permute-start(f32[42,32,512]{2,1,0:T(8,128)} %get-tuple-element.64), channel_id=1, source_target_pairs={{0,1},{1,0},{2,3},{3,2},{4,5},{5,4},{6,7},{7,6},{8,9},{9,8},{10,11... | collective-permute-start | bytes 8257544 | tf_op jit(solution)/shard_map/ppermute | solution.py:964
  230.3 35.4 %collective-permute-start = (bf16[1344,512]{1,0:T(8,128)(2,1)}, bf16[1344,512]{1,0:T(8,128)(2,1)}, u32[]{:S(2)}, u32[]{:S(2)}) collective-permute-start(bf16[1344,512]{1,0:T(8,128)(2,1)} %get-tuple-element.55), channel_id=1, source_target_pairs={{0,1},{1,0},{2,3},{3,2},{4,5},{5,4},{6,7},{7,6},{8,9},{9,8},{10,11... | collective-permute-start | bytes 4128776 | tf_op jit(solution)/shard_map/ppermute | solution.py:964
  233.0 32.7 %copy-start.3 = (bf16[1792,512]{1,0:T(8,128)(2,1)S(1)}, bf16[1792,512]{1,0:T(8,128)(2,1)}, u32[]{:S(2)}) copy-start(bf16[1792,512]{1,0:T(8,128)(2,1)} %get-tuple-element.56) | copy-start | bytes 5505028
  265.7 3.5 %copy-start.2 = (f32[56,32,512]{2,1,0:T(8,128)S(1)}, f32[56,32,512]{2,1,0:T(8,128)}, u32[]{:S(2)}) copy-start(f32[56,32,512]{2,1,0:T(8,128)} %get-tuple-element.65) | copy-start | bytes 11010052
  269.1 5.7 %copy-start.7 = (f32[32,1536]{1,0:T(8,128)S(1)}, f32[32,1536]{1,0:T(8,128)}, u32[]{:S(2)}) copy-start(f32[32,1536]{1,0:T(8,128)} %get-tuple-element.136) | copy-start | bytes 589828
  269.1 6.4 %copy-start.8 = (f32[32,512]{1,0:T(8,128)S(1)}, f32[32,512]{1,0:T(8,128)}, u32[]{:S(2)}) copy-start(f32[32,512]{1,0:T(8,128)} %get-tuple-element.139) | copy-start | bytes 196612
  269.1 7.0 %copy-start.6 = (f32[32,2048]{1,0:T(8,128)S(1)}, f32[32,2048]{1,0:T(8,128)}, u32[]{:S(2)}) copy-start(f32[32,2048]{1,0:T(8,128)} %get-tuple-element.143) | copy-start | bytes 786436
  269.2 7.7 %copy-start.5 = (f32[128,512]{1,0:T(8,128)S(1)}, f32[128,512]{1,0:T(8,128)}, u32[]{:S(2)}) copy-start(f32[128,512]{1,0:T(8,128)} %get-tuple-element.145) | copy-start | bytes 786436
  269.2 8.4 %copy-start.1 = (f32[169,16]{0,1:T(8,128)S(1)}, f32[169,16]{0,1:T(8,128)}, u32[]{:S(2)}) copy-start(f32[169,16]{0,1:T(8,128)} %param.35) | copy-start | bytes 32452
